TPU v7x, 32 devices: a whole 2x2x4 slice. The times are simulated.
32 devices in a mesh: lon: 8 (over y, x, core), lat: 4 (over z).
Axes of the slice: x: 2, y: 2, z: 4, core: 2. Of those that a mesh axis runs over, the one named last changes fastest.
Arguments:
- fields: bfloat16 [96, 192, 3, 512], P('lat', 'lon'), may hold values from -6 to 6
- region_ids: int32 [96], P('lat'), may hold values from 0 to 15, never falling along the last dimension, each value on 1 to 12 neighbouring positions
- w_qkv: bfloat16 [1536, 512], P(('lon', 'lat')), may hold values from -2 to 2
- w_proj: bfloat16 [512, 512], P(('lon', 'lat')), may hold values from -0.25 to 0.25
- grad_output: bfloat16 [96, 192, 3, 512], P('lat', 'lon'), may hold values from -6 to 6
Outputs:
- block_out: bfloat16 [96, 192, 3, 512], P('lat', 'lon')
- grad_fields: bfloat16 [96, 192, 3, 512], P('lat', 'lon')
- grad_w_qkv: float32 [1536, 512], P(('lon', 'lat'))
- grad_w_proj: float32 [512, 512], P(('lon', 'lat'))
Inputs may be any that keep to these rules, and one draw needn't show every extreme that they name: `region_ids`: region ids never fall along the rows; each region spans 1 to 12 rows.
All inputs are finite; a program needn't handle non-finite values.
Results may differ from a plain program's by a relative error of at most 0.018.
The roundings to bfloat16 on the way count: a program that leaves them out, or rounds other values in their place, can miss the bound.
Values may be sent and summed in bfloat16 or wider, within the bound.
No kernel may reach another device: no remote copies, remote signals or barrier semaphores. Data moves between devices by JAX's collectives and lax.ppermute only.
A program may use at most 128 MiB of HBM per device.

v0:
```python
import jax
import jax.numpy as jnp
from jax import lax
from jax.sharding import PartitionSpec as P

HEADS = 8
HEAD = 64
WIN = 12


EPSILON = 1e-05


def shifted_2(block, axis, distance):
    devices = range(lax.axis_size(axis))
    route = [((i - distance) % len(devices), i) for i in devices]
    return lax.ppermute(block, axis, route)


def to_windows(grid, side):
    rows, cols, depth, width = grid.shape
    blocks = grid.reshape(rows // side, side, cols // side, side, depth, width)
    return blocks.transpose(0, 2, 1, 3, 4, 5).reshape(-1, side * side * depth, width)


def from_windows(windows, rows, cols, side):
    depth = windows.shape[1] // (side * side)
    width = windows.shape[2]
    blocks = windows.reshape(rows // side, cols // side, side, side, depth, width)
    return blocks.transpose(0, 2, 1, 3, 4, 5).reshape(rows, cols, depth, width)


def window_regions(region_ids, cols, depth, side):
    bands = region_ids.shape[0] // side
    spread = jnp.broadcast_to(
        region_ids.reshape(bands, 1, side, 1, 1), (bands, cols // side, side, side, depth)
    )
    return spread.reshape(bands * (cols // side), side * side * depth)


def split_heads(qkv_window):
    count = qkv_window.shape[0]
    parts = qkv_window.reshape(count, 3, HEADS, HEAD)
    return (parts[:, 0], parts[:, 1], parts[:, 2])


def attention_probs(query, keys, region):
    scores = jnp.einsum("qhd,khd->hqk", query, keys, preferred_element_type=jnp.float32) * HEAD ** (
        -0.5
    )
    allowed = region[:, None] == region[None, :]
    scores = jnp.where(allowed[None], scores, -1e30)
    peak = jnp.max(scores, axis=-1, keepdims=True)
    weights = jnp.exp(scores - peak)
    return weights / jnp.sum(weights, axis=-1, keepdims=True)


def forward_window(operands):
    qkv_window, region = operands
    query, keys, values = split_heads(qkv_window)
    probs = attention_probs(query, keys, region).astype(jnp.bfloat16)
    mixed = jnp.einsum("hqk,khd->qhd", probs, values, preferred_element_type=jnp.float32)
    return mixed.reshape(qkv_window.shape[0], HEADS * HEAD).astype(jnp.bfloat16)


def backward_window(operands):
    qkv_window, region, grad_window = operands
    count = qkv_window.shape[0]
    query, keys, values = split_heads(qkv_window)
    probs = attention_probs(query, keys, region)
    rounded = probs.astype(jnp.bfloat16)
    grad_heads = grad_window.reshape(count, HEADS, HEAD)
    grad_probs = jnp.einsum("qhd,khd->hqk", grad_heads, values, preferred_element_type=jnp.float32)
    grad_values = jnp.einsum(
        "hqk,qhd->khd", rounded, grad_heads, preferred_element_type=jnp.float32
    )
    inner = jnp.sum(grad_probs * probs, axis=-1, keepdims=True)
    grad_scores = (probs * (grad_probs - inner) * HEAD ** (-0.5)).astype(jnp.bfloat16)
    grad_query = jnp.einsum("hqk,khd->qhd", grad_scores, keys, preferred_element_type=jnp.float32)
    grad_keys = jnp.einsum("hqk,qhd->khd", grad_scores, query, preferred_element_type=jnp.float32)
    joined = jnp.stack([grad_query, grad_keys, grad_values], axis=1)
    return joined.reshape(count, 3 * HEADS * HEAD).astype(jnp.bfloat16)


def shards(fields, region_ids, w_qkv, w_proj, grad_output):
    rows, cols, depth, width = fields.shape
    side = WIN
    half = side // 2
    count = rows * cols * depth
    factor = float(count * lax.axis_size("lon") * lax.axis_size("lat")) ** (-0.5)
    strip_fields, strip_grads = shifted_2((fields[:, :half], grad_output[:, :half]), "lon", -1)
    moved_fields = jnp.concatenate([fields[:, half:], strip_fields], axis=1)
    moved_grads = jnp.concatenate([grad_output[:, half:], strip_grads], axis=1)
    band_fields, band_grads = shifted_2((moved_fields[:half], moved_grads[:half]), "lat", -1)
    shifted = jnp.concatenate([moved_fields[half:], band_fields], axis=0)
    grad_shift = jnp.concatenate([moved_grads[half:], band_grads], axis=0)
    flat = shifted.reshape(count, width).astype(jnp.float32)
    centre = flat - jnp.mean(flat, axis=-1, keepdims=True)
    inverse = lax.rsqrt(jnp.mean(centre * centre, axis=-1, keepdims=True) + EPSILON)
    normal = centre * inverse
    normed = normal.astype(jnp.bfloat16)
    qkv = jnp.dot(
        normed,
        lax.all_gather(w_qkv, ("lon", "lat"), axis=0, tiled=True).T,
        preferred_element_type=jnp.float32,
    ).astype(jnp.bfloat16)
    regions = window_regions(region_ids, cols, depth, side)
    qkv_windows = to_windows(qkv.reshape(rows, cols, depth, 3 * width), side)
    attended_windows = lax.map(forward_window, (qkv_windows, regions))
    attended = from_windows(attended_windows, rows, cols, side).reshape(count, width)
    grad_flat = grad_shift.reshape(count, width)
    branch = jnp.dot(
        attended,
        lax.all_gather(w_proj, ("lon", "lat"), axis=0, tiled=True).T,
        preferred_element_type=jnp.float32,
    )
    section = grad_flat
    grad_attended = jnp.dot(
        section,
        lax.all_gather(w_proj, ("lon", "lat"), axis=0, tiled=True),
        preferred_element_type=jnp.float32,
    )
    branch = branch.astype(jnp.bfloat16)
    grad_attended = grad_attended.astype(jnp.bfloat16)
    section = grad_flat
    grad_w_proj = lax.psum_scatter(
        jnp.dot(section.T, attended, preferred_element_type=jnp.float32) * factor,
        ("lon", "lat"),
        scatter_dimension=0,
        tiled=True,
    )
    grad_windows = to_windows(grad_attended.reshape(rows, cols, depth, width), side)
    grad_qkv_windows = lax.map(backward_window, (qkv_windows, regions, grad_windows))
    grad_qkv = from_windows(grad_qkv_windows, rows, cols, side).reshape(count, 3 * width)
    section = grad_qkv
    grad_w_qkv = lax.psum_scatter(
        jnp.dot(section.T, normed, preferred_element_type=jnp.float32) * factor,
        ("lon", "lat"),
        scatter_dimension=0,
        tiled=True,
    )
    section = grad_qkv
    grad_normed = jnp.dot(
        section,
        lax.all_gather(w_qkv, ("lon", "lat"), axis=0, tiled=True),
        preferred_element_type=jnp.float32,
    )
    grad_pre = inverse * (
        grad_normed
        - jnp.mean(grad_normed, axis=-1, keepdims=True)
        - normal * jnp.mean(grad_normed * normal, axis=-1, keepdims=True)
    )
    grad_pre = grad_pre.astype(jnp.bfloat16).reshape(rows, cols, depth, width)
    branch_grid = branch.reshape(rows, cols, depth, width)
    edge_branch, edge_grads = shifted_2((branch_grid[:, -half:], grad_pre[:, -half:]), "lon", 1)
    placed_branch = jnp.concatenate([edge_branch, branch_grid[:, :-half]], axis=1)
    placed_grads = jnp.concatenate([edge_grads, grad_pre[:, :-half]], axis=1)
    rim_branch, rim_grads = shifted_2((placed_branch[-half:], placed_grads[-half:]), "lat", 1)
    branch_back = jnp.concatenate([rim_branch, placed_branch[:-half]], axis=0)
    grad_back = jnp.concatenate([rim_grads, placed_grads[:-half]], axis=0)
    block_out = (fields.astype(jnp.float32) + branch_back.astype(jnp.float32)).astype(jnp.bfloat16)
    grad_fields = (grad_output.astype(jnp.float32) + grad_back.astype(jnp.float32)).astype(
        jnp.bfloat16
    )
    return (block_out, grad_fields, grad_w_qkv, grad_w_proj)


def solution(mesh):
    return jax.shard_map(
        shards,
        mesh=mesh,
        in_specs=(
            P("lat", "lon", None, None),
            P("lat"),
            P(("lon", "lat"), None),
            P(("lon", "lat"), None),
            P("lat", "lon", None, None),
        ),
        out_specs=(
            P("lat", "lon", None, None),
            P("lat", "lon", None, None),
            P(("lon", "lat"), None),
            P(("lon", "lat"), None),
        ),
        check_vma=False,
    )
```

profile of v0, /device:TPU:0, one launch (start us, length us, event | category | flops | bytes accessed | tf_op | source)
XLA Modules:
  0.0 610.3 jit_solution(13301376276490204644)
XLA Ops:
  24.0 82.5 %all_gather.9 = bf16[512,512]{1,0:T(8,128)(2,1)} all-gather(bf16[16,512]{1,0:T(8,128)(2,1)S(1)} %copy-done.18), channel_id=1, replica_groups=mesh['lon'=8,'lat'=4] {'lon','lat'}, dimensions={0}, use_global_device_ids=true | all-gather | bytes 540672 | tf_op jit(solution)/shard_map/all_gather | solution.py:114
  166.9 8.1 %convolution_convert_fusion = bf16[1728,1536]{1,0:T(8,128)(2,1)} fusion(bf16[1536,512]{1,0:T(8,128)(2,1)} %all-gather.2.cloned.1.call-done, f32[1728,512]{1,0:T(8,128)S(1)} %reshape.241, f32[1728]{0:T(1024)S(1)} %rsqrt.13, f32[1728]{0:T(1024)} %div.31), kind=kOutput, calls=%fused_computation.61 | convolution fusion | flops 2723217408 | bytes 10434048 | tf_op jit(solution)/shard_map/dot_general | solution.py:102
  175.0 12.9 %reshape_reshape.12 = bf16[2,12,2,12,3,1536]{5,4,3,2,1,0:T(4,128)(2,1)} reshape(bf16[1728,1536]{1,0:T(8,128)(2,1)} %convolution_convert_fusion) | data formatting | bytes 10616832 | tf_op jit(solution)/shard_map/reshape;reshape | solution.py:22
  187.9 13.7 %copy.52 = bf16[2,2,12,12,3,1536]{5,1,0,4,3,2:T(2,128)(2,1)} copy(bf16[2,2,12,12,3,1536]{5,4,3,1,2,0:T(4,128)(2,1)} %bitcast.147) | data formatting | bytes 10616832 | tf_op jit(solution)/shard_map/transpose | solution.py:23
  201.6 12.6 %reshape.233 = bf16[4,432,1536]{2,0,1:T(4,128)(2,1)} reshape(bf16[2,2,12,12,3,1536]{5,1,0,4,3,2:T(2,128)(2,1)} %copy.52) | data formatting | bytes 10616832 | tf_op jit(solution)/shard_map/reshape | solution.py:23
  214.1 10.3 %copy.53 = bf16[4,432,1536]{1,2,0:T(8,128)(2,1)} copy(bf16[4,432,1536]{2,0,1:T(4,128)(2,1)} %reshape.233) | data formatting | bytes 10616832 | tf_op jit(solution)/shard_map/while | solution.py:109
  224.5 47.5 %while.20 = (s32[]{:T(128)}, bf16[4,432,512]{1,2,0:T(8,128)(2,1)}, bf16[4,432,1536]{1,2,0:T(8,128)(2,1)}, s32[4,432]{1,0:T(4,128)S(1)}, s32[]{:T(128)}) while((s32[]{:T(128)}, bf16[4,432,512]{1,2,0:T(8,128)(2,1)}, bf16[4,432,1536]{1,2,0:T(8,128)(2,1)}, s32[4,432]{1,0:T(4,128)S(1)}, s32[]{:T(128)}) %tuple.50), condition=%wide.region_5.6_spmd, body=%wide.region_2.5_spmd.sunk | while | flops 391572160 | bytes 18023312 | solution.py:109
  226.2 5.5 fusion.94
  238.1 5.6 fusion.94
  249.9 5.6 fusion.94
  261.8 5.6 fusion.94
  287.6 162.2 %while.21 = (s32[]{:T(128)}, bf16[4,432,1536]{1,2,0:T(8,128)(2,1)}, bf16[4,432,1536]{1,2,0:T(8,128)(2,1)}, s32[4,432]{1,0:T(4,128)S(1)}, bf16[4,432,512]{1,2,0:T(8,128)(2,1)}, /*index=5*/s32[]{:T(128)}) while((s32[]{:T(128)}, bf16[4,432,1536]{1,2,0:T(8,128)(2,1)}, bf16[4,432,1536]{1,2,0:T(8,128)(2,1)}, s32[4,432]{1,0:T(4,128)S(1)}, ...), condition=%wide.region_10.11_spmd, body=%wide.region_6.10_spmd.sunk | while | flops 987560256 | bytes 89053592 | solution.py:133
  290.6 5.5 fusion.101
  304.3 12.1 %fusion.105 = bf16[432,1,8,64]{0,3,2,1:T(8,128)(2,1)S(1)} fusion(f32[8,432,432]{1,2,0:T(8,128)} %fusion.103, bf16[432,3,8,64]{0,3,2,1:T(8,128)(2,1)S(1)} %bitcast.141, f32[8,432,432]{1,2,0:T(8,128)} %get-tuple-element.170, f32[8,432]{1,0:T(8,128)S(1)} %get-tuple-element.171), kind=kOutput, calls=%fused_computation.43.clone.1 | convolution fusion | flops 201778992 | bytes 29310976 | tf_op jit(solution)/shard_map/while/body/eval_jaxpr/hqk,khd->qhd/dot_general | solution.py:79
  316.4 10.4 %fusion.104 = bf16[432,1,8,64]{0,3,2,1:T(8,128)(2,1)S(1)} fusion(f32[8,432,432]{1,2,0:T(8,128)} %fusion.103, bf16[432,3,8,64]{0,3,2,1:T(8,128)(2,1)S(1)} %bitcast.142, f32[8,432,432]{1,2,0:T(8,128)} %get-tuple-element.170, f32[8,432]{1,0:T(8,128)S(1)} %get-tuple-element.171), kind=kOutput, calls=%fused_computation.42.clone.1 | convolution fusion | flops 201778992 | bytes 29310976 | tf_op jit(solution)/shard_map/while/body/eval_jaxpr/hqk,qhd->khd/dot_general | solution.py:80
  331.1 5.5 fusion.101
  344.8 12.1 %fusion.105 = bf16[432,1,8,64]{0,3,2,1:T(8,128)(2,1)S(1)} fusion(f32[8,432,432]{1,2,0:T(8,128)} %fusion.103, bf16[432,3,8,64]{0,3,2,1:T(8,128)(2,1)S(1)} %bitcast.141, f32[8,432,432]{1,2,0:T(8,128)} %get-tuple-element.170, f32[8,432]{1,0:T(8,128)S(1)} %get-tuple-element.171), kind=kOutput, calls=%fused_computation.43.clone.1 | convolution fusion | flops 201778992 | bytes 29310976 | tf_op jit(solution)/shard_map/while/body/eval_jaxpr/hqk,khd->qhd/dot_general | solution.py:79
  356.9 10.4 %fusion.104 = bf16[432,1,8,64]{0,3,2,1:T(8,128)(2,1)S(1)} fusion(f32[8,432,432]{1,2,0:T(8,128)} %fusion.103, bf16[432,3,8,64]{0,3,2,1:T(8,128)(2,1)S(1)} %bitcast.142, f32[8,432,432]{1,2,0:T(8,128)} %get-tuple-element.170, f32[8,432]{1,0:T(8,128)S(1)} %get-tuple-element.171), kind=kOutput, calls=%fused_computation.42.clone.1 | convolution fusion | flops 201778992 | bytes 29310976 | tf_op jit(solution)/shard_map/while/body/eval_jaxpr/hqk,qhd->khd/dot_general | solution.py:80
  371.6 5.5 fusion.101
  385.3 12.1 %fusion.105 = bf16[432,1,8,64]{0,3,2,1:T(8,128)(2,1)S(1)} fusion(f32[8,432,432]{1,2,0:T(8,128)} %fusion.103, bf16[432,3,8,64]{0,3,2,1:T(8,128)(2,1)S(1)} %bitcast.141, f32[8,432,432]{1,2,0:T(8,128)} %get-tuple-element.170, f32[8,432]{1,0:T(8,128)S(1)} %get-tuple-element.171), kind=kOutput, calls=%fused_computation.43.clone.1 | convolution fusion | flops 201778992 | bytes 29310976 | tf_op jit(solution)/shard_map/while/body/eval_jaxpr/hqk,khd->qhd/dot_general | solution.py:79
  397.4 10.4 %fusion.104 = bf16[432,1,8,64]{0,3,2,1:T(8,128)(2,1)S(1)} fusion(f32[8,432,432]{1,2,0:T(8,128)} %fusion.103, bf16[432,3,8,64]{0,3,2,1:T(8,128)(2,1)S(1)} %bitcast.142, f32[8,432,432]{1,2,0:T(8,128)} %get-tuple-element.170, f32[8,432]{1,0:T(8,128)S(1)} %get-tuple-element.171), kind=kOutput, calls=%fused_computation.42.clone.1 | convolution fusion | flops 201778992 | bytes 29310976 | tf_op jit(solution)/shard_map/while/body/eval_jaxpr/hqk,qhd->khd/dot_general | solution.py:80
  412.1 5.5 fusion.101
  425.9 12.0 %fusion.105 = bf16[432,1,8,64]{0,3,2,1:T(8,128)(2,1)S(1)} fusion(f32[8,432,432]{1,2,0:T(8,128)} %fusion.103, bf16[432,3,8,64]{0,3,2,1:T(8,128)(2,1)S(1)} %bitcast.141, f32[8,432,432]{1,2,0:T(8,128)} %get-tuple-element.170, f32[8,432]{1,0:T(8,128)S(1)} %get-tuple-element.171), kind=kOutput, calls=%fused_computation.43.clone.1 | convolution fusion | flops 201778992 | bytes 29310976 | tf_op jit(solution)/shard_map/while/body/eval_jaxpr/hqk,khd->qhd/dot_general | solution.py:79
  437.9 10.4 %fusion.104 = bf16[432,1,8,64]{0,3,2,1:T(8,128)(2,1)S(1)} fusion(f32[8,432,432]{1,2,0:T(8,128)} %fusion.103, bf16[432,3,8,64]{0,3,2,1:T(8,128)(2,1)S(1)} %bitcast.142, f32[8,432,432]{1,2,0:T(8,128)} %get-tuple-element.170, f32[8,432]{1,0:T(8,128)S(1)} %get-tuple-element.171), kind=kOutput, calls=%fused_computation.42.clone.1 | convolution fusion | flops 201778992 | bytes 29310976 | tf_op jit(solution)/shard_map/while/body/eval_jaxpr/hqk,qhd->khd/dot_general | solution.py:80
  449.8 10.3 %copy.67 = bf16[4,432,1536]{2,0,1:T(4,128)(2,1)} copy(bf16[4,432,1536]{1,2,0:T(8,128)(2,1)} %get-tuple-element.54) | data formatting | bytes 10616832 | tf_op jit(solution)/shard_map/while | solution.py:133
  460.1 11.8 %reshape.239 = bf16[2,2,12,12,3,1536]{5,1,0,4,3,2:T(2,128)(2,1)} reshape(bf16[4,432,1536]{2,0,1:T(4,128)(2,1)} %copy.67) | data formatting | bytes 10616832 | tf_op jit(solution)/shard_map/reshape | solution.py:29
  471.9 9.5 %copy.68 = bf16[2,12,2,12,3,1536]{5,4,3,2,1,0:T(4,128)(2,1)} copy(bf16[2,12,2,12,3,1536]{5,2,0,4,3,1:T(2,128)(2,1)} %bitcast.148) | data formatting | bytes 10616832 | tf_op jit(solution)/shard_map/transpose | solution.py:30
  481.4 13.9 %reshape_reshape.15 = bf16[1728,1536]{1,0:T(8,128)(2,1)} reshape(bf16[2,12,2,12,3,1536]{5,4,3,2,1,0:T(4,128)(2,1)} %copy.68) | data formatting | bytes 10616832 | tf_op jit(solution)/shard_map/reshape;reshape | solution.py:134
  495.3 7.2 %convolution_multiply_fusion = f32[1536,512]{1,0:T(8,128)} fusion(bf16[1728,1536]{1,0:T(8,128)(2,1)} %reshape_reshape.15, bf16[1728,512]{1,0:T(8,128)(2,1)S(1)} %copy-done.11), kind=kOutput, calls=%fused_computation.69 | convolution fusion | flops 2718695424 | bytes 10223616 | tf_op jit(solution)/shard_map/dot_general | solution.py:137
  515.0 6.0 fusion.66
  538.5 5.5 collective-permute-done.3
  556.4 47.2 %reduce-scatter.3.cloned.1.call-done = f32[48,512]{1,0:T(8,128)} async-done(((f32[1536,512]{1,0:T(8,128)}), f32[48,512]{1,0:T(8,128)}) %reduce-scatter.3.cloned.1.call-update) | async-done | bytes 98320 | tf_op jit(solution)/shard_map/reduce_scatter | solution.py:136
  (185 shorter events, 209.7 us)
Async XLA Ops:
  7.2 5.6 slice-start
  7.2 159.7 %all-gather.2.cloned.1.call-start = ((), (), s32[]{:S(2)}) async-start(), calls=%async_computation.2 | async-start | bytes 1622016 | tf_op jit(solution)/shard_map/all_gather | solution.py:104
  7.9 548.5 %reduce-scatter.5.cloned.1.call-start = ((), (), s32[]{:S(2)}) async-start(), calls=%async_computation.4 | async-start | bytes 1081344 | tf_op jit(solution)/shard_map/reduce_scatter | solution.py:126
  8.0 5.7 copy-start.3
  9.3 9.2 %collective-permute-start = (bf16[24,6,3,512]{3,0,2,1:T(8,128)(2,1)S(1)}, bf16[24,6,3,512]{3,0,2,1:T(8,128)(2,1)S(1)}, u32[]{:S(2)}, u32[]{:S(2)}) collective-permute-start(bf16[24,6,3,512]{3,0,2,1:T(8,128)(2,1)S(1)} %copy.80), channel_id=1, source_target_pairs={{4,0},{8,4},{12,8},{16,12},{20,16},{24,20},{28,24},{0,28},{5,1},{9... | collective-permute-start | bytes 1327112 | tf_op jit(solution)/shard_map/ppermute | solution.py:17
  12.9 97.6 %collective-permute-start.4 = (bf16[24,6,3,512]{3,0,2,1:T(8,128)(2,1)S(1)}, bf16[24,6,3,512]{3,0,2,1:T(8,128)(2,1)}, u32[]{:S(2)}, u32[]{:S(2)}) collective-permute-start(bf16[24,6,3,512]{3,0,2,1:T(8,128)(2,1)S(1)} %copy.81), channel_id=1, source_target_pairs={{4,0},{8,4},{12,8},{16,12},{20,16},{24,20},{28,24},{0,28},{5,1},{9... | collective-permute-start | bytes 1327112 | tf_op jit(solution)/shard_map/ppermute | solution.py:17
  14.5 9.4 %copy-start.18 = (bf16[16,512]{1,0:T(8,128)(2,1)S(1)}, bf16[16,512]{1,0:T(8,128)(2,1)}, u32[]{:S(2)}) copy-start(bf16[16,512]{1,0:T(8,128)(2,1)} %param.12) | copy-start | bytes 49156
  18.7 0.8 copy-start.10
  20.4 89.7 %copy-start.20 = (s32[24]{0:T(128)S(1)}, s32[24]{0:T(128)}, u32[]{:S(2)}) copy-start(s32[24]{0:T(128)} %param.10) | copy-start | bytes 292
  20.4 95.9 %collective-permute-start.1 = (bf16[6,24,3,512]{3,1,2,0:T(8,128)(2,1)}, bf16[6,24,3,512]{3,1,2,0:T(8,128)(2,1)S(1)}, u32[]{:S(2)}, u32[]{:S(2)}) collective-permute-start(bf16[6,24,3,512]{3,1,2,0:T(8,128)(2,1)} %pad_maximum_fusion.8), channel_id=1, source_target_pairs={{1,0},{2,1},{3,2},{0,3},{5,4},{6,5},{7,6},{4,7},{9,8},{10,9},{11,1... | collective-permute-start | bytes 1327112 | tf_op jit(solution)/shard_map/ppermute | solution.py:17
  111.6 3.3 copy-start
  113.6 15.7 %collective-permute-start.5 = (bf16[6,24,3,512]{3,1,2,0:T(8,128)(2,1)}, bf16[6,24,3,512]{3,1,2,0:T(8,128)(2,1)}, u32[]{:S(2)}, u32[]{:S(2)}) collective-permute-start(bf16[6,24,3,512]{3,1,2,0:T(8,128)(2,1)} %pad_maximum_fusion.7), channel_id=1, source_target_pairs={{1,0},{2,1},{3,2},{0,3},{5,4},{6,5},{7,6},{4,7},{9,8},{10,9},{11,1... | collective-permute-start | bytes 1327112 | tf_op jit(solution)/shard_map/ppermute | solution.py:17
  116.6 1.1 copy-start.12
  118.3 48.5 %copy-start.15 = (f32[1728]{0:T(1024)}, f32[1728]{0:T(1024)S(1)}, u32[]{:S(2)}) copy-start(f32[1728]{0:T(1024)S(1)} %rsqrt.13) | copy-start | bytes 20740
  137.6 3.7 copy-start.9
  166.8 8.2 %copy-start.1 = (f32[1728,512]{1,0:T(8,128)}, f32[1728,512]{1,0:T(8,128)S(1)}, u32[]{:S(2)}) copy-start(f32[1728,512]{1,0:T(8,128)S(1)} %reshape.241) | copy-start | bytes 10616836
  287.5 316.1 %reduce-scatter.3.cloned.1.call-start = ((), (), s32[]{:S(2)}) async-start(), calls=%async_computation.3 | async-start | bytes 3244032 | tf_op jit(solution)/shard_map/reduce_scatter | solution.py:136
  481.4 13.9 %copy-start.11 = (bf16[1728,512]{1,0:T(8,128)(2,1)S(1)}, bf16[1728,512]{1,0:T(8,128)(2,1)}, u32[]{:S(2)}) copy-start(bf16[1728,512]{1,0:T(8,128)(2,1)} %convert_element_type.112) | copy-start | bytes 5308420
  502.5 1.5 copy-start.8
  502.5 1.6 copy-start.13
  510.0 1.5 copy-start.7
  511.5 3.5 copy-start.2
  511.5 3.5 copy-start.16
  511.5 3.5 copy-start.17
  511.5 3.5 copy-start.19
  515.0 12.0 %collective-permute-start.2 = (bf16[24,6,3,512]{3,0,2,1:T(8,128)(2,1)}, bf16[24,6,3,512]{3,0,2,1:T(8,128)(2,1)}, u32[]{:S(2)}, u32[]{:S(2)}) collective-permute-start(bf16[24,6,3,512]{3,0,2,1:T(8,128)(2,1)} %copy.56), channel_id=1, source_target_pairs={{28,0},{0,4},{4,8},{8,12},{12,16},{16,20},{20,24},{24,28},{29,1},{... | collective-permute-start | bytes 1327112 | tf_op jit(solution)/shard_map/ppermute | solution.py:17
  526.9 4.4 copy-start.6
  526.9 8.7 %collective-permute-start.6 = (bf16[24,6,3,512]{3,0,2,1:T(8,128)(2,1)S(1)}, bf16[24,6,3,512]{3,0,2,1:T(8,128)(2,1)S(1)}, u32[]{:S(2)}, u32[]{:S(2)}) collective-permute-start(bf16[24,6,3,512]{3,0,2,1:T(8,128)(2,1)S(1)} %copy.69), channel_id=1, source_target_pairs={{28,0},{0,4},{4,8},{8,12},{12,16},{16,20},{20,24},{24,28},{29,1},{... | collective-permute-start | bytes 1327112 | tf_op jit(solution)/shard_map/ppermute | solution.py:17
  528.9 15.1 %collective-permute-start.3 = (bf16[6,24,3,512]{3,1,2,0:T(8,128)(2,1)S(1)}, bf16[6,24,3,512]{3,1,2,0:T(8,128)(2,1)S(1)}, u32[]{:S(2)}, u32[]{:S(2)}) collective-permute-start(bf16[6,24,3,512]{3,1,2,0:T(8,128)(2,1)S(1)} %copy.58), channel_id=1, source_target_pairs={{3,0},{0,1},{1,2},{2,3},{7,4},{4,5},{5,6},{6,7},{11,8},{8,9},{9,10... | collective-permute-start | bytes 1327112 | tf_op jit(solution)/shard_map/ppermute | solution.py:17
  535.9 8.4 %copy-start.4 = (bf16[24,24,3,512]{3,1,2,0:T(8,128)(2,1)S(1)}, bf16[24,24,3,512]{3,1,2,0:T(8,128)(2,1)}, u32[]{:S(2)}) copy-start(bf16[24,24,3,512]{3,1,2,0:T(8,128)(2,1)} %param.9) | copy-start | bytes 5308420
  536.4 16.2 %collective-permute-start.7 = (bf16[6,24,3,512]{3,1,2,0:T(8,128)(2,1)S(1)}, bf16[6,24,3,512]{3,1,2,0:T(8,128)(2,1)S(1)}, u32[]{:S(2)}, u32[]{:S(2)}) collective-permute-start(bf16[6,24,3,512]{3,1,2,0:T(8,128)(2,1)S(1)} %copy.71), channel_id=1, source_target_pairs={{3,0},{0,1},{1,2},{2,3},{7,4},{4,5},{5,6},{6,7},{11,8},{8,9},{9,10... | collective-permute-start | bytes 1327112 | tf_op jit(solution)/shard_map/ppermute | solution.py:17
  546.1 6.7 %copy-start.5 = (bf16[24,24,3,512]{3,1,2,0:T(8,128)(2,1)S(1)}, bf16[24,24,3,512]{3,1,2,0:T(8,128)(2,1)}, u32[]{:S(2)}) copy-start(bf16[24,24,3,512]{3,1,2,0:T(8,128)(2,1)} %param.13) | copy-start | bytes 5308420
  (1 other events, 0.6 us)
Sparse Core Ops, SparseCore 0:
  10.9 63.3 all-gather.1
  287.6 135.7 reduce-scatter.4
  502.6 100.9 reduce-scatter.2
where the time goes:
time: 618 us; the launch traced here: 610 us
  matrix products  213 us (34%)
  local copies, waits for them, and re-layouts  202 us (33%)
  blocking collectives  82.5 us (13%)
  waiting for transfers between devices  65.9 us (11%)
  other arithmetic  18.9 us (3%)
  between operations  14.4 us (2%)
  starting transfers between devices  12.3 us (2%)
    all_gather x1, blocking collectives, shards(): lax.all_gather(w_proj, ('lon', 'lat'), axis=0, tiled=True)  82.5 us
    dot_general x4, matrix products, backward_window(): jnp.einsum('hqk,khd->qhd', grad_scores, keys, preferred_element_type=jnp....  48.2 us
    reduce_scatter x1, waiting for transfers between devices, shards(): lax.psum_scatter(jnp.dot(section.T, normed, preferred_element_type=jnp.fl...  47.2 us
    sub x8, matrix products, attention_probs(): weights = jnp.exp(scores - peak)  44.4 us
    dot_general x4, matrix products, backward_window(): jnp.einsum('hqk,qhd->khd', grad_scores, query, preferred_element_type=jnp...  41.7 us
    transpose x2, local copies, waits for them, and re-layouts, to_windows(): blocks.transpose(0, 2, 1, 3, 4, 5).reshape(-1, side * side * depth, width)  18.1 us
    another operation x2, local copies, waits for them, and re-layouts, to_windows(): blocks = grid.reshape(rows // side, side, cols // side, side, depth, width)  18 us
    ppermute x8, waiting for transfers between devices, shifted_2(): return lax.ppermute(block, axis, route)  17.9 us
  transfers between devices with their start and end apart: 11, of which 5 were waited for; matrix products, arithmetic and copies ran while one was open for 51% of the time, Pallas kernels for 0%

commit v1 on v0

v1 whole, which is shorter than its diff:
```python
import functools

import jax
import jax.numpy as jnp
from jax import lax
from jax.experimental import pallas as pl
from jax.experimental.pallas import tpu as pltpu
from jax.sharding import PartitionSpec as P

HEADS = 8
HEAD = 64
WIN = 12
HALF = WIN // 2
EPSILON = 1e-05
AXES = ("lon", "lat")
LANES = 128
SUB = 8


F32 = jnp.float32
BF16 = jnp.bfloat16


def nt(a, b):
    return lax.dot_general(a, b, (((1,), (1,)), ((), ())), preferred_element_type=F32)


def nn(a, b):
    return lax.dot_general(a, b, (((1,), (0,)), ((), ())), preferred_element_type=F32)


def sub_index(width):
    return lax.broadcasted_iota(jnp.int32, (SUB, width), 0)


def pick(own, strip):
    s = sub_index(own.shape[1])
    t0a, t1a, t2a, t0b, t1b, t2b = [own[8 * i : 8 * i + 8] for i in range(6)]
    ha, hb = strip[:8], strip[8:]
    mixed = jnp.where(
        s < 2,
        t2a,
        jnp.where(s < 4, pltpu.roll(t2b, 2, 0), jnp.where(s < 6, pltpu.roll(t0b, 6, 0), t0a)),
    )
    first = jnp.concatenate([t1a, t1b, mixed], axis=0)
    n1 = jnp.where(s < 2, ha, t2a)
    n2 = jnp.where(s < 2, hb, t2b)
    n3 = jnp.where((s >= 2) & (s < 6), ha, pltpu.roll(hb, 4, 0))
    second = jnp.concatenate([n1, n2, n3], axis=0)
    return first, second


def unpick(first, second):
    s = sub_index(first.shape[1])
    t1a, t1b, mixed = first[:8], first[8:16], first[16:]
    n1, n2, n3 = second[:8], second[8:16], second[16:]
    zero = jnp.zeros_like(mixed)
    t0a = jnp.where(s >= 6, mixed, zero)
    t0b = jnp.where(s >= 6, pltpu.roll(mixed, 2, 0), zero)
    t2a = jnp.where(s < 2, mixed, n1)
    t2b = jnp.where(s < 2, pltpu.roll(mixed, 6, 0), n2)
    ha = jnp.where(s < 2, n1, n3)
    hb = jnp.where(s < 2, n2, pltpu.roll(n3, 4, 0))
    own = jnp.concatenate([t0a, t1a, t2a, t0b, t1b, t2b], axis=0)
    return own, jnp.concatenate([ha, hb], axis=0)


def token_regions(region_ids, levels):
    lines = jnp.repeat(region_ids, levels)
    pairs = lines.reshape(-1, 2)
    s = jnp.arange(3 * SUB)
    inner = s % SUB
    line0 = jnp.where(s < 8, 0, jnp.where(s < 16, 1, jnp.where((inner < 2) | (inner >= 6), 0, 1)))
    line1 = jnp.where(s < 8, 0, jnp.where(s < 16, 1, jnp.where((inner >= 2) & (inner < 6), 0, 1)))
    a, b = pairs[:, :1], pairs[:, 1:]
    both = jnp.stack([jnp.where(line0 == 0, a, b), jnp.where(line1 == 0, a, b)])
    per_band = WIN * levels // 2
    bands = pairs.shape[0] // per_band
    return both.reshape(2, bands, per_band * 3 * SUB).transpose(1, 0, 2)


def assemble_kernel(own_ref, low_ref, east_ref, corner_ref, g_own, g_low, g_east, g_corner,
                    normed_ref, inv_ref, gs_ref, *, skip, upper):
    per_band = normed_ref.shape[2]

    def norm(block):
        centre = block - jnp.mean(block, axis=-1, keepdims=True)
        inverse = lax.rsqrt(jnp.mean(centre * centre, axis=-1, keepdims=True) + EPSILON)
        return (centre * inverse).astype(BF16), inverse

    def step(own, strip, g_o, g_s, at):
        band, place = at // per_band, at % per_band
        firsts = pick(own.astype(F32), strip.astype(F32))
        grads = pick(g_o.astype(F32), g_s.astype(F32))
        for j in range(2):
            normed, inverse = norm(firsts[j])
            normed_ref[band, j, place] = normed
            inv_ref[band, j, place] = jnp.broadcast_to(inverse, (3 * SUB, LANES))
            gs_ref[band, j, place] = grads[j].astype(BF16)

    @pl.loop(0, upper)
    def _(p):
        step(own_ref[p + skip], east_ref[p], g_own[p + skip], g_east[p], p)

    @pl.loop(0, skip)
    def _(p):
        step(low_ref[p], corner_ref[p], g_low[p], g_corner[p], p + upper)


def assemble(fields, low, east, corner, grads, g_low, g_east, g_corner):
    pairs, _, width = fields.shape
    skip = low.shape[0]
    upper = east.shape[0]
    per_band = 2 * skip
    bands = (upper + skip) // per_band
    shape = (bands, 2, per_band, 3 * SUB)
    return pl.pallas_call(
        functools.partial(assemble_kernel, skip=skip, upper=upper),
        out_shape=(
            jax.ShapeDtypeStruct(shape + (width,), BF16),
            jax.ShapeDtypeStruct(shape + (LANES,), F32),
            jax.ShapeDtypeStruct(shape + (width,), BF16),
        ),
        name="assemble",
    )(fields, low, east, corner, grads, g_low, g_east, g_corner)


def attention_kernel(normed_ref, gs_ref, reg_col_ref, reg_row_ref, w_ref, wp_ref,
                     att_ref, gqkv_ref, gw_ref, gp_ref, gw_acc, gp_acc):
    window = pl.program_id(1)
    scale = HEAD ** (-0.5)
    normed = normed_ref[window]
    grads = gs_ref[window]
    count = normed.shape[0]
    weights = w_ref[...].reshape(3 * LANES, w_ref.shape[2])
    qkv = nt(normed, weights).astype(BF16)
    query, keys, values = [qkv[:, LANES * i : LANES * (i + 1)] for i in range(3)]
    query = query * jnp.asarray(scale, BF16)
    grad_att = nn(grads, wp_ref[...]).astype(BF16)
    keys_t = keys.astype(F32).T.astype(BF16) * jnp.asarray(scale, BF16)
    values_t = values.astype(F32).T.astype(BF16)
    allowed = reg_col_ref[window] == reg_row_ref[window]
    lane = lax.broadcasted_iota(jnp.int32, (count, LANES), 1)
    att_t, grad_q_t = [], []
    grad_k = grad_v = None
    for h in range(LANES // HEAD):
        mine = (lane >= h * HEAD) & (lane < (h + 1) * HEAD)
        zero = jnp.zeros((), BF16)
        rows = slice(h * HEAD, (h + 1) * HEAD)
        scores = nt(jnp.where(mine, keys, zero), query)
        scores = jnp.where(allowed, scores, -1e30)
        peak = jnp.max(scores, axis=0, keepdims=True)
        expo = jnp.exp(scores - peak)
        probs = expo * (1.0 / jnp.sum(expo, axis=0, keepdims=True))
        rounded = probs.astype(BF16)
        grad_probs = nt(jnp.where(mine, values, zero), grad_att)
        inner = jnp.sum(grad_probs * probs, axis=0, keepdims=True)
        grad_scores = (probs * (grad_probs - inner)).astype(BF16)
        att_t.append(nn(values_t[rows], rounded))
        grad_q_t.append(nn(keys_t[rows], grad_scores))
        part_v = nn(rounded, jnp.where(mine, grad_att, zero))
        part_k = nn(grad_scores, jnp.where(mine, query, zero))
        grad_v = part_v if grad_v is None else grad_v + part_v
        grad_k = part_k if grad_k is None else grad_k + part_k
    att_t = jnp.concatenate(att_t, axis=0)
    grad_q_t = jnp.concatenate(grad_q_t, axis=0)
    att_ref[0] = att_t.T.astype(BF16)
    gqkv_ref[0, 0] = grad_q_t.T.astype(BF16)
    gqkv_ref[0, 1] = grad_k.astype(BF16)
    gqkv_ref[0, 2] = grad_v.astype(BF16)
    grad_w = (
        nn(grad_q_t.astype(BF16), normed),
        nn(grad_k.T.astype(BF16), normed),
        nn(grad_v.T.astype(BF16), normed),
    )
    grad_p = nn(att_t.astype(BF16), grads)

    @pl.when(window == 0)
    def _():
        for i in range(3):
            gw_acc[i] = grad_w[i]
        gp_acc[...] = grad_p

    @pl.when(window > 0)
    def _():
        for i in range(3):
            gw_acc[i] += grad_w[i]
        gp_acc[...] += grad_p

    @pl.when(window == pl.num_programs(1) - 1)
    def _():
        gw_ref[...] = gw_acc[...]
        gp_ref[...] = gp_acc[...]


def attention(normed, gs, reg_col, reg_row, w_qkv, w_proj):
    windows, count, width = normed.shape
    groups = width // LANES
    whole = lambda *shape: pl.BlockSpec(shape, lambda p, w: (0,) * len(shape))
    return pl.pallas_call(
        attention_kernel,
        grid=(groups, windows),
        in_specs=[
            whole(windows, count, width),
            whole(windows, count, width),
            whole(windows, count, 1),
            whole(windows, 1, count),
            pl.BlockSpec((3, LANES, width), lambda p, w: (0, p, 0)),
            pl.BlockSpec((width, LANES), lambda p, w: (0, p)),
        ],
        out_specs=[
            pl.BlockSpec((1, count, LANES), lambda p, w: (w, 0, p)),
            pl.BlockSpec((1, 3, count, LANES), lambda p, w: (w, 0, 0, p)),
            pl.BlockSpec((3, LANES, width), lambda p, w: (0, p, 0)),
            pl.BlockSpec((LANES, width), lambda p, w: (p, 0)),
        ],
        out_shape=(
            jax.ShapeDtypeStruct((windows, count, width), BF16),
            jax.ShapeDtypeStruct((windows, 3, count, width), BF16),
            jax.ShapeDtypeStruct((3, width, width), F32),
            jax.ShapeDtypeStruct((width, width), F32),
        ),
        scratch_shapes=[pltpu.VMEM((3, LANES, width), F32), pltpu.VMEM((LANES, width), F32)],
        name="attention",
    )(normed, gs, reg_col, reg_row, w_qkv, w_proj)


def finish_kernel(att_ref, gqkv_ref, normed_ref, inv_ref, w_ref, wp_ref, fields_ref, grads_ref,
                  out_ref, gout_ref, low_ref, east_ref, corner_ref, g_low, g_east, g_corner,
                  branch_scr, pre_scr):
    band = pl.program_id(0)
    skip = low_ref.shape[0]
    per_band = 2 * skip
    width = wp_ref.shape[0]
    for j in range(2):
        branch = nt(att_ref[0, j], wp_ref[...])
        branch_scr[j] = branch.astype(BF16).astype(F32).reshape(per_band, 3 * SUB, width)
        grad_normed = nn(gqkv_ref[0, j, 0], w_ref[0])
        grad_normed += nn(gqkv_ref[0, j, 1], w_ref[1])
        grad_normed += nn(gqkv_ref[0, j, 2], w_ref[2])
        normal = normed_ref[0, j].astype(F32)
        mean = jnp.mean(grad_normed, axis=-1, keepdims=True)
        along = jnp.mean(grad_normed * normal, axis=-1, keepdims=True)
        pre = inv_ref[0, j][:, :1] * (grad_normed - mean - normal * along)
        pre_scr[j] = pre.astype(BF16).astype(F32).reshape(per_band, 3 * SUB, width)

    def own(p, at):
        add, strip = unpick(branch_scr[0, p], branch_scr[1, p])
        out_ref[at] = (fields_ref[at].astype(F32) + add).astype(BF16)
        east_ref[at - skip] = strip.astype(BF16)
        add, strip = unpick(pre_scr[0, p], pre_scr[1, p])
        gout_ref[at] = (grads_ref[at].astype(F32) + add).astype(BF16)
        g_east[at - skip] = strip.astype(BF16)

    def away(p, at):
        add, strip = unpick(branch_scr[0, p], branch_scr[1, p])
        low_ref[at] = add.astype(BF16)
        corner_ref[at] = strip.astype(BF16)
        add, strip = unpick(pre_scr[0, p], pre_scr[1, p])
        g_low[at] = add.astype(BF16)
        g_corner[at] = strip.astype(BF16)

    last = band == pl.num_programs(0) - 1

    @pl.loop(0, skip)
    def _(p):
        own(p, p + skip + band * per_band)

    @pl.when(jnp.logical_not(last))
    def _():
        @pl.loop(skip, per_band)
        def _(p):
            own(p, p + skip + band * per_band)

    @pl.when(last)
    def _():
        @pl.loop(skip, per_band)
        def _(p):
            away(p, p - skip)


def finish(att, gqkv, normed, inv, w_qkv, w_proj, fields, grads):
    bands, _, count, width = att.shape
    pairs = fields.shape[0]
    per_band = count // (3 * SUB)
    skip = per_band // 2
    upper = pairs - skip
    whole = lambda *shape: pl.BlockSpec(shape, lambda b: (0,) * len(shape))
    banded = lambda *shape: pl.BlockSpec((1,) + shape, lambda b: (b,) + (0,) * len(shape))
    outs = [(pairs, 48, width)] * 2 + [(skip, 48, width), (upper, 16, width), (skip, 16, width)] * 2
    return pl.pallas_call(
        finish_kernel,
        grid=(bands,),
        in_specs=[
            banded(2, count, width),
            banded(2, 3, count, width),
            banded(2, count, width),
            banded(2, count, LANES),
            whole(3, width, width),
            whole(width, width),
            whole(pairs, 48, width),
            whole(pairs, 48, width),
        ],
        out_specs=[whole(*shape) for shape in outs],
        out_shape=tuple(jax.ShapeDtypeStruct(shape, BF16) for shape in outs),
        scratch_shapes=[
            pltpu.VMEM((2, per_band, 3 * SUB, width), F32),
            pltpu.VMEM((2, per_band, 3 * SUB, width), F32),
        ],
        name="finish",
    )(att, gqkv, normed, inv, w_qkv, w_proj, fields, grads)


def edge_kernel(f_ref, o_ref, r_ref, g_ref, q_ref, gr_ref, out_ref, gout_ref):
    shape = f_ref.shape
    s = lax.broadcasted_iota(jnp.int32, shape, 1)
    for f, o, r, out in ((f_ref, o_ref, r_ref, out_ref), (g_ref, q_ref, gr_ref, gout_ref)):
        total = f[...].astype(F32) + r[...].astype(F32)
        out[...] = jnp.where(s < HALF, total, o[...].astype(F32)).astype(BF16)


def edge(fields, out, back, grads, gout, g_back, skip):
    lines, cols, width = fields.shape
    n = back.shape[0] // skip
    at = pl.BlockSpec((skip, SUB, width), lambda i: (i + 1, 0, 0))
    strip = pl.BlockSpec((skip, SUB, width), lambda i: (i, 0, 0))
    return pl.pallas_call(
        edge_kernel,
        grid=(n,),
        in_specs=[at, at, strip, at, at, strip],
        out_specs=[at, at],
        out_shape=(jax.ShapeDtypeStruct(out.shape, BF16),) * 2,
        input_output_aliases={1: 0, 4: 1},
        name="edge",
    )(fields, out, back, grads, gout, g_back)


def rim_kernel(f_ref, low_ref, c_ref, g_ref, g_low, gc_ref, out_any, gout_any, out_ref, gout_ref):
    for f, low, c, out in ((f_ref, low_ref, c_ref, out_ref), (g_ref, g_low, gc_ref, gout_ref)):
        back = low[...].astype(F32)
        s = lax.broadcasted_iota(jnp.int32, c.shape, 1)
        head = jnp.where(s < HALF, c[...].astype(F32), back[:, :SUB])
        back = jnp.concatenate([head, back[:, SUB:]], axis=1)
        out[...] = (f[...].astype(F32) + back).astype(BF16)


def rim(fields, low, corner, grads, g_low, g_corner, out, gout):
    skip = low.shape[0]
    _, cols, width = fields.shape
    at = pl.BlockSpec((skip, cols, width), lambda i: (0, 0, 0))
    strip = pl.BlockSpec((skip, SUB, width), lambda i: (0, 0, 0))
    anyw = pl.BlockSpec(memory_space=pl.ANY)
    return pl.pallas_call(
        rim_kernel,
        grid=(1,),
        in_specs=[at, at, strip, at, at, strip, anyw, anyw],
        out_specs=[at, at],
        out_shape=(jax.ShapeDtypeStruct(out.shape, BF16),) * 2,
        input_output_aliases={6: 0, 7: 1},
        name="rim",
    )(fields, low, corner, grads, g_low, g_corner, out, gout)


def linear(lon, lat, lats):
    return lon * lats + lat


def shift_by(block, step_lon, step_lat):
    lons, lats = lax.axis_size("lon"), lax.axis_size("lat")
    route = [
        (linear((i + step_lon) % lons, (j + step_lat) % lats, lats), linear(i, j, lats))
        for i in range(lons)
        for j in range(lats)
    ]
    return lax.ppermute(block, AXES, route)


def bit_order():
    lons, lats = lax.axis_size("lon"), lax.axis_size("lat")
    lat_bits = [1 << i for i in range(lats.bit_length() - 1)]
    lon_bits = [lats << i for i in range(lons.bit_length() - 1)]
    assert lats == 1 << len(lat_bits) and lons == 1 << len(lon_bits)
    return lat_bits, lon_bits


def swap(block, bit):
    total = lax.axis_size("lon") * lax.axis_size("lat")
    return lax.ppermute(block, AXES, [(i, i ^ bit) for i in range(total)])


def gather_rows(block):
    lat_bits, lon_bits = bit_order()
    order = lat_bits[::-1] + lon_bits[1:] + lon_bits[:1]
    bits = sorted(order)[::-1]
    place = lax.axis_index(AXES)
    held = block.reshape((1,) * len(bits) + block.shape)
    for bit in order:
        axis = bits.index(bit)
        other = swap(held, bit)
        high = (place & bit) != 0
        held = jnp.concatenate(
            [jnp.where(high, other, held), jnp.where(high, held, other)], axis=axis
        )
    return held.reshape((-1,) + block.shape[1:])


def scatter_sum(blocks):
    lat_bits, lon_bits = bit_order()
    order = lon_bits[:1] + lon_bits[1:][::-1] + lat_bits
    bits = sorted(order)[::-1]
    place = lax.axis_index(AXES)
    held = blocks.reshape((2,) * len(bits) + blocks.shape[1:])
    for bit in order:
        axis = bits.index(bit)
        mine = jnp.where((place & bit) != 0, 1, 0)
        keep = lax.dynamic_index_in_dim(held, mine, axis, keepdims=True)
        send = lax.dynamic_index_in_dim(held, 1 - mine, axis, keepdims=True).astype(BF16)
        held = keep + swap(send, bit).astype(F32)
    return held.reshape(blocks.shape[1:])


def lines_of(grid):
    rows, cols, levels, width = grid.shape
    return grid.transpose(0, 2, 1, 3).reshape(rows * levels, cols, width)


def grid_of(lines, levels):
    count, cols, width = lines.shape
    return lines.reshape(count // levels, levels, cols, width).transpose(0, 2, 1, 3)


def paired(lines):
    count, cols, width = lines.shape
    return lines.reshape(count // 2, 2 * cols, width)


def unpaired(pairs):
    count, cols, width = pairs.shape
    return pairs.reshape(count * 2, cols // 2, width)


def shards(fields, region_ids, w_qkv, w_proj, grad_output):
    rows, cols, levels, width = fields.shape
    skip = HALF * levels
    devices = lax.axis_size("lon") * lax.axis_size("lat")
    factor = float(rows * cols * levels * devices) ** (-0.5)
    w_all = gather_rows(w_qkv)
    p_all = gather_rows(w_proj)
    f_lines, g_lines = lines_of(fields), lines_of(grad_output)
    east, g_east = [shift_by(x[skip:, :SUB], 1, 0) for x in (f_lines, g_lines)]
    low, g_low = [shift_by(x[:skip], 0, 1) for x in (f_lines, g_lines)]
    corner, g_corner = [shift_by(x[:skip, :SUB], 1, 1) for x in (f_lines, g_lines)]
    normed, inv, gs = assemble(
        *[paired(x) for x in (f_lines, low, east, corner, g_lines, g_low, g_east, g_corner)]
    )
    bands = normed.shape[0]
    count = WIN * WIN * levels
    regions = token_regions(region_ids, levels).reshape(2 * bands, count)
    flat = lambda x: x.reshape(2 * bands, count, x.shape[-1])
    w3 = w_all.reshape(3, width, width)
    att, gqkv, grad_w, grad_p = attention(
        flat(normed), flat(gs), regions[:, :, None], regions[:, None, :], w3, p_all
    )
    blocks = jnp.concatenate(
        [
            grad_w.reshape(devices, -1, width),
            grad_p.T.reshape(devices, -1, width),
        ],
        axis=1,
    )
    out, gout, r_low, r_east, r_corner, gr_low, gr_east, gr_corner = finish(
        att.reshape(bands, 2, count, width),
        gqkv.reshape(bands, 2, 3, count, width),
        normed.reshape(bands, 2, count, width),
        inv.reshape(bands, 2, count, LANES),
        w3,
        p_all,
        paired(f_lines),
        paired(g_lines),
    )
    own = scatter_sum(blocks) * factor
    r_low, gr_low = [shift_by(unpaired(x), 0, -1) for x in (r_low, gr_low)]
    r_east, gr_east = [shift_by(unpaired(x), -1, 0) for x in (r_east, gr_east)]
    r_corner, gr_corner = [shift_by(unpaired(x), -1, -1) for x in (r_corner, gr_corner)]
    out, gout = edge(f_lines, unpaired(out), r_east, g_lines, unpaired(gout), gr_east, skip)
    out, gout = rim(f_lines, r_low, r_corner, g_lines, gr_low, gr_corner, out, gout)
    share = w_qkv.shape[0]
    return (grid_of(out, levels), grid_of(gout, levels), own[:share], own[share:])


def solution(mesh):
    return jax.shard_map(
        shards,
        mesh=mesh,
        in_specs=(
            P("lat", "lon", None, None),
            P("lat"),
            P(AXES, None),
            P(AXES, None),
            P("lat", "lon", None, None),
        ),
        out_specs=(
            P("lat", "lon", None, None),
            P("lat", "lon", None, None),
            P(AXES, None),
            P(AXES, None),
        ),
        check_vma=False,
    )
```

time: 618 us -> 213 us (0.34); the launches traced: 610 us -> 212 us
  matrix products: 213 us -> 0 us
  local copies, waits for them, and re-layouts: 202 us -> 17.9 us
  Pallas kernels: 0 us -> 83.5 us
  blocking collectives: 82.5 us -> 0 us
  starting transfers between devices: 12.3 us -> 26.7 us
  between operations: 14.4 us -> 1.05 us
  other arithmetic: 18.9 us -> 10.4 us
  waiting for transfers between devices: 65.9 us -> 72.5 us
    dot_general x26 -> x0, matrix products: 169 us -> none  [the longest x4 48.2 us: backward_window(): jnp.einsum('hqk,khd->qhd', grad_scores, keys, preferred_element_type=jnp....]
    pallas_call x0 -> x5, Pallas kernels: none -> 83.5 us  [the longest x1 52.9 us: attention(): pl.pallas_call(attention_kernel, grid=(groups, windows), in_specs=[whole(...]
    all_gather x1 -> x0, blocking collectives: 82.5 us -> none  [shards(): lax.all_gather(w_proj, ('lon', 'lat'), axis=0, tiled=True)]
    ppermute x8 -> x27, waiting for transfers between devices: 17.9 us -> 72.5 us  [the longest x12 39.2 us: shift_by(): return lax.ppermute(block, AXES, route)]
    reduce_scatter x2 -> x0, waiting for transfers between devices: 47.2 us -> none  [the longest x1 47.2 us: shards(): lax.psum_scatter(jnp.dot(section.T, normed, preferred_element_type=jnp.fl...]
    sub x8 -> x0, matrix products: 44.4 us -> none  [attention_probs(): weights = jnp.exp(scores - peak)]
    reshape x8 -> x0, local copies, waits for them, and re-layouts: 39.4 us -> none  [the longest x2 14.7 us: to_windows(): blocks.transpose(0, 2, 1, 3, 4, 5).reshape(-1, side * side * depth, width)]
    another operation x4 -> x3, local copies, waits for them, and re-layouts: 35.1 us -> 2 us  [the longest x1 1.3 us: shards(): regions[:, :, None]]
  transfers between devices with their start and end apart: 11 -> 27, of which waited for: 5 -> 15; matrix products, arithmetic and copies ran while one was open for 51% -> 6% of each run, Pallas kernels for 0% -> 14%
where the time goes in v1:
time: 213 us; the launch traced here: 212 us
  Pallas kernels  83.5 us (39%)
  waiting for transfers between devices  72.5 us (34%)
  starting transfers between devices  26.7 us (13%)
  local copies, waits for them, and re-layouts  17.9 us (8%)
  other arithmetic  10.4 us (5%)
    pallas_call x1, Pallas kernels, attention(): pl.pallas_call(attention_kernel, grid=(groups, windows), in_specs=[whole(...  52.9 us
    ppermute x12, waiting for transfers between devices, shift_by(): return lax.ppermute(block, AXES, route)  39.2 us
    ppermute x15, waiting for transfers between devices, swap(): return lax.ppermute(block, AXES, [(i, i ^ bit) for i in range(total)])  33.3 us
    ppermute x15, starting transfers between devices, swap(): return lax.ppermute(block, AXES, [(i, i ^ bit) for i in range(total)])  17.3 us
    pallas_call x1, Pallas kernels, finish(): pl.pallas_call(finish_kernel, grid=(bands,), in_specs=[banded(2, count, w...  12.9 us
    pallas_call x1, Pallas kernels, assemble(): pl.pallas_call(functools.partial(assemble_kernel, skip=skip, upper=upper)...  11.6 us
    ppermute x12, starting transfers between devices, shift_by(): return lax.ppermute(block, AXES, route)  9.45 us
  transfers between devices with their start and end apart: 27, of which 15 were waited for; matrix products, arithmetic and copies ran while one was open for 6% of the time, Pallas kernels for 14%

profile of v1, /device:TPU:0, one launch (start us, length us, event | category | flops | bytes accessed | tf_op | source)
XLA Modules:
  0.0 212.0 jit_solution(5131309689074150943)
XLA Ops:
  0.7 4.1 %collective-permute-start.11 = (bf16[1,1,1,1,1,16,512]{6,5,4,3,2,1,0:T(8,128)(2,1)}, bf16[1,1,1,1,1,16,512]{6,5,4,3,2,1,0:T(8,128)(2,1)S(1)}, u32[]{:S(2)}, u32[]{:S(2)}) collective-permute-start(bf16[1,1,1,1,1,16,512]{6,5,4,3,2,1,0:T(8,128)(2,1)} %bitcast.94), channel_id=1, source_target_pairs={{0,2},{1,3},{2,0},{3,1},{4,6},{5,7},{6,4},{7,5},{8,10},{9,11},{10,... | collective-permute-start | bytes 49160 | tf_op jit(solution)/shard_map/ppermute | solution.py:388
  4.8 1.9 collective-permute-done.11
  7.4 2.0 collective-permute-start.12
  9.4 2.7 %collective-permute-start.6 = (bf16[1,1,1,1,1,48,512]{6,5,4,3,2,1,0:T(8,128)(2,1)}, bf16[1,1,1,1,1,48,512]{6,5,4,3,2,1,0:T(8,128)(2,1)S(1)}, u32[]{:S(2)}, u32[]{:S(2)}) collective-permute-start(bf16[1,1,1,1,1,48,512]{6,5,4,3,2,1,0:T(8,128)(2,1)} %bitcast.93), channel_id=1, source_target_pairs={{0,2},{1,3},{2,0},{3,1},{4,6},{5,7},{6,4},{7,5},{8,10},{9,11},{10,... | collective-permute-start | bytes 147464 | tf_op jit(solution)/shard_map/ppermute | solution.py:388
  12.1 1.8 slice.66
  15.1 2.4 %collective-permute-start.1 = (bf16[54,8,512]{2,1,0:T(8,128)(2,1)S(1)}, bf16[54,8,512]{2,1,0:T(8,128)(2,1)}, u32[]{:S(2)}, u32[]{:S(2)}) collective-permute-start(bf16[54,8,512]{2,1,0:T(8,128)(2,1)S(1)} %slice.63), channel_id=1, source_target_pairs={{4,0},{5,1},{6,2},{7,3},{8,4},{9,5},{10,6},{11,7},{12,8},{13,9},{1... | collective-permute-start | bytes 1327112 | tf_op jit(solution)/shard_map/ppermute | solution.py:375
  20.4 6.4 %collective-permute-done.7 = bf16[1,1,1,2,1,48,512]{6,5,4,3,2,1,0:T(8,128)(2,1)S(1)} collective-permute-done((bf16[1,1,1,2,1,48,512]{6,5,4,3,2,1,0:T(8,128)(2,1)S(1)}, bf16[1,1,1,2,1,48,512]{6,5,4,3,2,1,0:T(8,128)(2,1)S(1)}, u32[]{:S(2)}, u32[]{:S(2)}) %collective-permute-start.7) | collective-permute-done | bytes 98336 | tf_op jit(solution)/shard_map/ppermute | solution.py:388
  26.9 2.7 %collective-permute-done.13 = bf16[1,1,1,2,2,16,512]{6,5,4,3,2,1,0:T(8,128)(2,1)S(1)} collective-permute-done((bf16[1,1,1,2,2,16,512]{6,5,4,3,2,1,0:T(8,128)(2,1)S(1)}, bf16[1,1,1,2,2,16,512]{6,5,4,3,2,1,0:T(8,128)(2,1)S(1)}, u32[]{:S(2)}, u32[]{:S(2)}) %collective-permute-start.13) | collective-permute-done | bytes 65568 | tf_op jit(solution)/shard_map/ppermute | solution.py:388
  29.7 2.6 %collective-permute-start.14 = (bf16[1,2,1,2,2,16,512]{6,5,4,3,2,1,0:T(8,128)(2,1)S(1)}, bf16[1,2,1,2,2,16,512]{6,5,4,3,2,1,0:T(8,128)(2,1)S(1)}, u32[]{:S(2)}, u32[]{:S(2)}) collective-permute-start(bf16[1,2,1,2,2,16,512]{6,5,4,3,2,1,0:T(8,128)(2,1)S(1)} %pad_maximum_fusion.6), channel_id=1, source_target_pairs={{0,16},{1,17},{2,18},{3,19},{4,20},{5,21},{6,22},{7,23},{8,24},{9,... | collective-permute-start | bytes 393224 | tf_op jit(solution)/shard_map/ppermute | solution.py:388
  32.3 1.6 collective-permute-done.8
  33.9 1.6 collective-permute-start.9
  36.6 1.8 slice.65
  38.4 1.8 slice.62
  40.9 3.4 %collective-permute-done.9 = bf16[1,2,1,2,2,48,512]{6,5,4,3,2,1,0:T(8,128)(2,1)S(1)} collective-permute-done((bf16[1,2,1,2,2,48,512]{6,5,4,3,2,1,0:T(8,128)(2,1)S(1)}, bf16[1,2,1,2,2,48,512]{6,5,4,3,2,1,0:T(8,128)(2,1)S(1)}, u32[]{:S(2)}, u32[]{:S(2)}) %collective-permute-start.9) | collective-permute-done | bytes 393248 | tf_op jit(solution)/shard_map/ppermute | solution.py:388
  49.3 8.3 %collective-permute-done.3 = bf16[18,24,512]{2,1,0:T(8,128)(2,1)} collective-permute-done((bf16[18,24,512]{2,1,0:T(8,128)(2,1)}, bf16[18,24,512]{2,1,0:T(8,128)(2,1)}, u32[]{:S(2)}, u32[]{:S(2)}) %collective-permute-start.3) | collective-permute-done | bytes 442400 | tf_op jit(solution)/shard_map/ppermute | solution.py:375
  57.6 8.1 %collective-permute-done = bf16[18,24,512]{2,1,0:T(8,128)(2,1)} collective-permute-done((bf16[18,24,512]{2,1,0:T(8,128)(2,1)}, bf16[18,24,512]{2,1,0:T(8,128)(2,1)}, u32[]{:S(2)}, u32[]{:S(2)}) %collective-permute-start) | collective-permute-done | bytes 442400 | tf_op jit(solution)/shard_map/ppermute | solution.py:375
  65.7 11.6 %assemble.1 = (bf16[2,2,18,24,512]{4,3,2,1,0:T(8,128)(2,1)}, f32[2,2,18,24,128]{4,3,2,1,0:T(8,128)}, bf16[2,2,18,24,512]{4,3,2,1,0:T(8,128)(2,1)}) custom-call(bf16[36,48,512]{2,1,0:T(8,128)(2,1)} %bitcast.69, bf16[9,48,512]{2,1,0:T(8,128)(2,1)} %bitcast.4.low_ref, bf16[27,16,512]{2,1,0:T(8,128)(2,1)} %bitcast.6.east_ref, ...), custom_call_target="tpu_custom_call" | custom-call | tf_op jit(solution)/shard_map/assemble/pallas_call | solution.py:117
  80.6 52.9 %attention.1 = (bf16[4,432,512]{2,1,0:T(8,128)(2,1)}, bf16[4,3,432,512]{3,2,1,0:T(8,128)(2,1)}, f32[3,512,512]{2,1,0:T(8,128)}, f32[512,512]{1,0:T(8,128)}) custom-call(bf16[4,432,512]{2,1,0:T(8,128)(2,1)} %bitcast.79, bf16[4,432,512]{2,1,0:T(8,128)(2,1)} %bitcast.88, s32[4,432,1]{2,1,0:T(8,128)} %broadcast_in_dim_reshape.8.reg_col_ref, ...), custom_call_target="tpu_custom_call" | custom-call | tf_op jit(solution)/shard_map/attention/pallas_call | solution.py:200
  133.5 2.5 %copy.17 = f32[512,512]{1,0:T(8,128)} copy(f32[512,512]{0,1:T(8,128)} %bitcast.90) | data formatting | bytes 2097152 | tf_op jit(solution)/shard_map/transpose | solution.py:467
  136.0 2.8 %fusion.1 = bf16[2,2,1,2,2,64,512]{6,5,4,3,2,1,0:T(8,128)(2,1)} fusion(s32[]{:T(128)S(6)} %select_n.253, f32[2,2,2,2,2,48,512]{6,5,4,3,2,1,0:T(8,128)} %bitcast.75, f32[2,2,2,2,2,16,512]{6,5,4,3,2,1,0:T(8,128)} %bitcast.77), kind=kLoop, calls=%fused_computation.5 | loop fusion | flops 2097152 | bytes 5242884 | tf_op jit(solution)/shard_map/convert_element_type | solution.py:417
  138.8 3.0 %collective-permute-done.22 = bf16[2,2,1,2,2,64,512]{6,5,4,3,2,1,0:T(8,128)(2,1)} collective-permute-done((bf16[2,2,1,2,2,64,512]{6,5,4,3,2,1,0:T(8,128)(2,1)}, bf16[2,2,1,2,2,64,512]{6,5,4,3,2,1,0:T(8,128)(2,1)}, u32[]{:S(2)}, u32[]{:S(2)}) %collective-permute-start.22) | collective-permute-done | bytes 1048608 | tf_op jit(solution)/shard_map/ppermute | solution.py:388
  141.8 1.7 fusion.3
  145.9 13.1 %collective-permute-done.23 = bf16[1,2,1,2,2,64,512]{6,5,4,3,2,1,0:T(8,128)(2,1)S(1)} collective-permute-done((bf16[1,2,1,2,2,64,512]{6,5,4,3,2,1,0:T(8,128)(2,1)S(1)}, bf16[1,2,1,2,2,64,512]{6,5,4,3,2,1,0:T(8,128)(2,1)S(1)}, u32[]{:S(2)}, u32[]{:S(2)}) %collective-permute-start.23) | collective-permute-done | bytes 524320 | tf_op jit(solution)/shard_map/ppermute | solution.py:388
  161.3 12.9 %finish.1 = (bf16[36,48,512]{2,1,0:T(8,128)(2,1)}, bf16[36,48,512]{2,1,0:T(8,128)(2,1)}, bf16[9,48,512]{2,1,0:T(8,128)(2,1)}, bf16[27,16,512]{2,1,0:T(8,128)(2,1...) custom-call(bf16[2,2,432,512]{3,2,1,0:T(8,128)(2,1)} %bitcast.89, ...), custom_call_target="tpu_custom_call" | custom-call | tf_op jit(solution)/shard_map/finish/pallas_call | solution.py:291
  176.0 1.7 collective-permute-start.16
  177.6 1.7 collective-permute-start.18
  180.7 2.5 %collective-permute-done.20.r_ref = bf16[54,8,512]{2,1,0:T(8,128)(2,1)S(1)} collective-permute-done((bf16[54,8,512]{2,1,0:T(8,128)(2,1)}, bf16[54,8,512]{2,1,0:T(8,128)(2,1)S(1)}, u32[]{:S(2)}, u32[]{:S(2)}) %collective-permute-start.20) | collective-permute-done | bytes 442400 | tf_op jit(solution)/shard_map/ppermute | solution.py:375
  183.2 4.7 %collective-permute-done.21.gr_ref = bf16[54,8,512]{2,1,0:T(8,128)(2,1)S(1)} collective-permute-done((bf16[54,8,512]{2,1,0:T(8,128)(2,1)}, bf16[54,8,512]{2,1,0:T(8,128)(2,1)S(1)}, u32[]{:S(2)}, u32[]{:S(2)}) %collective-permute-start.21) | collective-permute-done | bytes 442400 | tf_op jit(solution)/shard_map/ppermute | solution.py:375
  188.7 3.5 %edge.1 = (bf16[72,24,512]{2,1,0:T(8,128)(2,1)}, bf16[72,24,512]{2,1,0:T(8,128)(2,1)}) custom-call(bf16[72,24,512]{2,1,0:T(8,128)(2,1)} %bitcast.71, bf16[72,24,512]{2,1,0:T(8,128)(2,1)} %bitcast.81, bf16[54,8,512]{2,1,0:T(8,128)(2,1)} %copy-done.4, bf16[72,24,512]{2,1,0:T(8,128)(2,1)} %bitcast.64, ...), custom_call_target="tpu_custom_call", output_to_operand_aliasing={{0}: (1, {}), {1}: (4, {})} | custom-call | tf_op jit(solution)/shard_map/edge/pallas_call | solution.py:327
  192.2 11.9 %collective-permute-done.17.c_ref = bf16[18,8,512]{2,1,0:T(8,128)(2,1)S(1)} collective-permute-done((bf16[18,8,512]{2,1,0:T(8,128)(2,1)}, bf16[18,8,512]{2,1,0:T(8,128)(2,1)S(1)}, u32[]{:S(2)}, u32[]{:S(2)}) %collective-permute-start.17) | collective-permute-done | bytes 147488 | tf_op jit(solution)/shard_map/ppermute | solution.py:375
  204.1 3.2 %collective-permute-done.19.gc_ref = bf16[18,8,512]{2,1,0:T(8,128)(2,1)S(1)} collective-permute-done((bf16[18,8,512]{2,1,0:T(8,128)(2,1)S(1)}, bf16[18,8,512]{2,1,0:T(8,128)(2,1)S(1)}, u32[]{:S(2)}, u32[]{:S(2)}) %collective-permute-start.19) | collective-permute-done | bytes 147488 | tf_op jit(solution)/shard_map/ppermute | solution.py:375
  208.2 2.5 %rim.1 = (bf16[72,24,512]{2,1,0:T(8,128)(2,1)}, bf16[72,24,512]{2,1,0:T(8,128)(2,1)}) custom-call(bf16[72,24,512]{2,1,0:T(8,128)(2,1)} %bitcast.72, bf16[18,24,512]{2,1,0:T(8,128)(2,1)} %copy-done.2, bf16[18,8,512]{2,1,0:T(8,128)(2,1)} %copy-done.7, bf16[72,24,512]{2,1,0:T(8,128)(2,1)} %bitcast.65, ...), custom_call_target="tpu_custom_call", output_to_operand_aliasing={{0}: (6, {}), {1}: (7, {})} | custom-call | tf_op jit(solution)/shard_map/rim/pallas_call | solution.py:353
  (107 shorter events, 25.5 us)
Async XLA Ops:
  0.6 18.1 %copy-start.9 = (bf16[48,512]{1,0:T(8,128)(2,1)S(1)}, bf16[48,512]{1,0:T(8,128)(2,1)}, u32[]{:S(2)}) copy-start(bf16[48,512]{1,0:T(8,128)(2,1)} %param.7) | copy-start | bytes 147460
  0.6 17.9 %copy-start.10 = (s32[24]{0:T(128)S(1)}, s32[24]{0:T(128)}, u32[]{:S(2)}) copy-start(s32[24]{0:T(128)} %param.6) | copy-start | bytes 292
  0.7 6.1 %collective-permute-start.11 = (bf16[1,1,1,1,1,16,512]{6,5,4,3,2,1,0:T(8,128)(2,1)}, bf16[1,1,1,1,1,16,512]{6,5,4,3,2,1,0:T(8,128)(2,1)S(1)}, u32[]{:S(2)}, u32[]{:S(2)}) collective-permute-start(bf16[1,1,1,1,1,16,512]{6,5,4,3,2,1,0:T(8,128)(2,1)} %bitcast.94), channel_id=1, source_target_pairs={{0,2},{1,3},{2,0},{3,1},{4,6},{5,7},{6,4},{7,5},{8,10},{9,11},{10,... | collective-permute-start | bytes 49160 | tf_op jit(solution)/shard_map/ppermute | solution.py:388
  7.4 11.3 %collective-permute-start.12 = (bf16[1,1,1,2,1,16,512]{6,5,4,3,2,1,0:T(8,128)(2,1)S(1)}, bf16[1,1,1,2,1,16,512]{6,5,4,3,2,1,0:T(8,128)(2,1)S(1)}, u32[]{:S(2)}, u32[]{:S(2)}) collective-permute-start(bf16[1,1,1,2,1,16,512]{6,5,4,3,2,1,0:T(8,128)(2,1)S(1)} %pad_maximum_fusion.9), channel_id=1, source_target_pairs={{0,1},{1,0},{2,3},{3,2},{4,5},{5,4},{6,7},{7,6},{8,9},{9,8},{10,11... | collective-permute-start | bytes 98312 | tf_op jit(solution)/shard_map/ppermute | solution.py:388
  9.4 9.3 %collective-permute-start.6 = (bf16[1,1,1,1,1,48,512]{6,5,4,3,2,1,0:T(8,128)(2,1)}, bf16[1,1,1,1,1,48,512]{6,5,4,3,2,1,0:T(8,128)(2,1)S(1)}, u32[]{:S(2)}, u32[]{:S(2)}) collective-permute-start(bf16[1,1,1,1,1,48,512]{6,5,4,3,2,1,0:T(8,128)(2,1)} %bitcast.93), channel_id=1, source_target_pairs={{0,2},{1,3},{2,0},{3,1},{4,6},{5,7},{6,4},{7,5},{8,10},{9,11},{10,... | collective-permute-start | bytes 147464 | tf_op jit(solution)/shard_map/ppermute | solution.py:388
  13.9 32.9 %collective-permute-start.4 = (bf16[54,8,512]{2,1,0:T(8,128)(2,1)}, bf16[54,8,512]{2,1,0:T(8,128)(2,1)}, u32[]{:S(2)}, u32[]{:S(2)}) collective-permute-start(bf16[54,8,512]{2,1,0:T(8,128)(2,1)} %slice.66), channel_id=1, source_target_pairs={{4,0},{5,1},{6,2},{7,3},{8,4},{9,5},{10,6},{11,7},{12,8},{13,9},{1... | collective-permute-start | bytes 1327112 | tf_op jit(solution)/shard_map/ppermute | solution.py:375
  15.1 34.2 %collective-permute-start.1 = (bf16[54,8,512]{2,1,0:T(8,128)(2,1)S(1)}, bf16[54,8,512]{2,1,0:T(8,128)(2,1)}, u32[]{:S(2)}, u32[]{:S(2)}) collective-permute-start(bf16[54,8,512]{2,1,0:T(8,128)(2,1)S(1)} %slice.63), channel_id=1, source_target_pairs={{4,0},{5,1},{6,2},{7,3},{8,4},{9,5},{10,6},{11,7},{12,8},{13,9},{1... | collective-permute-start | bytes 1327112 | tf_op jit(solution)/shard_map/ppermute | solution.py:375
  18.5 27.1 %collective-permute-start.5 = (bf16[18,8,512]{2,1,0:T(8,128)(2,1)S(1)}, bf16[18,8,512]{2,1,0:T(8,128)(2,1)S(1)}, u32[]{:S(2)}, u32[]{:S(2)}) collective-permute-start(bf16[18,8,512]{2,1,0:T(8,128)(2,1)S(1)} %slice.67), channel_id=1, source_target_pairs={{5,0},{6,1},{7,2},{4,3},{9,4},{10,5},{11,6},{8,7},{13,8},{14,9},{1... | collective-permute-start | bytes 442376 | tf_op jit(solution)/shard_map/ppermute | solution.py:375
  18.8 8.0 %collective-permute-start.7 = (bf16[1,1,1,2,1,48,512]{6,5,4,3,2,1,0:T(8,128)(2,1)S(1)}, bf16[1,1,1,2,1,48,512]{6,5,4,3,2,1,0:T(8,128)(2,1)S(1)}, u32[]{:S(2)}, u32[]{:S(2)}) collective-permute-start(bf16[1,1,1,2,1,48,512]{6,5,4,3,2,1,0:T(8,128)(2,1)S(1)} %pad_maximum_fusion.7), channel_id=1, source_target_pairs={{0,1},{1,0},{2,3},{3,2},{4,5},{5,4},{6,7},{7,6},{8,9},{9,8},{10,11... | collective-permute-start | bytes 294920 | tf_op jit(solution)/shard_map/ppermute | solution.py:388
  20.3 9.3 %collective-permute-start.13 = (bf16[1,1,1,2,2,16,512]{6,5,4,3,2,1,0:T(8,128)(2,1)S(1)}, bf16[1,1,1,2,2,16,512]{6,5,4,3,2,1,0:T(8,128)(2,1)S(1)}, u32[]{:S(2)}, u32[]{:S(2)}) collective-permute-start(bf16[1,1,1,2,2,16,512]{6,5,4,3,2,1,0:T(8,128)(2,1)S(1)} %pad_maximum_fusion.8), channel_id=1, source_target_pairs={{0,8},{1,9},{2,10},{3,11},{4,12},{5,13},{6,14},{7,15},{8,0},{9,1},... | collective-permute-start | bytes 196616 | tf_op jit(solution)/shard_map/ppermute | solution.py:388
  26.8 7.0 %collective-permute-start.8 = (bf16[1,1,1,2,2,48,512]{6,5,4,3,2,1,0:T(8,128)(2,1)S(1)}, bf16[1,1,1,2,2,48,512]{6,5,4,3,2,1,0:T(8,128)(2,1)S(1)}, u32[]{:S(2)}, u32[]{:S(2)}) collective-permute-start(bf16[1,1,1,2,2,48,512]{6,5,4,3,2,1,0:T(8,128)(2,1)S(1)} %pad_maximum_fusion.5), channel_id=1, source_target_pairs={{0,8},{1,9},{2,10},{3,11},{4,12},{5,13},{6,14},{7,15},{8,0},{9,1},... | collective-permute-start | bytes 589832 | tf_op jit(solution)/shard_map/ppermute | solution.py:388
  29.7 11.1 %collective-permute-start.14 = (bf16[1,2,1,2,2,16,512]{6,5,4,3,2,1,0:T(8,128)(2,1)S(1)}, bf16[1,2,1,2,2,16,512]{6,5,4,3,2,1,0:T(8,128)(2,1)S(1)}, u32[]{:S(2)}, u32[]{:S(2)}) collective-permute-start(bf16[1,2,1,2,2,16,512]{6,5,4,3,2,1,0:T(8,128)(2,1)S(1)} %pad_maximum_fusion.6), channel_id=1, source_target_pairs={{0,16},{1,17},{2,18},{3,19},{4,20},{5,21},{6,22},{7,23},{8,24},{9,... | collective-permute-start | bytes 393224 | tf_op jit(solution)/shard_map/ppermute | solution.py:388
  33.9 10.3 %collective-permute-start.9 = (bf16[1,2,1,2,2,48,512]{6,5,4,3,2,1,0:T(8,128)(2,1)S(1)}, bf16[1,2,1,2,2,48,512]{6,5,4,3,2,1,0:T(8,128)(2,1)S(1)}, u32[]{:S(2)}, u32[]{:S(2)}) collective-permute-start(bf16[1,2,1,2,2,48,512]{6,5,4,3,2,1,0:T(8,128)(2,1)S(1)} %pad_maximum_fusion.3), channel_id=1, source_target_pairs={{0,16},{1,17},{2,18},{3,19},{4,20},{5,21},{6,22},{7,23},{8,24},{9,... | collective-permute-start | bytes 1179656 | tf_op jit(solution)/shard_map/ppermute | solution.py:388
  40.8 6.0 %collective-permute-start.2 = (bf16[18,8,512]{2,1,0:T(8,128)(2,1)S(1)}, bf16[18,8,512]{2,1,0:T(8,128)(2,1)}, u32[]{:S(2)}, u32[]{:S(2)}) collective-permute-start(bf16[18,8,512]{2,1,0:T(8,128)(2,1)S(1)} %slice.64), channel_id=1, source_target_pairs={{5,0},{6,1},{7,2},{4,3},{9,4},{10,5},{11,6},{8,7},{13,8},{14,9},{1... | collective-permute-start | bytes 442376 | tf_op jit(solution)/shard_map/ppermute | solution.py:375
  44.2 13.4 %collective-permute-start.3 = (bf16[18,24,512]{2,1,0:T(8,128)(2,1)}, bf16[18,24,512]{2,1,0:T(8,128)(2,1)}, u32[]{:S(2)}, u32[]{:S(2)}) collective-permute-start(bf16[18,24,512]{2,1,0:T(8,128)(2,1)} %bitcast.10), channel_id=1, source_target_pairs={{1,0},{2,1},{3,2},{0,3},{5,4},{6,5},{7,6},{4,7},{9,8},{10,9},{11,1... | collective-permute-start | bytes 1327112 | tf_op jit(solution)/shard_map/ppermute | solution.py:375
  45.6 20.1 %collective-permute-start = (bf16[18,24,512]{2,1,0:T(8,128)(2,1)}, bf16[18,24,512]{2,1,0:T(8,128)(2,1)}, u32[]{:S(2)}, u32[]{:S(2)}) collective-permute-start(bf16[18,24,512]{2,1,0:T(8,128)(2,1)} %bitcast.3), channel_id=1, source_target_pairs={{1,0},{2,1},{3,2},{0,3},{5,4},{6,5},{7,6},{4,7},{9,8},{10,9},{11,1... | collective-permute-start | bytes 1327112 | tf_op jit(solution)/shard_map/ppermute | solution.py:375
  46.7 32.4 %collective-permute-start.10 = (bf16[2,2,1,2,2,48,512]{6,5,4,3,2,1,0:T(8,128)(2,1)S(1)}, bf16[2,2,1,2,2,48,512]{6,5,4,3,2,1,0:T(8,128)(2,1)S(1)}, u32[]{:S(2)}, u32[]{:S(2)}) collective-permute-start(bf16[2,2,1,2,2,48,512]{6,5,4,3,2,1,0:T(8,128)(2,1)S(1)} %pad_maximum_fusion.1), channel_id=1, source_target_pairs={{0,4},{1,5},{2,6},{3,7},{4,0},{5,1},{6,2},{7,3},{8,12},{9,13},{10,... | collective-permute-start | bytes 2359304 | tf_op jit(solution)/shard_map/ppermute | solution.py:388
  46.8 30.5 %collective-permute-start.15 = (bf16[2,2,1,2,2,16,512]{6,5,4,3,2,1,0:T(8,128)(2,1)S(1)}, bf16[2,2,1,2,2,16,512]{6,5,4,3,2,1,0:T(8,128)(2,1)}, u32[]{:S(2)}, u32[]{:S(2)}) collective-permute-start(bf16[2,2,1,2,2,16,512]{6,5,4,3,2,1,0:T(8,128)(2,1)S(1)} %pad_maximum_fusion.4), channel_id=1, source_target_pairs={{0,4},{1,5},{2,6},{3,7},{4,0},{5,1},{6,2},{7,3},{8,12},{9,13},{10,... | collective-permute-start | bytes 786440 | tf_op jit(solution)/shard_map/ppermute | solution.py:388
  136.0 5.8 %copy-start = (f32[3,512,512]{2,1,0:T(8,128)S(1)}, f32[3,512,512]{2,1,0:T(8,128)}, u32[]{:S(2)}) copy-start(f32[3,512,512]{2,1,0:T(8,128)} %get-tuple-element.40) | copy-start | bytes 9437188
  138.8 3.0 %collective-permute-start.22 = (bf16[2,2,1,2,2,64,512]{6,5,4,3,2,1,0:T(8,128)(2,1)}, bf16[2,2,1,2,2,64,512]{6,5,4,3,2,1,0:T(8,128)(2,1)}, u32[]{:S(2)}, u32[]{:S(2)}) collective-permute-start(bf16[2,2,1,2,2,64,512]{6,5,4,3,2,1,0:T(8,128)(2,1)} %fusion.1), channel_id=1, source_target_pairs={{0,4},{1,5},{2,6},{3,7},{4,0},{5,1},{6,2},{7,3},{8,12},{9,13},{10,... | collective-permute-start | bytes 3145736 | tf_op jit(solution)/shard_map/ppermute | solution.py:388
  145.0 14.0 %collective-permute-start.23 = (bf16[1,2,1,2,2,64,512]{6,5,4,3,2,1,0:T(8,128)(2,1)S(1)}, bf16[1,2,1,2,2,64,512]{6,5,4,3,2,1,0:T(8,128)(2,1)S(1)}, u32[]{:S(2)}, u32[]{:S(2)}) collective-permute-start(bf16[1,2,1,2,2,64,512]{6,5,4,3,2,1,0:T(8,128)(2,1)S(1)} %dynamic-slice_convert_fusion), channel_id=1, source_target_pairs={{0,16},{1,17},{2,18},{3,19},{4,20},{5,21},{6,22},{7,23},{8,24},{9,... | collective-permute-start | bytes 1572872 | tf_op jit(solution)/shard_map/ppermute | solution.py:388
  160.5 13.9 %collective-permute-start.24 = (bf16[1,1,1,2,2,64,512]{6,5,4,3,2,1,0:T(8,128)(2,1)S(1)}, bf16[1,1,1,2,2,64,512]{6,5,4,3,2,1,0:T(8,128)(2,1)S(1)}, u32[]{:S(2)}, u32[]{:S(2)}) collective-permute-start(bf16[1,1,1,2,2,64,512]{6,5,4,3,2,1,0:T(8,128)(2,1)S(1)} %dynamic-slice_convert_fusion.1), channel_id=1, source_target_pairs={{0,8},{1,9},{2,10},{3,11},{4,12},{5,13},{6,14},{7,15},{8,0},{9,1},... | collective-permute-start | bytes 786440 | tf_op jit(solution)/shard_map/ppermute | solution.py:388
  174.3 8.9 %copy-start.11 = (bf16[9,16,512]{2,1,0:T(8,128)(2,1)S(1)}, bf16[9,16,512]{2,1,0:T(8,128)(2,1)}, u32[]{:S(2)}) copy-start(bf16[9,16,512]{2,1,0:T(8,128)(2,1)} %get-tuple-element.31) | copy-start | bytes 442372
  174.3 8.9 %collective-permute-start.20 = (bf16[54,8,512]{2,1,0:T(8,128)(2,1)}, bf16[54,8,512]{2,1,0:T(8,128)(2,1)S(1)}, u32[]{:S(2)}, u32[]{:S(2)}) collective-permute-start(bf16[54,8,512]{2,1,0:T(8,128)(2,1)} %bitcast.98), channel_id=1, source_target_pairs={{28,0},{29,1},{30,2},{31,3},{0,4},{1,5},{2,6},{3,7},{4,8},{5,9},{6... | collective-permute-start | bytes 1327112 | tf_op jit(solution)/shard_map/ppermute | solution.py:375
  174.5 6.1 %collective-permute-start.25 = (bf16[1,1,1,2,1,64,512]{6,5,4,3,2,1,0:T(8,128)(2,1)S(1)}, bf16[1,1,1,2,1,64,512]{6,5,4,3,2,1,0:T(8,128)(2,1)S(1)}, u32[]{:S(2)}, u32[]{:S(2)}) collective-permute-start(bf16[1,1,1,2,1,64,512]{6,5,4,3,2,1,0:T(8,128)(2,1)S(1)} %dynamic-slice_convert_fusion.2), channel_id=1, source_target_pairs={{0,1},{1,0},{2,3},{3,2},{4,5},{5,4},{6,7},{7,6},{8,9},{9,8},{10,11... | collective-permute-start | bytes 393224 | tf_op jit(solution)/shard_map/ppermute | solution.py:388
  174.6 13.4 %collective-permute-start.21 = (bf16[54,8,512]{2,1,0:T(8,128)(2,1)}, bf16[54,8,512]{2,1,0:T(8,128)(2,1)S(1)}, u32[]{:S(2)}, u32[]{:S(2)}) collective-permute-start(bf16[54,8,512]{2,1,0:T(8,128)(2,1)} %bitcast.97), channel_id=1, source_target_pairs={{28,0},{29,1},{30,2},{31,3},{0,4},{1,5},{2,6},{3,7},{4,8},{5,9},{6... | collective-permute-start | bytes 1327112 | tf_op jit(solution)/shard_map/ppermute | solution.py:375
  176.0 31.3 %collective-permute-start.16 = (bf16[18,24,512]{2,1,0:T(8,128)(2,1)}, bf16[18,24,512]{2,1,0:T(8,128)(2,1)S(1)}, u32[]{:S(2)}, u32[]{:S(2)}) collective-permute-start(bf16[18,24,512]{2,1,0:T(8,128)(2,1)} %bitcast.96), channel_id=1, source_target_pairs={{3,0},{0,1},{1,2},{2,3},{7,4},{4,5},{5,6},{6,7},{11,8},{8,9},{9,10... | collective-permute-start | bytes 1327112 | tf_op jit(solution)/shard_map/ppermute | solution.py:375
  177.6 29.6 %collective-permute-start.18 = (bf16[18,24,512]{2,1,0:T(8,128)(2,1)}, bf16[18,24,512]{2,1,0:T(8,128)(2,1)S(1)}, u32[]{:S(2)}, u32[]{:S(2)}) collective-permute-start(bf16[18,24,512]{2,1,0:T(8,128)(2,1)} %bitcast.95), channel_id=1, source_target_pairs={{3,0},{0,1},{1,2},{2,3},{7,4},{4,5},{5,6},{6,7},{11,8},{8,9},{9,10... | collective-permute-start | bytes 1327112 | tf_op jit(solution)/shard_map/ppermute | solution.py:375
  180.5 23.5 %collective-permute-start.17 = (bf16[18,8,512]{2,1,0:T(8,128)(2,1)}, bf16[18,8,512]{2,1,0:T(8,128)(2,1)S(1)}, u32[]{:S(2)}, u32[]{:S(2)}) collective-permute-start(bf16[18,8,512]{2,1,0:T(8,128)(2,1)} %bitcast.100), channel_id=1, source_target_pairs={{31,0},{28,1},{29,2},{30,3},{3,4},{0,5},{1,6},{2,7},{7,8},{4,9},{5... | collective-permute-start | bytes 442376 | tf_op jit(solution)/shard_map/ppermute | solution.py:375
  183.2 5.0 %copy-start.4 = (bf16[54,8,512]{2,1,0:T(8,128)(2,1)}, bf16[54,8,512]{2,1,0:T(8,128)(2,1)S(1)}, u32[]{:S(2)}) copy-start(bf16[54,8,512]{2,1,0:T(8,128)(2,1)S(1)} %collective-permute-done.20.r_ref) | copy-start | bytes 1327108
  183.2 24.0 %collective-permute-start.19 = (bf16[18,8,512]{2,1,0:T(8,128)(2,1)S(1)}, bf16[18,8,512]{2,1,0:T(8,128)(2,1)S(1)}, u32[]{:S(2)}, u32[]{:S(2)}) collective-permute-start(bf16[18,8,512]{2,1,0:T(8,128)(2,1)S(1)} %bitcast.99), channel_id=1, source_target_pairs={{31,0},{28,1},{29,2},{30,3},{3,4},{0,5},{1,6},{2,7},{7,8},{4,9},{5... | collective-permute-start | bytes 442376 | tf_op jit(solution)/shard_map/ppermute | solution.py:375
  187.9 22.8 %collective-permute-start.26 = (bf16[1,1,1,1,1,64,512]{6,5,4,3,2,1,0:T(8,128)(2,1)S(1)}, bf16[1,1,1,1,1,64,512]{6,5,4,3,2,1,0:T(8,128)(2,1)S(1)}, u32[]{:S(2)}, u32[]{:S(2)}) collective-permute-start(bf16[1,1,1,1,1,64,512]{6,5,4,3,2,1,0:T(8,128)(2,1)S(1)} %dynamic-slice_convert_fusion.3), channel_id=1, source_target_pairs={{0,2},{1,3},{2,0},{3,1},{4,6},{5,7},{6,4},{7,5},{8,10},{9,11},{10,... | collective-permute-start | bytes 196616 | tf_op jit(solution)/shard_map/ppermute | solution.py:388
  (7 other events, 8.4 us)

commit v2 on v1

v2 whole, which is shorter than its diff:
```python
import functools

import jax
import jax.numpy as jnp
from jax import lax
from jax.experimental import pallas as pl
from jax.experimental.pallas import tpu as pltpu
from jax.sharding import PartitionSpec as P


HEAD = 64
WIN = 12
HALF = WIN // 2
EPSILON = 1e-05
AXES = ("lon", "lat")
LANES = 128
SUB = 8


F32 = jnp.float32
BF16 = jnp.bfloat16


def nt(a, b):
    return lax.dot_general(a, b, (((1,), (1,)), ((), ())), preferred_element_type=F32)


def nn(a, b):
    return lax.dot_general(a, b, (((1,), (0,)), ((), ())), preferred_element_type=F32)


def sub_index(width):
    return lax.broadcasted_iota(jnp.int32, (SUB, width), 0)


def pick_first(own):
    s = sub_index(own.shape[1])
    t0a, t1a, t2a, t0b, t1b, t2b = [own[8 * i : 8 * i + 8] for i in range(6)]
    mixed = jnp.where(
        s < 2,
        t2a,
        jnp.where(s < 4, pltpu.roll(t2b, 2, 0), jnp.where(s < 6, pltpu.roll(t0b, 6, 0), t0a)),
    )
    return jnp.concatenate([t1a, t1b, mixed], axis=0)


def pick_second(own, strip):
    s = sub_index(own.shape[1])
    t2a, t2b = own[16:24], own[40:48]
    ha, hb = strip[:8], strip[8:]
    n1 = jnp.where(s < 2, ha, t2a)
    n2 = jnp.where(s < 2, hb, t2b)
    n3 = jnp.where((s >= 2) & (s < 6), ha, pltpu.roll(hb, 4, 0))
    return jnp.concatenate([n1, n2, n3], axis=0)


def unpick(first, second):
    s = sub_index(first.shape[1])
    t1a, t1b, mixed = first[:8], first[8:16], first[16:]
    n1, n2, n3 = second[:8], second[8:16], second[16:]
    zero = jnp.zeros_like(mixed)
    t0a = jnp.where(s >= 6, mixed, zero)
    t0b = jnp.where(s >= 6, pltpu.roll(mixed, 2, 0), zero)
    t2a = jnp.where(s < 2, mixed, n1)
    t2b = jnp.where(s < 2, pltpu.roll(mixed, 6, 0), n2)
    ha = jnp.where(s < 2, n1, n3)
    hb = jnp.where(s < 2, n2, pltpu.roll(n3, 4, 0))
    own = jnp.concatenate([t0a, t1a, t2a, t0b, t1b, t2b], axis=0)
    return own, jnp.concatenate([ha, hb], axis=0)


def token_regions(region_ids, levels):
    lines = jnp.repeat(region_ids, levels)
    pairs = lines.reshape(-1, 2)
    s = jnp.arange(3 * SUB)
    inner = s % SUB
    line0 = jnp.where(s < 8, 0, jnp.where(s < 16, 1, jnp.where((inner < 2) | (inner >= 6), 0, 1)))
    line1 = jnp.where(s < 8, 0, jnp.where(s < 16, 1, jnp.where((inner >= 2) & (inner < 6), 0, 1)))
    a, b = pairs[:, :1], pairs[:, 1:]
    both = jnp.stack([jnp.where(line0 == 0, a, b), jnp.where(line1 == 0, a, b)])
    per_band = WIN * levels // 2
    bands = pairs.shape[0] // per_band
    return both.reshape(2, bands, per_band * 3 * SUB).transpose(1, 0, 2)


def norm(block):
    centre = block - jnp.mean(block, axis=-1, keepdims=True)
    inverse = lax.rsqrt(jnp.mean(centre * centre, axis=-1, keepdims=True) + EPSILON)
    return (centre * inverse).astype(BF16), inverse


def put(at, p, block, grads, normed_ref, inv_ref, gs_ref):
    normed, inverse = norm(block)
    normed_ref[at, p] = normed
    inv_ref[at, p] = jnp.broadcast_to(inverse, (3 * SUB, LANES))
    gs_ref[at, p] = grads.astype(BF16)


def assemble_own_kernel(f_ref, g_ref, *outs):
    @pl.loop(0, f_ref.shape[0], unroll=3)
    def _(p):
        put(0, p, pick_first(f_ref[p].astype(F32)), pick_first(g_ref[p].astype(F32)), *outs)


def assemble_east_kernel(f_ref, g_ref, east_ref, *outs):
    @pl.loop(0, f_ref.shape[0], unroll=3)
    def _(p):
        put(
            0,
            p,
            pick_second(f_ref[p].astype(F32), east_ref[0, p].astype(F32)),
            pick_second(g_ref[p].astype(F32), east_ref[1, p].astype(F32)),
            *outs,
        )


def assemble_low_kernel(f_ref, g_ref, east_ref, low_ref, corner_ref, *outs):
    def both(p, f, g, fs, gs):
        f, g = f.astype(F32), g.astype(F32)
        put(0, p, pick_first(f), pick_first(g), *outs)
        put(1, p, pick_second(f, fs.astype(F32)), pick_second(g, gs.astype(F32)), *outs)

    @pl.when(pl.program_id(0) == 0)
    def _():
        @pl.loop(0, f_ref.shape[0], unroll=3)
        def _(p):
            both(p, f_ref[p], g_ref[p], east_ref[0, p], east_ref[1, p])

    @pl.when(pl.program_id(0) == 1)
    def _():
        @pl.loop(0, f_ref.shape[0], unroll=3)
        def _(p):
            both(p, low_ref[0, p], low_ref[1, p], corner_ref[0, p], corner_ref[1, p])


def assembled(kernel, windows, skip, width, specs, args):
    shape = (windows, 2 * skip, 3 * SUB)
    out = lambda w: pl.BlockSpec((windows, skip, 3 * SUB, w), lambda s: (0, s, 0, 0))
    outs = pl.pallas_call(
        kernel,
        grid=(2,),
        in_specs=specs,
        out_specs=[out(width), out(LANES), out(width)],
        out_shape=(
            jax.ShapeDtypeStruct(shape + (width,), BF16),
            jax.ShapeDtypeStruct(shape + (LANES,), F32),
            jax.ShapeDtypeStruct(shape + (width,), BF16),
        ),
        cost_estimate=pl.CostEstimate(
            flops=windows * skip * 3 * SUB * width * 100, transcendentals=0,
            bytes_accessed=windows * skip * 3 * SUB * width * 16),
    )(*args)
    count = 2 * skip * 3 * SUB
    return [x.reshape(windows, count, x.shape[-1]) for x in outs]


def assemble_own(fields, grads, skip):
    width = fields.shape[2]
    own = pl.BlockSpec((skip, 48, width), lambda s: (s + 1, 0, 0))
    return assembled(assemble_own_kernel, 1, skip, width, [own, own], (fields, grads))


def assemble_east(fields, grads, east, skip):
    width = fields.shape[2]
    own = pl.BlockSpec((skip, 48, width), lambda s: (s + 1, 0, 0))
    strip = pl.BlockSpec((2, skip, 16, width), lambda s: (0, s, 0, 0))
    return assembled(assemble_east_kernel, 1, skip, width, [own, own, strip], (fields, grads, east))


def assemble_low(fields, grads, east, low, corner, skip):
    width = fields.shape[2]
    last = fields.shape[0] // skip - 1
    own = pl.BlockSpec((skip, 48, width), lambda s: (last, 0, 0))
    strip = pl.BlockSpec((2, skip, 16, width), lambda s: (0, last - 1, 0, 0))
    below = pl.BlockSpec((2, skip, 48, width), lambda s: (0, 0, 0, 0))
    diagonal = pl.BlockSpec((2, skip, 16, width), lambda s: (0, 0, 0, 0))
    return assembled(
        assemble_low_kernel, 2, skip, width, [own, own, strip, below, diagonal],
        (fields, grads, east, low, corner),
    )


def attention_kernel(*refs, carried, last):
    normed_ref, gs_ref, reg_col_ref, reg_row_ref, w_ref, wp_ref = refs[:6]
    refs = refs[6:]
    if carried:
        gw_in, gp_in = refs[:2]
        refs = refs[2:]
    att_ref, gqkv_ref, gw_ref, gp_ref = refs[:4]
    gw_acc, gp_acc = refs[4:] if last else (gw_ref, gp_ref)
    window = pl.program_id(1)
    scale = HEAD ** (-0.5)
    normed = normed_ref[window]
    grads = gs_ref[window]
    count = normed.shape[0]
    weights = w_ref[...].reshape(3 * LANES, w_ref.shape[2])
    qkv = nt(normed, weights).astype(BF16)
    query, keys, values = [qkv[:, LANES * i : LANES * (i + 1)] for i in range(3)]
    query = query * jnp.asarray(scale, BF16)
    grad_att = nn(grads, wp_ref[...]).astype(BF16)
    keys_t = keys.astype(F32).T.astype(BF16) * jnp.asarray(scale, BF16)
    values_t = values.astype(F32).T.astype(BF16)
    allowed = reg_col_ref[window] == reg_row_ref[window]
    lane = lax.broadcasted_iota(jnp.int32, (count, LANES), 1)
    att_t, grad_q_t = [], []
    grad_k = grad_v = None
    for h in range(LANES // HEAD):
        mine = (lane >= h * HEAD) & (lane < (h + 1) * HEAD)
        zero = jnp.zeros((), BF16)
        rows = slice(h * HEAD, (h + 1) * HEAD)
        scores = nt(jnp.where(mine, keys, zero), query)
        scores = jnp.where(allowed, scores, -1e30)
        peak = jnp.max(scores, axis=0, keepdims=True)
        expo = jnp.exp(scores - peak)
        probs = expo * (1.0 / jnp.sum(expo, axis=0, keepdims=True))
        rounded = probs.astype(BF16)
        grad_probs = nt(jnp.where(mine, values, zero), grad_att)
        inner = jnp.sum(grad_probs * probs, axis=0, keepdims=True)
        grad_scores = (probs * (grad_probs - inner)).astype(BF16)
        att_t.append(nn(values_t[rows], rounded))
        grad_q_t.append(nn(keys_t[rows], grad_scores))
        part_v = nn(rounded, jnp.where(mine, grad_att, zero))
        part_k = nn(grad_scores, jnp.where(mine, query, zero))
        grad_v = part_v if grad_v is None else grad_v + part_v
        grad_k = part_k if grad_k is None else grad_k + part_k
    att_t = jnp.concatenate(att_t, axis=0)
    grad_q_t = jnp.concatenate(grad_q_t, axis=0)
    att_ref[0] = att_t.T.astype(BF16)
    gqkv_ref[0, 0] = grad_q_t.T.astype(BF16)
    gqkv_ref[0, 1] = grad_k.astype(BF16)
    gqkv_ref[0, 2] = grad_v.astype(BF16)
    grad_w = (
        nn(grad_q_t.astype(BF16), normed),
        nn(grad_k.T.astype(BF16), normed),
        nn(grad_v.T.astype(BF16), normed),
    )
    grad_p = nn(att_t.astype(BF16), grads)

    @pl.when(window == 0)
    def _():
        for i in range(3):
            gw_acc[i] = grad_w[i] + gw_in[i] if carried else grad_w[i]
        gp_acc[...] = grad_p + gp_in[...] if carried else grad_p

    @pl.when(window > 0)
    def _():
        for i in range(3):
            gw_acc[i] += grad_w[i]
        gp_acc[...] += grad_p

    if last:

        @pl.when(window == pl.num_programs(1) - 1)
        def _():
            gw_ref[...] = gw_acc[...].astype(BF16)
            gp_ref[...] = gp_acc[...].T.astype(BF16)


def attention(normed, gs, regions, w_qkv, w_proj, carry=(), last=False):
    windows, count, width = normed.shape
    groups = width // LANES
    whole = lambda *shape: pl.BlockSpec(shape, lambda p, w: (0,) * len(shape))
    rows3 = pl.BlockSpec((3, LANES, width), lambda p, w: (0, p, 0))
    rows1 = pl.BlockSpec((LANES, width), lambda p, w: (p, 0))
    cols1 = pl.BlockSpec((width, LANES), lambda p, w: (0, p))
    kind = BF16 if last else F32
    scratch = [pltpu.VMEM((3, LANES, width), F32), pltpu.VMEM((LANES, width), F32)]
    return pl.pallas_call(
        functools.partial(attention_kernel, carried=bool(carry), last=last),
        grid=(groups, windows),
        in_specs=[
            whole(windows, count, width),
            whole(windows, count, width),
            whole(windows, count, 1),
            whole(windows, 1, count),
            rows3,
            cols1,
        ]
        + ([rows3, rows1] if carry else []),
        out_specs=[
            pl.BlockSpec((1, count, LANES), lambda p, w: (w, 0, p)),
            pl.BlockSpec((1, 3, count, LANES), lambda p, w: (w, 0, 0, p)),
            rows3,
            cols1 if last else rows1,
        ],
        out_shape=(
            jax.ShapeDtypeStruct((windows, count, width), BF16),
            jax.ShapeDtypeStruct((windows, 3, count, width), BF16),
            jax.ShapeDtypeStruct((3, width, width), kind),
            jax.ShapeDtypeStruct((width, width), kind),
        ),
        scratch_shapes=scratch if last else [],
        cost_estimate=pl.CostEstimate(
            flops=windows * count * width * (16 * width + 12 * count), transcendentals=0,
            bytes_accessed=windows * count * width * 12),
    )(normed, gs, regions[:, :, None], regions[:, None, :], w_qkv, w_proj, *carry)


def finish_kernel(*refs, low):
    ins = refs[:8]
    w_ref, wp_ref, fields_ref, grads_ref = refs[8:12]
    branch_scr, pre_scr = refs[-2:]
    outs = refs[12:-2] if low else refs[14:-2]
    out_ref, gout_ref, east_ref = outs[:3]
    n = fields_ref.shape[0]
    width = wp_ref.shape[0]
    for j in range(2):
        att, gqkv, normed, inv = ins[4 * j : 4 * j + 4]
        branch = nt(att[0], wp_ref[...])
        branch_scr[j] = branch.astype(BF16).astype(F32).reshape(n, 3 * SUB, width)
        grad_normed = nn(gqkv[0, 0], w_ref[0]) + nn(gqkv[0, 1], w_ref[1]) + nn(gqkv[0, 2], w_ref[2])
        normal = normed[0].astype(F32)
        mean = jnp.mean(grad_normed, axis=-1, keepdims=True)
        along = jnp.mean(grad_normed * normal, axis=-1, keepdims=True)
        pre = inv[0][:, :1] * (grad_normed - mean - normal * along)
        pre_scr[j] = pre.astype(BF16).astype(F32).reshape(n, 3 * SUB, width)

    def own():
        @pl.loop(0, n, unroll=3)
        def _(p):
            add, strip = unpick(branch_scr[0, p], branch_scr[1, p])
            out_ref[p] = (fields_ref[p].astype(F32) + add).astype(BF16)
            east_ref[0, p] = strip.astype(BF16)
            add, strip = unpick(pre_scr[0, p], pre_scr[1, p])
            gout_ref[p] = (grads_ref[p].astype(F32) + add).astype(BF16)
            east_ref[1, p] = strip.astype(BF16)

    if not low:
        own()
        return
    low_ref, corner_ref = outs[3:]
    pl.when(pl.program_id(0) == 0)(own)

    @pl.when(pl.program_id(0) == 1)
    def _():
        @pl.loop(0, n, unroll=3)
        def _(p):
            for i, scr in enumerate((branch_scr, pre_scr)):
                add, strip = unpick(scr[0, p], scr[1, p])
                low_ref[i, p] = add.astype(BF16)
                corner_ref[i, p] = strip.astype(BF16)


def finish(sets, places, w_qkv, w_proj, fields, grads, skip, low, into=()):
    pairs, _, width = fields.shape
    last = pairs // skip - 1
    part = skip * 3 * SUB
    own = pl.BlockSpec((skip, 48, width), (lambda s: (last, 0, 0)) if low else (lambda s: (s + 1, 0, 0)))
    whole = lambda *shape: pl.BlockSpec(shape, lambda s: (0,) * len(shape))
    specs, args = [], []
    for (att, gqkv, normed, inv), at in zip(sets, places):
        specs += [
            pl.BlockSpec((1, part, width), lambda s, at=at: (at, s, 0)),
            pl.BlockSpec((1, 3, part, width), lambda s, at=at: (at, 0, s, 0)),
            pl.BlockSpec((1, part, width), lambda s, at=at: (at, s, 0)),
            pl.BlockSpec((1, part, LANES), lambda s, at=at: (at, s, 0)),
        ]
        args += [att, gqkv, normed, inv]
    specs += [whole(3, width, width), whole(width, width), own, own]
    args += [w_qkv, w_proj, fields, grads]
    alias = {}
    if not low:
        alias = {len(args): 0, len(args) + 1: 1}
        specs += [pl.BlockSpec(memory_space=pl.ANY)] * 2
        args += list(into)
    shapes = [(pairs, 48, width)] * 2 + [(2, skip if low else 2 * skip, 16, width)]
    outs = [own, own]
    if low:
        shapes += [(2, skip, 48, width), (2, skip, 16, width)]
        outs += [whole(*shape) for shape in shapes[2:]]
    else:
        outs += [pl.BlockSpec((2, skip, 16, width), lambda s: (0, s, 0, 0))]
    return pl.pallas_call(
        functools.partial(finish_kernel, low=low),
        grid=(2,),
        in_specs=specs,
        out_specs=outs,
        out_shape=tuple(jax.ShapeDtypeStruct(shape, BF16) for shape in shapes),
        scratch_shapes=[pltpu.VMEM((2, skip, 3 * SUB, width), F32)] * 2,
        input_output_aliases=alias,
        cost_estimate=pl.CostEstimate(
            flops=4 * part * 8 * width * width, transcendentals=0, bytes_accessed=8 * part * width * 16),
        name="finish_low" if low else "finish_top",
    )(*args)


def edge_kernel(f_ref, o_ref, r_ref, g_ref, q_ref, out_ref, gout_ref):
    s = lax.broadcasted_iota(jnp.int32, f_ref.shape, 1)
    for i, (f, o, out) in enumerate(((f_ref, o_ref, out_ref), (g_ref, q_ref, gout_ref))):
        total = f[...].astype(F32) + r_ref[i].astype(F32)
        out[...] = jnp.where(s < HALF, total, o[...].astype(F32)).astype(BF16)


def edge(fields, out, back, grads, gout, skip, first):
    _, _, width = fields.shape
    n = back.shape[1] // skip
    at = pl.BlockSpec((skip, SUB, width), lambda i: (i + first, 0, 0))
    strip = pl.BlockSpec((2, skip, SUB, width), lambda i: (0, i, 0, 0))
    return pl.pallas_call(
        edge_kernel,
        grid=(n,),
        in_specs=[at, at, strip, at, at],
        out_specs=[at, at],
        out_shape=(jax.ShapeDtypeStruct(out.shape, BF16),) * 2,
        input_output_aliases={1: 0, 4: 1},
        name="edge",
    )(fields, out, back, grads, gout)


def rim_kernel(f_ref, low_ref, c_ref, g_ref, out_any, gout_any, out_ref, gout_ref):
    for i, (f, out) in enumerate(((f_ref, out_ref), (g_ref, gout_ref))):
        back = low_ref[i].astype(F32)
        corner = c_ref[i].astype(F32)
        s = lax.broadcasted_iota(jnp.int32, corner.shape, 1)
        head = jnp.where(s < HALF, corner, back[:, :SUB])
        back = jnp.concatenate([head, back[:, SUB:]], axis=1)
        out[...] = (f[...].astype(F32) + back).astype(BF16)


def rim(fields, low, corner, grads, out, gout):
    _, skip, cols, width = low.shape
    at = pl.BlockSpec((skip, cols, width), lambda i: (0, 0, 0))
    whole = lambda *shape: pl.BlockSpec(shape, lambda i: (0,) * len(shape))
    anyw = pl.BlockSpec(memory_space=pl.ANY)
    return pl.pallas_call(
        rim_kernel,
        grid=(1,),
        in_specs=[at, whole(2, skip, cols, width), whole(2, skip, SUB, width), at, anyw, anyw],
        out_specs=[at, at],
        out_shape=(jax.ShapeDtypeStruct(out.shape, BF16),) * 2,
        input_output_aliases={4: 0, 5: 1},
        name="rim",
    )(fields, low, corner, grads, out, gout)


def linear(lon, lat, lats):
    return lon * lats + lat


def shift_by(block, step_lon, step_lat):
    lons, lats = lax.axis_size("lon"), lax.axis_size("lat")
    route = [
        (linear((i + step_lon) % lons, (j + step_lat) % lats, lats), linear(i, j, lats))
        for i in range(lons)
        for j in range(lats)
    ]
    return lax.ppermute(block, AXES, route)


def stages():
    lons, lats = lax.axis_size("lon"), lax.axis_size("lat")
    lat_bits = [1 << i for i in range(lats.bit_length() - 1)]
    lon_bits = [lats << i for i in range(lons.bit_length() - 1)]
    assert lats == 1 << len(lat_bits) and lons == 1 << len(lon_bits)
    far = lon_bits[1:]
    groups = [lat_bits[i : i + 2] for i in range(0, len(lat_bits), 2)]
    groups += [far[i : i + 2] for i in range(0, len(far), 2)]
    groups += [lon_bits[:1]]
    return groups, sorted(lat_bits + lon_bits)[::-1]


def swap(block, bit):
    total = lax.axis_size("lon") * lax.axis_size("lat")
    return lax.ppermute(block, AXES, [(i, i ^ bit) for i in range(total)])


def join(mine, other, bit, bits, place):
    high = (place & bit) != 0
    return jnp.concatenate(
        [jnp.where(high, other, mine), jnp.where(high, mine, other)], axis=bits.index(bit)
    )


def gather_stage(held, group, bits, place):
    if len(group) == 1:
        return join(held, swap(held, group[0]), group[0], bits, place)
    b1, b2 = group
    o1, o2, o3 = swap(held, b1), swap(held, b2), swap(held, b1 | b2)
    return join(join(held, o1, b1, bits, place), join(o2, o3, b1, bits, place), b2, bits, place)


def part_of(held, bit, bits, index):
    return lax.dynamic_index_in_dim(held, index, bits.index(bit), keepdims=True)


def scatter_stage(held, group, bits, place):
    here = [jnp.where((place & bit) != 0, 1, 0) for bit in group]
    total = held
    for bit, i in zip(group, here):
        total = part_of(total, bit, bits, i)
    total = total.astype(F32)
    for flips in range(1, 1 << len(group)):
        send, mask = held, 0
        for k, (bit, i) in enumerate(zip(group, here)):
            flip = (flips >> k) & 1
            send = part_of(send, bit, bits, 1 - i if flip else i)
            mask |= bit * flip
        total = total + swap(send.astype(BF16), mask).astype(F32)
    return total


def lines_of(grid):
    rows, cols, levels, width = grid.shape
    return grid.transpose(0, 2, 1, 3).reshape(rows * levels, cols, width)


def grid_of(lines, levels):
    count, cols, width = lines.shape
    return lines.reshape(count // levels, levels, cols, width).transpose(0, 2, 1, 3)


def paired(lines):
    *lead, count, cols, width = lines.shape
    return lines.reshape(*lead, count // 2, 2 * cols, width)


def unpaired(pairs):
    *lead, count, cols, width = pairs.shape
    return pairs.reshape(*lead, count * 2, cols // 2, width)


def block(fields, region_ids, w_qkv, w_proj, grad_output):
    rows, cols, levels, width = fields.shape
    skip = HALF * levels // 2
    devices = lax.axis_size("lon") * lax.axis_size("lat")
    factor = float(rows * cols * levels * devices) ** (-0.5)
    place = lax.axis_index(AXES)
    groups, bits = stages()
    share = w_qkv.shape[0]
    f_lines, g_lines = lines_of(fields), lines_of(grad_output)
    f_pairs, g_pairs = paired(f_lines), paired(g_lines)
    held = jnp.concatenate([w_qkv, w_proj], axis=0)
    held = held.reshape((1,) * len(bits) + held.shape)
    for group in groups:
        held = gather_stage(held, group, bits, place)
    held = held.reshape(devices, -1, width)
    w3 = held[:, :share].reshape(3, width, width)
    p_all = held[:, share:].reshape(width, width)
    both = jnp.stack
    low = shift_by(both([f_lines[: 2 * skip], g_lines[: 2 * skip]]), 0, 1)
    east = shift_by(both([f_lines[2 * skip :, :SUB], g_lines[2 * skip :, :SUB]]), 1, 0)
    corner = shift_by(both([f_lines[: 2 * skip, :SUB], g_lines[: 2 * skip, :SUB]]), 1, 1)
    low, east, corner = paired(low), paired(east), paired(corner)
    regions = token_regions(region_ids, levels)
    n00, i00, g00 = assemble_own(f_pairs, g_pairs, skip)
    a00, q00, *carry = attention(n00, g00, regions[0, :1], w3, p_all)
    n1, i1, g1 = assemble_low(f_pairs, g_pairs, east, low, corner, skip)
    a1, q1, *carry = attention(n1, g1, regions[1], w3, p_all, carry)
    n01, i01, g01 = assemble_east(f_pairs, g_pairs, east, skip)
    set1 = (a1, q1, n1, i1)
    out, gout, r_east1, r_low, r_corner = finish(
        (set1, set1), (0, 1), w3, p_all, f_pairs, g_pairs, skip, True
    )
    r_low = shift_by(unpaired(r_low), 0, -1)
    r_corner = shift_by(unpaired(r_corner), -1, -1)
    r_east1 = shift_by(unpaired(r_east1), -1, 0)
    a01, q01, grad_w, grad_p = attention(n01, g01, regions[0, 1:], w3, p_all, carry, True)
    grads = jnp.concatenate(
        [grad_w.reshape(devices, -1, width), grad_p.reshape(devices, -1, width)], axis=1
    )
    grads = grads.reshape((2,) * len(bits) + grads.shape[1:])
    for group in groups[::-1]:
        grads = scatter_stage(grads, group, bits, place)
    grads = grads.reshape(-1, width) * factor
    out, gout, r_east0 = finish(
        ((a00, q00, n00, i00), (a01, q01, n01, i01)), (0, 0), w3, p_all, f_pairs, g_pairs,
        skip, False, (out, gout),
    )
    r_east0 = shift_by(unpaired(r_east0), -1, 0)
    out, gout = unpaired(out), unpaired(gout)
    out, gout = rim(f_lines, r_low, r_corner, g_lines, out, gout)
    out, gout = edge(f_lines, out, r_east1, g_lines, gout, 2 * skip, rows * levels // (2 * skip) - 1)
    out, gout = edge(f_lines, out, r_east0, g_lines, gout, 2 * skip, 1)
    return (grid_of(out, levels), grid_of(gout, levels), grads[:share], grads[share:])


def solution(mesh):
    return jax.shard_map(
        block,
        mesh=mesh,
        in_specs=(
            P("lat", "lon", None, None),
            P("lat"),
            P(AXES, None),
            P(AXES, None),
            P("lat", "lon", None, None),
        ),
        out_specs=(
            P("lat", "lon", None, None),
            P("lat", "lon", None, None),
            P(AXES, None),
            P(AXES, None),
        ),
        check_vma=False,
    )
```

time: 213 us -> 182 us (0.85)
  waiting for transfers between devices: 72.5 us -> 35.5 us
  Pallas kernels: 83.5 us -> 88.4 us
  starting transfers between devices: 26.7 us -> 30.5 us
    ppermute x12 -> x7, waiting for transfers between devices: 39.2 us -> 10.2 us  [shift_by(): return lax.ppermute(block, AXES, route)]
    ppermute x15 -> x14, waiting for transfers between devices: 33.3 us -> 25.4 us  [swap(): return lax.ppermute(block, AXES, [(i, i ^ bit) for i in range(total)])]
    pallas_call x5 -> x11, Pallas kernels: 83.5 us -> 88.4 us  [the longest x3 56.6 us: attention(): pl.pallas_call(functools.partial(attention_kernel, carried=bool(carry), l...]
    another operation x2 -> x7, local copies, waits for them, and re-layouts: 1.92 us -> 5.5 us  [the longest x3 2.69 us: attention(): regions[:, :, None]]
    slice x8 -> x7, local copies, waits for them, and re-layouts: 9.58 us -> 6.09 us  [the longest x2 2.09 us: block(): low = shift_by(both([f_lines[:2 * skip], g_lines[:2 * skip]]), 0, 1)]
    convert_element_type x1 -> x0, other arithmetic: 2.78 us -> none  [scatter_sum(): lax.dynamic_index_in_dim(held, 1 - mine, axis, keepdims=True).astype(BF16)]
    another operation x0 -> x3, other arithmetic: none -> 2.71 us  [the longest x1 0.99 us: block(): low = shift_by(both([f_lines[:2 * skip], g_lines[:2 * skip]]), 0, 1)]
    ppermute x15 -> x14, starting transfers between devices: 17.3 us -> 19.8 us  [swap(): return lax.ppermute(block, AXES, [(i, i ^ bit) for i in range(total)])]
  transfers between devices with their start and end apart: 27 -> 21, of which waited for: 15 -> 7; matrix products, arithmetic and copies ran while one was open for 6% -> 9% of each run, Pallas kernels for 14% -> 18%
where the time goes in v2:
time: 182 us; the launch traced here: 181 us
  Pallas kernels  88.4 us (49%)
  waiting for transfers between devices  35.5 us (20%)
  starting transfers between devices  30.5 us (17%)
  local copies, waits for them, and re-layouts  16.4 us (9%)
  other arithmetic  9.35 us (5%)
    pallas_call x3, Pallas kernels, attention(): pl.pallas_call(functools.partial(attention_kernel, carried=bool(carry), l...  56.6 us
    ppermute x14, waiting for transfers between devices, swap(): return lax.ppermute(block, AXES, [(i, i ^ bit) for i in range(total)])  25.4 us
    ppermute x14, starting transfers between devices, swap(): return lax.ppermute(block, AXES, [(i, i ^ bit) for i in range(total)])  19.8 us
    pallas_call x2, Pallas kernels, finish(): pl.pallas_call(functools.partial(finish_kernel, low=low), grid=(2,), in_s...  14.3 us
    ppermute x7, starting transfers between devices, shift_by(): return lax.ppermute(block, AXES, route)  10.7 us
    pallas_call x3, Pallas kernels, assembled(): pl.pallas_call(kernel, grid=(2,), in_specs=specs, out_specs=[out(width),...  10.6 us
    ppermute x7, waiting for transfers between devices, shift_by(): return lax.ppermute(block, AXES, route)  10.2 us
    pallas_call x2, Pallas kernels, edge(): pl.pallas_call(edge_kernel, grid=(n,), in_specs=[at, at, strip, at, at],...  4.24 us
  transfers between devices with their start and end apart: 21, of which 7 were waited for; matrix products, arithmetic and copies ran while one was open for 9% of the time, Pallas kernels for 18%

profile of v2, /device:TPU:0, one launch (start us, length us, event | category | flops | bytes accessed | tf_op | source)
XLA Modules:
  0.0 181.1 jit_solution(7560350345158843797)
XLA Ops:
  1.5 5.1 %collective-permute-start.3 = (bf16[1,1,1,1,1,64,512]{6,5,4,3,2,1,0:T(8,128)(2,1)S(1)}, bf16[1,1,1,1,1,64,512]{6,5,4,3,2,1,0:T(8,128)(2,1)S(1)}, u32[]{:S(2)}, u32[]{:S(2)}) collective-permute-start(bf16[1,1,1,1,1,64,512]{6,5,4,3,2,1,0:T(8,128)(2,1)S(1)} %maximum_bitcast_fusion), channel_id=1, source_target_pairs={{0,3},{1,2},{2,1},{3,0},{4,7},{5,6},{6,5},{7,4},{8,11},{9,10},{10,... | collective-permute-start | bytes 196616 | tf_op jit(solution)/shard_map/ppermute | solution.py:464
  9.4 1.3 collective-permute-start
  10.9 1.3 collective-permute-done.4
  12.3 1.6 collective-permute-start.8
  14.8 1.6 collective-permute-start.6
  17.6 2.2 %collective-permute-start.2 = (bf16[2,18,8,512]{3,2,1,0:T(8,128)(2,1)}, bf16[2,18,8,512]{3,2,1,0:T(8,128)(2,1)S(1)}, u32[]{:S(2)}, u32[]{:S(2)}) collective-permute-start(bf16[2,18,8,512]{3,2,1,0:T(8,128)(2,1)} %pad_maximum_fusion.6), channel_id=1, source_target_pairs={{5,0},{6,1},{7,2},{4,3},{9,4},{10,5},{11,6},{8,7},{13,8},{14,9},{1... | collective-permute-start | bytes 884744 | tf_op jit(solution)/shard_map/ppermute | solution.py:447
  21.9 11.9 %collective-permute-done.8 = bf16[1,1,1,2,2,64,512]{6,5,4,3,2,1,0:T(8,128)(2,1)S(1)} collective-permute-done((bf16[1,1,1,2,2,64,512]{6,5,4,3,2,1,0:T(8,128)(2,1)S(1)}, bf16[1,1,1,2,2,64,512]{6,5,4,3,2,1,0:T(8,128)(2,1)S(1)}, u32[]{:S(2)}, u32[]{:S(2)}) %collective-permute-start.8) | collective-permute-done | bytes 262176 | tf_op jit(solution)/shard_map/ppermute | solution.py:464
  33.9 3.7 %collective-permute-done.6 = bf16[1,1,1,2,2,64,512]{6,5,4,3,2,1,0:T(8,128)(2,1)S(1)} collective-permute-done((bf16[1,1,1,2,2,64,512]{6,5,4,3,2,1,0:T(8,128)(2,1)S(1)}, bf16[1,1,1,2,2,64,512]{6,5,4,3,2,1,0:T(8,128)(2,1)S(1)}, u32[]{:S(2)}, u32[]{:S(2)}) %collective-permute-start.6) | collective-permute-done | bytes 262176 | tf_op jit(solution)/shard_map/ppermute | solution.py:464
  39.9 3.6 %collective-permute-start.1 = (bf16[2,18,24,512]{3,2,1,0:T(8,128)(2,1)}, bf16[2,18,24,512]{3,2,1,0:T(8,128)(2,1)}, u32[]{:S(2)}, u32[]{:S(2)}) collective-permute-start(bf16[2,18,24,512]{3,2,1,0:T(8,128)(2,1)} %pad_maximum_fusion.3), channel_id=1, source_target_pairs={{1,0},{2,1},{3,2},{0,3},{5,4},{6,5},{7,6},{4,7},{9,8},{10,9},{11,1... | collective-permute-start | bytes 2654216 | tf_op jit(solution)/shard_map/ppermute | solution.py:447
  48.3 3.2 %shard_map.85 = (bf16[1,18,24,512]{3,2,1,0:T(8,128)(2,1)}, f32[1,18,24,128]{3,2,1,0:T(8,128)}, bf16[1,18,24,512]{3,2,1,0:T(8,128)(2,1)}) custom-call(bf16[36,48,512]{2,1,0:T(8,128)(2,1)} %bitcast.76, bf16[36,48,512]{2,1,0:T(8,128)(2,1)} %bitcast.87), custom_call_target="tpu_custom_call" | custom-call | flops 11059200 | bytes 1769472 | tf_op jit(solution)/shard_map/pallas_call | solution.py:139
  52.4 3.3 %shard_map.88 = (bf16[1,18,24,512]{3,2,1,0:T(8,128)(2,1)}, f32[1,18,24,128]{3,2,1,0:T(8,128)}, bf16[1,18,24,512]{3,2,1,0:T(8,128)(2,1)}) custom-call(bf16[36,48,512]{2,1,0:T(8,128)(2,1)} %bitcast.77, bf16[36,48,512]{2,1,0:T(8,128)(2,1)} %bitcast.88, bf16[2,27,16,512]{3,2,1,0:T(8,128)(2,1)} %bitcast.113), custom_call_target="tpu_custom_call" | custom-call | flops 11059200 | bytes 1769472 | tf_op jit(solution)/shard_map/pallas_call | solution.py:139
  55.7 7.7 %collective-permute-done.1 = bf16[2,18,24,512]{3,2,1,0:T(8,128)(2,1)} collective-permute-done((bf16[2,18,24,512]{3,2,1,0:T(8,128)(2,1)}, bf16[2,18,24,512]{3,2,1,0:T(8,128)(2,1)}, u32[]{:S(2)}, u32[]{:S(2)}) %collective-permute-start.1) | collective-permute-done | bytes 884768 | tf_op jit(solution)/shard_map/ppermute | solution.py:447
  63.4 4.2 %shard_map.84 = (bf16[2,18,24,512]{3,2,1,0:T(8,128)(2,1)}, f32[2,18,24,128]{3,2,1,0:T(8,128)}, bf16[2,18,24,512]{3,2,1,0:T(8,128)(2,1)}) custom-call(bf16[36,48,512]{2,1,0:T(8,128)(2,1)} %bitcast.78, bf16[36,48,512]{2,1,0:T(8,128)(2,1)} %bitcast.89, bf16[2,27,16,512]{3,2,1,0:T(8,128)(2,1)} %bitcast.114, bf16[2,9,48,512]{3,2,1,0:T(8,128)(2,1)} %bitcast.12.low_ref, ...), custom_call_target="tpu_custom_call" | custom-call | flops 22118400 | bytes 3538944 | tf_op jit(solution)/shard_map/pallas_call | solution.py:139
  67.9 1.3 slice.85
  70.0 14.1 %shard_map.86 = (bf16[1,432,512]{2,1,0:T(8,128)(2,1)}, bf16[1,3,432,512]{3,2,1,0:T(8,128)(2,1)}, f32[3,512,512]{2,1,0:T(8,128)}, f32[512,512]{1,0:T(8,128)}) custom-call(bf16[1,432,512]{2,1,0:T(8,128)(2,1)} %bitcast.124, bf16[1,432,512]{2,1,0:T(8,128)(2,1)} %bitcast.135, s32[1,432,1]{2,1,0:T(8,128)} %copy.23.refs_2_, ...), custom_call_target="tpu_custom_call" | custom-call | flops 2958557184 | bytes 2654208 | tf_op jit(solution)/shard_map/pallas_call | solution.py:268
  84.2 27.9 %shard_map.87 = (bf16[2,432,512]{2,1,0:T(8,128)(2,1)}, bf16[2,3,432,512]{3,2,1,0:T(8,128)(2,1)}, f32[3,512,512]{2,1,0:T(8,128)}, f32[512,512]{1,0:T(8,128)}) custom-call(bf16[2,432,512]{2,1,0:T(8,128)(2,1)} %bitcast.115, bf16[2,432,512]{2,1,0:T(8,128)(2,1)} %bitcast.132, s32[2,432,1]{2,1,0:T(8,128)} %copy.24.refs_2_, s32[2,1,432]{2,1,0:T(1,128)} %copy.25.refs_3_, ...), custom_call_target="tpu_custom_call" | custom-call | flops 5917114368 | bytes 5308416 | tf_op jit(solution)/shard_map/pallas_call | solution.py:268
  112.0 14.6 %shard_map.89 = (bf16[1,432,512]{2,1,0:T(8,128)(2,1)}, bf16[1,3,432,512]{3,2,1,0:T(8,128)(2,1)}, bf16[3,512,512]{2,1,0:T(8,128)(2,1)}, bf16[512,512]{1,0:T(8,128)(2,1)}) custom-call(bf16[1,432,512]{2,1,0:T(8,128)(2,1)} %bitcast.126, bf16[1,432,512]{2,1,0:T(8,128)(2,1)} %bitcast.134, s32[1,432,1]{2,1,0:T(8,128)} %copy.26.refs_2_, ...), custom_call_target="tpu_custom_call" | custom-call | flops 2958557184 | bytes 2654208 | tf_op jit(solution)/shard_map/pallas_call | solution.py:268
  126.7 1.3 fusion
  128.1 7.3 %finish_low.1 = (bf16[36,48,512]{2,1,0:T(8,128)(2,1)}, bf16[36,48,512]{2,1,0:T(8,128)(2,1)}, bf16[2,9,16,512]{3,2,1,0:T(8,128)(2,1)}, bf16[2,9,48,512]{3,2,1,0:T(8,128)(2,1)}, bf16[2,9,16,512]{3,2,1,0:T(8,128)(2,1)}) custom-call(bf16[2,432,512]{2,1,0:T(8,128)(2,1)} %get-tuple-element.45.refs_0_.refs_4_, ...), custom_call_target="tpu_custom_call" | custom-call | flops 1811939328 | bytes 14155776 | tf_op jit(solution)/shard_map/finish_low/pallas_call | solution.py:373
  135.8 1.6 convert_add_fusion
  137.4 1.3 copy-done.1
  138.8 2.1 %collective-permute-start.15 = (bf16[1,1,1,2,2,64,512]{6,5,4,3,2,1,0:T(8,128)(2,1)S(1)}, bf16[1,1,1,2,2,64,512]{6,5,4,3,2,1,0:T(8,128)(2,1)S(1)}, u32[]{:S(2)}, u32[]{:S(2)}) collective-permute-start(bf16[1,1,1,2,2,64,512]{6,5,4,3,2,1,0:T(8,128)(2,1)S(1)} %get-tuple-element.76), channel_id=1, source_target_pairs={{0,8},{1,9},{2,10},{3,11},{4,12},{5,13},{6,14},{7,15},{8,0},{9,1},... | collective-permute-start | bytes 786440 | tf_op jit(solution)/shard_map/ppermute | solution.py:464
  141.0 1.5 collective-permute-start.16
  142.5 7.0 %finish_top.1 = (bf16[36,48,512]{2,1,0:T(8,128)(2,1)}, bf16[36,48,512]{2,1,0:T(8,128)(2,1)}, bf16[2,18,16,512]{3,2,1,0:T(8,128)(2,1)}) custom-call(bf16[1,432,512]{2,1,0:T(8,128)(2,1)} %get-tuple-element.50.refs_0_, bf16[1,3,432,512]{3,2,1,0:T(8,128)(2,1)} %get-tuple-element.51.refs_1_, ...), custom_call_target="tpu_custom_call", output_to_operand_aliasing={{0}: (12, {}), {1}: (13, {})} | custom-call | flops 1811939328 | bytes 14155776 | tf_op jit(solution)/shard_map/finish_top/pallas_call | solution.py:373
  149.6 3.1 %collective-permute-start.11 = (bf16[2,18,8,512]{3,2,1,0:T(8,128)(2,1)}, bf16[2,18,8,512]{3,2,1,0:T(8,128)(2,1)S(1)}, u32[]{:S(2)}, u32[]{:S(2)}) collective-permute-start(bf16[2,18,8,512]{3,2,1,0:T(8,128)(2,1)} %bitcast.33), channel_id=1, source_target_pairs={{31,0},{28,1},{29,2},{30,3},{3,4},{0,5},{1,6},{2,7},{7,8},{4,9},{5... | collective-permute-start | bytes 884744 | tf_op jit(solution)/shard_map/ppermute | solution.py:447
  152.7 8.3 %collective-permute-done.16 = bf16[1,1,1,2,2,64,512]{6,5,4,3,2,1,0:T(8,128)(2,1)S(1)} collective-permute-done((bf16[1,1,1,2,2,64,512]{6,5,4,3,2,1,0:T(8,128)(2,1)S(1)}, bf16[1,1,1,2,2,64,512]{6,5,4,3,2,1,0:T(8,128)(2,1)S(1)}, u32[]{:S(2)}, u32[]{:S(2)}) %collective-permute-start.16) | collective-permute-done | bytes 262176 | tf_op jit(solution)/shard_map/ppermute | solution.py:464
  162.3 4.1 %collective-permute-start.18 = (bf16[1,1,1,1,1,64,512]{6,5,4,3,2,1,0:T(8,128)(2,1)S(1)}, bf16[1,1,1,1,1,64,512]{6,5,4,3,2,1,0:T(8,128)(2,1)S(1)}, u32[]{:S(2)}, u32[]{:S(2)}) collective-permute-start(bf16[1,1,1,1,1,64,512]{6,5,4,3,2,1,0:T(8,128)(2,1)S(1)} %get-tuple-element.83), channel_id=1, source_target_pairs={{0,1},{1,0},{2,3},{3,2},{4,5},{5,4},{6,7},{7,6},{8,9},{9,8},{10,11... | collective-permute-start | bytes 196616 | tf_op jit(solution)/shard_map/ppermute | solution.py:464
  166.3 2.5 %collective-permute-done.11.c_ref = bf16[2,18,8,512]{3,2,1,0:T(8,128)(2,1)S(1)} collective-permute-done((bf16[2,18,8,512]{3,2,1,0:T(8,128)(2,1)}, bf16[2,18,8,512]{3,2,1,0:T(8,128)(2,1)S(1)}, u32[]{:S(2)}, u32[]{:S(2)}) %collective-permute-start.11) | collective-permute-done | bytes 294944 | tf_op jit(solution)/shard_map/ppermute | solution.py:447
  170.0 1.4 collective-permute-start.20
  171.5 2.5 %rim.1 = (bf16[72,24,512]{2,1,0:T(8,128)(2,1)}, bf16[72,24,512]{2,1,0:T(8,128)(2,1)}) custom-call(bf16[72,24,512]{2,1,0:T(8,128)(2,1)} %bitcast.81, bf16[2,18,24,512]{3,2,1,0:T(8,128)(2,1)} %collective-permute-done.10.low_ref, bf16[2,18,8,512]{3,2,1,0:T(8,128)(2,1)} %copy-done.6, ...), custom_call_target="tpu_custom_call", output_to_operand_aliasing={{0}: (4, {}), {1}: (5, {})} | custom-call | tf_op jit(solution)/shard_map/rim/pallas_call | solution.py:425
  174.7 2.0 %edge.2 = (bf16[72,24,512]{2,1,0:T(8,128)(2,1)}, bf16[72,24,512]{2,1,0:T(8,128)(2,1)}) custom-call(bf16[72,24,512]{2,1,0:T(8,128)(2,1)} %bitcast.82, bf16[72,24,512]{2,1,0:T(8,128)(2,1)} %get-tuple-element.64.o_ref, bf16[2,18,8,512]{3,2,1,0:T(8,128)(2,1)} %copy-done.7, bf16[72,24,512]{2,1,0:T(8,128)(2,1)} %bitcast.93, ...), custom_call_target="tpu_custom_call", output_to_operand_aliasing={{0}: (1, {}), {1}: (4, {})} | custom-call | tf_op jit(solution)/shard_map/edge/pallas_call | solution.py:399
  177.5 2.3 %edge.3 = (bf16[72,24,512]{2,1,0:T(8,128)(2,1)}, bf16[72,24,512]{2,1,0:T(8,128)(2,1)}) custom-call(bf16[72,24,512]{2,1,0:T(8,128)(2,1)} %bitcast.83, bf16[72,24,512]{2,1,0:T(8,128)(2,1)} %get-tuple-element.67.o_ref, bf16[2,36,8,512]{3,2,1,0:T(8,128)(2,1)} %copy-done.4, bf16[72,24,512]{2,1,0:T(8,128)(2,1)} %bitcast.94, ...), custom_call_target="tpu_custom_call", output_to_operand_aliasing={{0}: (1, {}), {1}: (4, {})} | custom-call | tf_op jit(solution)/shard_map/edge/pallas_call | solution.py:399
  (93 shorter events, 23.3 us)
Async XLA Ops:
  0.6 10.2 %copy-start.8 = (bf16[48,512]{1,0:T(8,128)(2,1)S(1)}, bf16[48,512]{1,0:T(8,128)(2,1)}, u32[]{:S(2)}) copy-start(bf16[48,512]{1,0:T(8,128)(2,1)} %param.7) | copy-start | bytes 147460
  0.6 10.2 %copy-start.9 = (bf16[16,512]{1,0:T(8,128)(2,1)S(1)}, bf16[16,512]{1,0:T(8,128)(2,1)}, u32[]{:S(2)}) copy-start(bf16[16,512]{1,0:T(8,128)(2,1)} %param.8) | copy-start | bytes 49156
  1.5 9.4 %collective-permute-start.3 = (bf16[1,1,1,1,1,64,512]{6,5,4,3,2,1,0:T(8,128)(2,1)S(1)}, bf16[1,1,1,1,1,64,512]{6,5,4,3,2,1,0:T(8,128)(2,1)S(1)}, u32[]{:S(2)}, u32[]{:S(2)}) collective-permute-start(bf16[1,1,1,1,1,64,512]{6,5,4,3,2,1,0:T(8,128)(2,1)S(1)} %maximum_bitcast_fusion), channel_id=1, source_target_pairs={{0,3},{1,2},{2,1},{3,0},{4,7},{5,6},{6,5},{7,4},{8,11},{9,10},{10,... | collective-permute-start | bytes 196616 | tf_op jit(solution)/shard_map/ppermute | solution.py:464
  6.6 5.6 %collective-permute-start.4 = (bf16[1,1,1,1,1,64,512]{6,5,4,3,2,1,0:T(8,128)(2,1)S(1)}, bf16[1,1,1,1,1,64,512]{6,5,4,3,2,1,0:T(8,128)(2,1)S(1)}, u32[]{:S(2)}, u32[]{:S(2)}) collective-permute-start(bf16[1,1,1,1,1,64,512]{6,5,4,3,2,1,0:T(8,128)(2,1)S(1)} %maximum_bitcast_fusion), channel_id=1, source_target_pairs={{0,2},{1,3},{2,0},{3,1},{4,6},{5,7},{6,4},{7,5},{8,10},{9,11},{10,... | collective-permute-start | bytes 196616 | tf_op jit(solution)/shard_map/ppermute | solution.py:464
  6.6 4.3 %collective-permute-start.5 = (bf16[1,1,1,1,1,64,512]{6,5,4,3,2,1,0:T(8,128)(2,1)S(1)}, bf16[1,1,1,1,1,64,512]{6,5,4,3,2,1,0:T(8,128)(2,1)S(1)}, u32[]{:S(2)}, u32[]{:S(2)}) collective-permute-start(bf16[1,1,1,1,1,64,512]{6,5,4,3,2,1,0:T(8,128)(2,1)S(1)} %maximum_bitcast_fusion), channel_id=1, source_target_pairs={{0,1},{1,0},{2,3},{3,2},{4,5},{5,4},{6,7},{7,6},{8,9},{9,8},{10,11... | collective-permute-start | bytes 196616 | tf_op jit(solution)/shard_map/ppermute | solution.py:464
  9.4 42.0 %collective-permute-start = (bf16[2,54,8,512]{3,2,1,0:T(8,128)(2,1)}, bf16[2,54,8,512]{3,2,1,0:T(8,128)(2,1)S(1)}, u32[]{:S(2)}, u32[]{:S(2)}) collective-permute-start(bf16[2,54,8,512]{3,2,1,0:T(8,128)(2,1)} %pad_maximum_fusion.2), channel_id=1, source_target_pairs={{4,0},{5,1},{6,2},{7,3},{8,4},{9,5},{10,6},{11,7},{12,8},{13,9},{1... | collective-permute-start | bytes 2654216 | tf_op jit(solution)/shard_map/ppermute | solution.py:447
  12.3 21.6 %collective-permute-start.8 = (bf16[1,1,1,2,2,64,512]{6,5,4,3,2,1,0:T(8,128)(2,1)S(1)}, bf16[1,1,1,2,2,64,512]{6,5,4,3,2,1,0:T(8,128)(2,1)S(1)}, u32[]{:S(2)}, u32[]{:S(2)}) collective-permute-start(bf16[1,1,1,2,2,64,512]{6,5,4,3,2,1,0:T(8,128)(2,1)S(1)} %pad_maximum_fusion.7), channel_id=1, source_target_pairs={{0,8},{1,9},{2,10},{3,11},{4,12},{5,13},{6,14},{7,15},{8,0},{9,1},... | collective-permute-start | bytes 786440 | tf_op jit(solution)/shard_map/ppermute | solution.py:464
  14.8 22.8 %collective-permute-start.6 = (bf16[1,1,1,2,2,64,512]{6,5,4,3,2,1,0:T(8,128)(2,1)S(1)}, bf16[1,1,1,2,2,64,512]{6,5,4,3,2,1,0:T(8,128)(2,1)S(1)}, u32[]{:S(2)}, u32[]{:S(2)}) collective-permute-start(bf16[1,1,1,2,2,64,512]{6,5,4,3,2,1,0:T(8,128)(2,1)S(1)} %pad_maximum_fusion.7), channel_id=1, source_target_pairs={{0,24},{1,25},{2,26},{3,27},{4,28},{5,29},{6,30},{7,31},{8,16},{9,... | collective-permute-start | bytes 786440 | tf_op jit(solution)/shard_map/ppermute | solution.py:464
  16.4 21.3 %collective-permute-start.7 = (bf16[1,1,1,2,2,64,512]{6,5,4,3,2,1,0:T(8,128)(2,1)S(1)}, bf16[1,1,1,2,2,64,512]{6,5,4,3,2,1,0:T(8,128)(2,1)S(1)}, u32[]{:S(2)}, u32[]{:S(2)}) collective-permute-start(bf16[1,1,1,2,2,64,512]{6,5,4,3,2,1,0:T(8,128)(2,1)S(1)} %pad_maximum_fusion.7), channel_id=1, source_target_pairs={{0,16},{1,17},{2,18},{3,19},{4,20},{5,21},{6,22},{7,23},{8,24},{9,... | collective-permute-start | bytes 786440 | tf_op jit(solution)/shard_map/ppermute | solution.py:464
  17.6 38.1 %collective-permute-start.2 = (bf16[2,18,8,512]{3,2,1,0:T(8,128)(2,1)}, bf16[2,18,8,512]{3,2,1,0:T(8,128)(2,1)S(1)}, u32[]{:S(2)}, u32[]{:S(2)}) collective-permute-start(bf16[2,18,8,512]{3,2,1,0:T(8,128)(2,1)} %pad_maximum_fusion.6), channel_id=1, source_target_pairs={{5,0},{6,1},{7,2},{4,3},{9,4},{10,5},{11,6},{8,7},{13,8},{14,9},{1... | collective-permute-start | bytes 884744 | tf_op jit(solution)/shard_map/ppermute | solution.py:447
  37.8 5.7 %copy-start.10 = (s32[24]{0:T(128)S(1)}, s32[24]{0:T(128)}, u32[]{:S(2)}) copy-start(s32[24]{0:T(128)} %param.6) | copy-start | bytes 292
  38.9 28.7 %collective-permute-start.9 = (bf16[2,2,1,2,2,64,512]{6,5,4,3,2,1,0:T(8,128)(2,1)}, bf16[2,2,1,2,2,64,512]{6,5,4,3,2,1,0:T(8,128)(2,1)S(1)}, u32[]{:S(2)}, u32[]{:S(2)}) collective-permute-start(bf16[2,2,1,2,2,64,512]{6,5,4,3,2,1,0:T(8,128)(2,1)} %pad_maximum_fusion.1), channel_id=1, source_target_pairs={{0,4},{1,5},{2,6},{3,7},{4,0},{5,1},{6,2},{7,3},{8,12},{9,13},{10,... | collective-permute-start | bytes 3145736 | tf_op jit(solution)/shard_map/ppermute | solution.py:464
  39.9 23.5 %collective-permute-start.1 = (bf16[2,18,24,512]{3,2,1,0:T(8,128)(2,1)}, bf16[2,18,24,512]{3,2,1,0:T(8,128)(2,1)}, u32[]{:S(2)}, u32[]{:S(2)}) collective-permute-start(bf16[2,18,24,512]{3,2,1,0:T(8,128)(2,1)} %pad_maximum_fusion.3), channel_id=1, source_target_pairs={{1,0},{2,1},{3,2},{0,3},{5,4},{6,5},{7,6},{4,7},{9,8},{10,9},{11,1... | collective-permute-start | bytes 2654216 | tf_op jit(solution)/shard_map/ppermute | solution.py:447
  51.5 0.9 copy-start.2
  55.7 7.7 %copy-start.5 = (bf16[2,18,8,512]{3,2,1,0:T(8,128)(2,1)}, bf16[2,18,8,512]{3,2,1,0:T(8,128)(2,1)S(1)}, u32[]{:S(2)}) copy-start(bf16[2,18,8,512]{3,2,1,0:T(8,128)(2,1)S(1)} %collective-permute-done.2) | copy-start | bytes 884740
  128.0 7.8 %collective-permute-start.14 = (bf16[2,2,1,2,2,64,512]{6,5,4,3,2,1,0:T(8,128)(2,1)S(1)}, bf16[2,2,1,2,2,64,512]{6,5,4,3,2,1,0:T(8,128)(2,1)}, u32[]{:S(2)}, u32[]{:S(2)}) collective-permute-start(bf16[2,2,1,2,2,64,512]{6,5,4,3,2,1,0:T(8,128)(2,1)S(1)} %fusion), channel_id=1, source_target_pairs={{0,4},{1,5},{2,6},{3,7},{4,0},{5,1},{6,2},{7,3},{8,12},{9,13},{10,... | collective-permute-start | bytes 3145736 | tf_op jit(solution)/shard_map/ppermute | solution.py:464
  128.1 7.8 %copy-start = (bf16[3,512,512]{2,1,0:T(8,128)(2,1)S(1)}, bf16[3,512,512]{2,1,0:T(8,128)(2,1)}, u32[]{:S(2)}) copy-start(bf16[3,512,512]{2,1,0:T(8,128)(2,1)} %get-tuple-element.72) | copy-start | bytes 4718596
  128.1 7.7 %copy-start.3 = (bf16[512,512]{1,0:T(8,128)(2,1)S(1)}, bf16[512,512]{1,0:T(8,128)(2,1)}, u32[]{:S(2)}) copy-start(bf16[512,512]{1,0:T(8,128)(2,1)} %get-tuple-element.73) | copy-start | bytes 1572868
  135.4 34.6 %collective-permute-start.10 = (bf16[2,18,24,512]{3,2,1,0:T(8,128)(2,1)}, bf16[2,18,24,512]{3,2,1,0:T(8,128)(2,1)}, u32[]{:S(2)}, u32[]{:S(2)}) collective-permute-start(bf16[2,18,24,512]{3,2,1,0:T(8,128)(2,1)} %bitcast.131), channel_id=1, source_target_pairs={{3,0},{0,1},{1,2},{2,3},{7,4},{4,5},{5,6},{6,7},{11,8},{8,9},{9,10... | collective-permute-start | bytes 2654216 | tf_op jit(solution)/shard_map/ppermute | solution.py:447
  137.4 1.3 copy-start.1
  138.8 10.8 %collective-permute-start.15 = (bf16[1,1,1,2,2,64,512]{6,5,4,3,2,1,0:T(8,128)(2,1)S(1)}, bf16[1,1,1,2,2,64,512]{6,5,4,3,2,1,0:T(8,128)(2,1)S(1)}, u32[]{:S(2)}, u32[]{:S(2)}) collective-permute-start(bf16[1,1,1,2,2,64,512]{6,5,4,3,2,1,0:T(8,128)(2,1)S(1)} %get-tuple-element.76), channel_id=1, source_target_pairs={{0,8},{1,9},{2,10},{3,11},{4,12},{5,13},{6,14},{7,15},{8,0},{9,1},... | collective-permute-start | bytes 786440 | tf_op jit(solution)/shard_map/ppermute | solution.py:464
  141.0 20.0 %collective-permute-start.16 = (bf16[1,1,1,2,2,64,512]{6,5,4,3,2,1,0:T(8,128)(2,1)S(1)}, bf16[1,1,1,2,2,64,512]{6,5,4,3,2,1,0:T(8,128)(2,1)S(1)}, u32[]{:S(2)}, u32[]{:S(2)}) collective-permute-start(bf16[1,1,1,2,2,64,512]{6,5,4,3,2,1,0:T(8,128)(2,1)S(1)} %get-tuple-element.78), channel_id=1, source_target_pairs={{0,16},{1,17},{2,18},{3,19},{4,20},{5,21},{6,22},{7,23},{8,24},{9,... | collective-permute-start | bytes 786440 | tf_op jit(solution)/shard_map/ppermute | solution.py:464
  142.5 18.5 %collective-permute-start.17 = (bf16[1,1,1,2,2,64,512]{6,5,4,3,2,1,0:T(8,128)(2,1)S(1)}, bf16[1,1,1,2,2,64,512]{6,5,4,3,2,1,0:T(8,128)(2,1)S(1)}, u32[]{:S(2)}, u32[]{:S(2)}) collective-permute-start(bf16[1,1,1,2,2,64,512]{6,5,4,3,2,1,0:T(8,128)(2,1)S(1)} %get-tuple-element.77), channel_id=1, source_target_pairs={{0,24},{1,25},{2,26},{3,27},{4,28},{5,29},{6,30},{7,31},{8,16},{9,... | collective-permute-start | bytes 786440 | tf_op jit(solution)/shard_map/ppermute | solution.py:464
  142.5 18.5 %copy-start.11 = (bf16[2,9,16,512]{3,2,1,0:T(8,128)(2,1)S(1)}, bf16[2,9,16,512]{3,2,1,0:T(8,128)(2,1)}, u32[]{:S(2)}) copy-start(bf16[2,9,16,512]{3,2,1,0:T(8,128)(2,1)} %get-tuple-element.65) | copy-start | bytes 884740
  149.5 27.2 %collective-permute-start.13 = (bf16[2,36,8,512]{3,2,1,0:T(8,128)(2,1)}, bf16[2,36,8,512]{3,2,1,0:T(8,128)(2,1)S(1)}, u32[]{:S(2)}, u32[]{:S(2)}) collective-permute-start(bf16[2,36,8,512]{3,2,1,0:T(8,128)(2,1)} %bitcast.133), channel_id=1, source_target_pairs={{28,0},{29,1},{30,2},{31,3},{0,4},{1,5},{2,6},{3,7},{4,8},{5,9},{6... | collective-permute-start | bytes 1769480 | tf_op jit(solution)/shard_map/ppermute | solution.py:447
  149.6 19.2 %collective-permute-start.11 = (bf16[2,18,8,512]{3,2,1,0:T(8,128)(2,1)}, bf16[2,18,8,512]{3,2,1,0:T(8,128)(2,1)S(1)}, u32[]{:S(2)}, u32[]{:S(2)}) collective-permute-start(bf16[2,18,8,512]{3,2,1,0:T(8,128)(2,1)} %bitcast.33), channel_id=1, source_target_pairs={{31,0},{28,1},{29,2},{30,3},{3,4},{0,5},{1,6},{2,7},{7,8},{4,9},{5... | collective-permute-start | bytes 884744 | tf_op jit(solution)/shard_map/ppermute | solution.py:447
  161.0 13.0 %collective-permute-start.12 = (bf16[2,18,8,512]{3,2,1,0:T(8,128)(2,1)S(1)}, bf16[2,18,8,512]{3,2,1,0:T(8,128)(2,1)S(1)}, u32[]{:S(2)}, u32[]{:S(2)}) collective-permute-start(bf16[2,18,8,512]{3,2,1,0:T(8,128)(2,1)S(1)} %bitcast.136), channel_id=1, source_target_pairs={{28,0},{29,1},{30,2},{31,3},{0,4},{1,5},{2,6},{3,7},{4,8},{5,9},{6... | collective-permute-start | bytes 884744 | tf_op jit(solution)/shard_map/ppermute | solution.py:447
  162.3 17.5 %collective-permute-start.18 = (bf16[1,1,1,1,1,64,512]{6,5,4,3,2,1,0:T(8,128)(2,1)S(1)}, bf16[1,1,1,1,1,64,512]{6,5,4,3,2,1,0:T(8,128)(2,1)S(1)}, u32[]{:S(2)}, u32[]{:S(2)}) collective-permute-start(bf16[1,1,1,1,1,64,512]{6,5,4,3,2,1,0:T(8,128)(2,1)S(1)} %get-tuple-element.83), channel_id=1, source_target_pairs={{0,1},{1,0},{2,3},{3,2},{4,5},{5,4},{6,7},{7,6},{8,9},{9,8},{10,11... | collective-permute-start | bytes 196616 | tf_op jit(solution)/shard_map/ppermute | solution.py:464
  168.8 2.7 %copy-start.6 = (bf16[2,18,8,512]{3,2,1,0:T(8,128)(2,1)}, bf16[2,18,8,512]{3,2,1,0:T(8,128)(2,1)S(1)}, u32[]{:S(2)}) copy-start(bf16[2,18,8,512]{3,2,1,0:T(8,128)(2,1)S(1)} %collective-permute-done.11.c_ref) | copy-start | bytes 884740
  168.8 11.0 %collective-permute-start.19 = (bf16[1,1,1,1,1,64,512]{6,5,4,3,2,1,0:T(8,128)(2,1)S(1)}, bf16[1,1,1,1,1,64,512]{6,5,4,3,2,1,0:T(8,128)(2,1)S(1)}, u32[]{:S(2)}, u32[]{:S(2)}) collective-permute-start(bf16[1,1,1,1,1,64,512]{6,5,4,3,2,1,0:T(8,128)(2,1)S(1)} %get-tuple-element.85), channel_id=1, source_target_pairs={{0,2},{1,3},{2,0},{3,1},{4,6},{5,7},{6,4},{7,5},{8,10},{9,11},{10,... | collective-permute-start | bytes 196616 | tf_op jit(solution)/shard_map/ppermute | solution.py:464
  170.0 9.8 %collective-permute-start.20 = (bf16[1,1,1,1,1,64,512]{6,5,4,3,2,1,0:T(8,128)(2,1)S(1)}, bf16[1,1,1,1,1,64,512]{6,5,4,3,2,1,0:T(8,128)(2,1)S(1)}, u32[]{:S(2)}, u32[]{:S(2)}) collective-permute-start(bf16[1,1,1,1,1,64,512]{6,5,4,3,2,1,0:T(8,128)(2,1)S(1)} %get-tuple-element.84), channel_id=1, source_target_pairs={{0,3},{1,2},{2,1},{3,0},{4,7},{5,6},{6,5},{7,4},{8,11},{9,10},{10,... | collective-permute-start | bytes 196616 | tf_op jit(solution)/shard_map/ppermute | solution.py:464
  176.7 0.8 copy-start.4
  (1 other events, 0.7 us)

commit v3 on v2

v3 whole, which is shorter than its diff:
```python
import functools

import jax
import jax.numpy as jnp
from jax import lax
from jax.experimental import pallas as pl
from jax.experimental.pallas import tpu as pltpu
from jax.sharding import PartitionSpec as P


HEAD = 64
WIN = 12
HALF = WIN // 2
EPSILON = 1e-05
AXES = ("lon", "lat")
LANES = 128
SUB = 8


F32 = jnp.float32
BF16 = jnp.bfloat16


def nt(a, b):
    return lax.dot_general(a, b, (((1,), (1,)), ((), ())), preferred_element_type=F32)


def nn(a, b):
    return lax.dot_general(a, b, (((1,), (0,)), ((), ())), preferred_element_type=F32)


GROUP = 2


def sub_index(width):
    return lax.broadcasted_iota(jnp.int32, (SUB, width), 0)


def pick_first(own):
    s = sub_index(own.shape[1])
    t0a, t1a, t2a, t0b, t1b, t2b = [own[8 * i : 8 * i + 8] for i in range(6)]
    mixed = jnp.where(
        s < 2,
        t2a,
        jnp.where(s < 4, pltpu.roll(t2b, 2, 0), jnp.where(s < 6, pltpu.roll(t0b, 6, 0), t0a)),
    )
    return jnp.concatenate([t1a, t1b, mixed], axis=0)


def pick_second(own, strip):
    s = sub_index(own.shape[1])
    t2a, t2b = own[16:24], own[40:48]
    ha, hb = strip[:8], strip[8:]
    n1 = jnp.where(s < 2, ha, t2a)
    n2 = jnp.where(s < 2, hb, t2b)
    n3 = jnp.where((s >= 2) & (s < 6), ha, pltpu.roll(hb, 4, 0))
    return jnp.concatenate([n1, n2, n3], axis=0)


def unpick(first, second):
    s = sub_index(first.shape[1])
    t1a, t1b, mixed = first[:8], first[8:16], first[16:]
    n1, n2, n3 = second[:8], second[8:16], second[16:]
    zero = jnp.zeros_like(mixed)
    t0a = jnp.where(s >= 6, mixed, zero)
    t0b = jnp.where(s >= 6, pltpu.roll(mixed, 2, 0), zero)
    t2a = jnp.where(s < 2, mixed, n1)
    t2b = jnp.where(s < 2, pltpu.roll(mixed, 6, 0), n2)
    ha = jnp.where(s < 2, n1, n3)
    hb = jnp.where(s < 2, n2, pltpu.roll(n3, 4, 0))
    own = jnp.concatenate([t0a, t1a, t2a, t0b, t1b, t2b], axis=0)
    return own, jnp.concatenate([ha, hb], axis=0)


def token_regions(region_ids, levels):
    lines = jnp.repeat(region_ids, levels)
    pairs = lines.reshape(-1, 2)
    s = jnp.arange(3 * SUB)
    inner = s % SUB
    line0 = jnp.where(s < 8, 0, jnp.where(s < 16, 1, jnp.where((inner < 2) | (inner >= 6), 0, 1)))
    line1 = jnp.where(s < 8, 0, jnp.where(s < 16, 1, jnp.where((inner >= 2) & (inner < 6), 0, 1)))
    a, b = pairs[:, :1], pairs[:, 1:]
    both = jnp.stack([jnp.where(line0 == 0, a, b), jnp.where(line1 == 0, a, b)])
    per_band = WIN * levels // 2
    bands = pairs.shape[0] // per_band
    return both.reshape(2, bands, per_band * 3 * SUB).transpose(1, 0, 2)


def pack_kernel(f_ref, f_first, g_ref, g_first, low_ref, corner_ref, east_ref):
    n = low_ref.shape[1]
    for i, (x, first) in enumerate(((f_ref, f_first), (g_ref, g_first))):
        low_ref[i] = x[...]
        corner_ref[i] = first[:n]
        east_ref[i] = first[n:]


def pack(f_lines, g_lines, n):
    lines, cols, width = f_lines.shape
    low = pl.BlockSpec((n, cols, width), lambda i: (0, 0, 0))
    first = pl.BlockSpec((lines, SUB, width), lambda i: (0, 0, 0))
    shapes = [(2, n, cols, width), (2, n, SUB, width), (2, lines - n, SUB, width)]
    return pl.pallas_call(
        pack_kernel,
        grid=(1,),
        in_specs=[low, first, low, first],
        out_specs=[pl.BlockSpec(shape, lambda i: (0,) * 4) for shape in shapes],
        out_shape=tuple(jax.ShapeDtypeStruct(shape, BF16) for shape in shapes),
        name="pack",
    )(f_lines, f_lines, g_lines, g_lines)


def norm(block):
    centre = block - jnp.mean(block, axis=-1, keepdims=True)
    inverse = lax.rsqrt(jnp.mean(centre * centre, axis=-1, keepdims=True) + EPSILON)
    return (centre * inverse).astype(BF16), inverse


def put(at, p, block, grads, normed_ref, inv_ref, gs_ref):
    normed, inverse = norm(block)
    normed_ref[at, p] = normed
    inv_ref[at, p] = jnp.broadcast_to(inverse, (3 * SUB, LANES))
    gs_ref[at, p] = grads.astype(BF16)


def assemble_own_kernel(f_ref, g_ref, *outs):
    @pl.loop(0, f_ref.shape[0], unroll=3)
    def _(p):
        put(0, p, pick_first(f_ref[p].astype(F32)), pick_first(g_ref[p].astype(F32)), *outs)


def assemble_below_kernel(f_ref, g_ref, low_ref, *outs):
    @pl.when(pl.program_id(0) == 0)
    def _():
        @pl.loop(0, f_ref.shape[0], unroll=3)
        def _(p):
            put(0, p, pick_first(f_ref[p].astype(F32)), pick_first(g_ref[p].astype(F32)), *outs)

    @pl.when(pl.program_id(0) == 1)
    def _():
        @pl.loop(0, f_ref.shape[0], unroll=3)
        def _(p):
            put(0, p, pick_first(low_ref[0, p].astype(F32)), pick_first(low_ref[1, p].astype(F32)), *outs)


def assemble_second_kernel(f_ref, g_ref, east_ref, low_ref, corner_ref, *outs):
    last = pl.num_programs(0) - 1

    @pl.when(pl.program_id(0) < last)
    def _():
        @pl.loop(0, f_ref.shape[0], unroll=3)
        def _(p):
            put(
                0,
                p,
                pick_second(f_ref[p].astype(F32), east_ref[0, p].astype(F32)),
                pick_second(g_ref[p].astype(F32), east_ref[1, p].astype(F32)),
                *outs,
            )

    @pl.when(pl.program_id(0) == last)
    def _():
        @pl.loop(0, f_ref.shape[0], unroll=3)
        def _(p):
            put(
                0,
                p,
                pick_second(low_ref[0, p].astype(F32), corner_ref[0, p].astype(F32)),
                pick_second(low_ref[1, p].astype(F32), corner_ref[1, p].astype(F32)),
                *outs,
            )


def assembled(kernel, windows, skip, width, specs, args):
    shape = (windows, 2 * skip, 3 * SUB)
    out = lambda w: pl.BlockSpec((1, skip, 3 * SUB, w), lambda s: (s // 2, s % 2, 0, 0))
    outs = pl.pallas_call(
        kernel,
        grid=(2 * windows,),
        in_specs=specs,
        out_specs=[out(width), out(LANES), out(width)],
        out_shape=(
            jax.ShapeDtypeStruct(shape + (width,), BF16),
            jax.ShapeDtypeStruct(shape + (LANES,), F32),
            jax.ShapeDtypeStruct(shape + (width,), BF16),
        ),
        cost_estimate=pl.CostEstimate(
            flops=windows * skip * 3 * SUB * width * 100, transcendentals=0,
            bytes_accessed=windows * skip * 3 * SUB * width * 16),
    )(*args)
    count = 2 * skip * 3 * SUB
    return [x.reshape(windows, count, x.shape[-1]) for x in outs]


def assemble_own(fields, grads, skip):
    width = fields.shape[2]
    own = pl.BlockSpec((skip, 48, width), lambda s: (s + 1, 0, 0))
    return assembled(assemble_own_kernel, 1, skip, width, [own, own], (fields, grads))


def assemble_below(fields, grads, low, skip):
    width = fields.shape[2]
    last = fields.shape[0] // skip - 1
    own = pl.BlockSpec((skip, 48, width), lambda s: (last, 0, 0))
    below = pl.BlockSpec((2, skip, 48, width), lambda s: (0, 0, 0, 0))
    return assembled(assemble_below_kernel, 1, skip, width, [own, own, below], (fields, grads, low))


def assemble_second(fields, grads, east, low, corner, skip):
    width = fields.shape[2]
    n = fields.shape[0] // skip - 1
    own = pl.BlockSpec((skip, 48, width), lambda s: (jnp.minimum(s + 1, n), 0, 0))
    strip = pl.BlockSpec((2, skip, 16, width), lambda s: (0, jnp.minimum(s, n - 1), 0, 0))
    below = pl.BlockSpec((2, skip, 48, width), lambda s: (0, 0, 0, 0))
    diagonal = pl.BlockSpec((2, skip, 16, width), lambda s: (0, 0, 0, 0))
    return assembled(
        assemble_second_kernel, (n + 1) // 2, skip, width, [own, own, strip, below, diagonal],
        (fields, grads, east, low, corner),
    )


def attention_kernel(*refs, first, carried, into):
    normed_ref, gs_ref, reg_ref, w_ref, wp_ref = refs[:5]
    refs = refs[5:]
    if carried:
        gw_in, gp_in = refs[:2]
        refs = refs[2 + (2 if into else 0):]
    att_ref, gqkv_ref, gw_ref, gp_ref = refs
    group = pl.program_id(0) + first
    window = pl.program_id(1)
    scale = HEAD ** (-0.5)
    normed = normed_ref[window]
    grads = gs_ref[window]
    count = normed.shape[0]
    wide = GROUP * LANES
    weights = w_ref[...].reshape(3 * wide, w_ref.shape[2])
    qkv = nt(normed, weights).astype(BF16)
    queries, all_keys, all_values = [qkv[:, wide * i : wide * (i + 1)] for i in range(3)]
    queries = queries * jnp.asarray(scale, BF16)
    grad_att_all = nn(grads, wp_ref[...]).astype(BF16)
    all_keys_t = all_keys.astype(F32).T.astype(BF16) * jnp.asarray(scale, BF16)
    all_values_t = all_values.astype(F32).T.astype(BF16)
    region = reg_ref[window]
    region_t = jnp.broadcast_to(region, (LANES, count)).T
    spread = jnp.concatenate([region_t] * -(-count // LANES), axis=1)[:, :count]
    allowed = spread == region
    lane = lax.broadcasted_iota(jnp.int32, (count, LANES), 1)
    zero = jnp.zeros((), BF16)
    att_t, grad_q_t, grad_ks, grad_vs = [], [], [], []
    for pair in range(GROUP):
        cols = slice(pair * LANES, (pair + 1) * LANES)
        query, keys, values = queries[:, cols], all_keys[:, cols], all_values[:, cols]
        keys_t, values_t = all_keys_t[cols], all_values_t[cols]
        grad_att = grad_att_all[:, cols]
        grad_k = grad_v = None
        for h in range(LANES // HEAD):
            mine = (lane >= h * HEAD) & (lane < (h + 1) * HEAD)
            rows = slice(h * HEAD, (h + 1) * HEAD)
            scores = nt(jnp.where(mine, keys, zero), query)
            scores = jnp.where(allowed, scores, -1e30)
            peak = jnp.max(scores, axis=0, keepdims=True)
            expo = jnp.exp(scores - peak)
            ratio = 1.0 / jnp.sum(expo, axis=0, keepdims=True)
            rounded = (expo * ratio).astype(BF16)
            grad_probs = nt(jnp.where(mine, values, zero), grad_att)
            att_t.append(nn(values_t[rows], rounded))
            inner = jnp.sum(grad_probs * expo, axis=0, keepdims=True) * ratio
            grad_scores = (expo * (grad_probs - inner) * ratio).astype(BF16)
            grad_q_t.append(nn(keys_t[rows], grad_scores))
            part_v = nn(rounded, jnp.where(mine, grad_att, zero))
            part_k = nn(grad_scores, jnp.where(mine, query, zero))
            grad_k = part_k if grad_k is None else grad_k + part_k
            grad_v = part_v if grad_v is None else grad_v + part_v
        grad_ks.append(grad_k)
        grad_vs.append(grad_v)
    att_t = jnp.concatenate(att_t, axis=0)
    grad_q_t = jnp.concatenate(grad_q_t, axis=0)
    grad_k = jnp.concatenate(grad_ks, axis=1)
    grad_v = jnp.concatenate(grad_vs, axis=1)
    att_ref[0] = att_t.T.astype(BF16)
    gqkv_ref[0, 0] = grad_q_t.T.astype(BF16)
    gqkv_ref[0, 1] = grad_k.astype(BF16)
    gqkv_ref[0, 2] = grad_v.astype(BF16)
    turned = [grad_q_t.astype(BF16), grad_k.T.astype(BF16), grad_v.T.astype(BF16)]
    grad_w = nn(jnp.concatenate(turned, axis=0), normed).reshape(3, wide, grads.shape[1])
    grad_p = nn(att_t.astype(BF16), grads).T

    def start(add):
        gw_ref[...] = grad_w + gw_in[...] if add else grad_w
        gp_ref[...] = grad_p + gp_in[...] if add else grad_p

    opening = window == 0
    if carried:
        pl.when(opening & (group < carried))(lambda: start(True))
    pl.when(opening & (group >= carried))(lambda: start(False))

    @pl.when(window > 0)
    def _():
        gw_ref[...] += grad_w
        gp_ref[...] += grad_p


def attention(normed, gs, regions, w_qkv, w_proj, carry=(), carried=0, groups=None, into=()):
    windows, count, width = normed.shape
    wide = GROUP * LANES
    first, number = groups or (0, width // wide)
    whole = lambda *shape: pl.BlockSpec(shape, lambda p, w: (0,) * len(shape))
    rows3 = pl.BlockSpec((3, wide, width), lambda p, w: (0, p + first, 0))
    cols1 = pl.BlockSpec((width, wide), lambda p, w: (0, p + first))
    anyw = pl.BlockSpec(memory_space=pl.ANY)
    args = [normed, gs, regions[:, None, :], w_qkv, w_proj, *carry, *into]
    alias = {}
    if carry:
        alias = {5: 2, 6: 3}
    if into:
        alias |= {7: 0, 8: 1}
    return pl.pallas_call(
        functools.partial(attention_kernel, first=first, carried=carried, into=bool(into)),
        grid=(number, windows),
        in_specs=[
            whole(windows, count, width),
            whole(windows, count, width),
            whole(windows, 1, count),
            rows3,
            cols1,
        ]
        + ([rows3, cols1] if carry else [])
        + ([anyw, anyw] if into else []),
        out_specs=[
            pl.BlockSpec((1, count, wide), lambda p, w: (w, 0, p + first)),
            pl.BlockSpec((1, 3, count, wide), lambda p, w: (w, 0, 0, p + first)),
            rows3,
            cols1,
        ],
        out_shape=(
            jax.ShapeDtypeStruct((windows, count, width), BF16),
            jax.ShapeDtypeStruct((windows, 3, count, width), BF16),
            jax.ShapeDtypeStruct((3, width, width), F32),
            jax.ShapeDtypeStruct((width, width), F32),
        ),
        input_output_aliases=alias,
        cost_estimate=pl.CostEstimate(
            flops=windows * count * number * wide * (16 * width + 12 * count), transcendentals=0,
            bytes_accessed=windows * count * number * wide * 12),
    )(*args)


def back(att, gqkv, normed, inv, w_ref, wp_ref, scr):
    shape = scr.shape[1:]
    branch = nt(att[0], wp_ref[...])
    scr[0] = branch.astype(BF16).astype(F32).reshape(shape)
    grad_normed = nn(gqkv[0, 0], w_ref[0]) + nn(gqkv[0, 1], w_ref[1]) + nn(gqkv[0, 2], w_ref[2])
    normal = normed[0].astype(F32)
    mean = jnp.mean(grad_normed, axis=-1, keepdims=True)
    along = jnp.mean(grad_normed * normal, axis=-1, keepdims=True)
    pre = inv[0][:, :1] * (grad_normed - mean - normal * along)
    scr[1] = pre.astype(BF16).astype(F32).reshape(shape)


def finish_low_kernel(*refs):
    ins, (w_ref, wp_ref, f_ref, g_ref) = refs[:8], refs[8:12]
    out_ref, gout_ref, east_ref, low_ref, corner_ref, first, second = refs[12:]
    back(*ins[:4], w_ref, wp_ref, first)
    back(*ins[4:], w_ref, wp_ref, second)
    n = f_ref.shape[0]

    @pl.when(pl.program_id(0) == 0)
    def _():
        @pl.loop(0, n, unroll=3)
        def _(p):
            for i, (x, o) in enumerate(((f_ref, out_ref), (g_ref, gout_ref))):
                add, strip = unpick(first[i, p], second[i, p])
                o[p] = (x[p].astype(F32) + add).astype(BF16)
                east_ref[i, p] = strip.astype(BF16)

    @pl.when(pl.program_id(0) == 1)
    def _():
        @pl.loop(0, n, unroll=3)
        def _(p):
            for i in range(2):
                add, strip = unpick(first[i, p], second[i, p])
                low_ref[i, p] = add.astype(BF16)
                corner_ref[i, p] = strip.astype(BF16)


def finish_east_kernel(att, gqkv, normed, inv, w_ref, wp_ref, east_ref, kept_ref, second):
    back(att, gqkv, normed, inv, w_ref, wp_ref, second)
    kept_ref[...] = second[...].astype(BF16)

    @pl.loop(0, second.shape[1], unroll=3)
    def _(p):
        for i in range(2):
            _, strip = unpick(second[i, p], second[i, p])
            east_ref[i, p] = strip.astype(BF16)


def finish_top_kernel(att, gqkv, normed, inv, kept_ref, w_ref, wp_ref, f_ref, g_ref, any0, any1,
                      out_ref, gout_ref, first):
    back(att, gqkv, normed, inv, w_ref, wp_ref, first)

    @pl.loop(0, f_ref.shape[0], unroll=3)
    def _(p):
        for i, (x, o) in enumerate(((f_ref, out_ref), (g_ref, gout_ref))):
            add, _ = unpick(first[i, p], kept_ref[i, p].astype(F32))
            o[p] = (x[p].astype(F32) + add).astype(BF16)


def finish_call(kernel, sets, width, skip, w_qkv, w_proj, more, specs, outs, out_specs, alias,
                ahead=()):
    part = skip * 3 * SUB
    whole = lambda *shape: pl.BlockSpec(shape, lambda s: (0,) * len(shape))
    ins, args = [], []
    for at, arrays in sets:
        ins += [
            pl.BlockSpec((1, part, width), lambda s, at=at: (at, s, 0)),
            pl.BlockSpec((1, 3, part, width), lambda s, at=at: (at, 0, s, 0)),
            pl.BlockSpec((1, part, width), lambda s, at=at: (at, s, 0)),
            pl.BlockSpec((1, part, LANES), lambda s, at=at: (at, s, 0)),
        ]
        args += arrays
    args += [x for x, _ in ahead] + [w_qkv, w_proj] + list(more)
    ins += [x for _, x in ahead] + [whole(3, width, width), whole(width, width)] + list(specs)
    return pl.pallas_call(
        kernel,
        grid=(2,),
        in_specs=ins,
        out_specs=out_specs,
        out_shape=tuple(jax.ShapeDtypeStruct(shape, BF16) for shape in outs),
        scratch_shapes=[pltpu.VMEM((2, skip, 3 * SUB, width), F32)] * len(sets),
        input_output_aliases={len(args) - back_at: at for back_at, at in alias.items()},
        cost_estimate=pl.CostEstimate(
            flops=2 * len(sets) * part * 8 * width * width, transcendentals=0,
            bytes_accessed=4 * len(sets) * part * width * 16),
    )(*args)


def finish_low(first, second, w_qkv, w_proj, fields, grads, skip):
    pairs, _, width = fields.shape
    last = pairs // skip - 1
    own = pl.BlockSpec((skip, 48, width), lambda s: (last, 0, 0))
    whole = lambda *shape: pl.BlockSpec(shape, lambda s: (0,) * len(shape))
    strips = [(2, skip, 16, width), (2, skip, 48, width), (2, skip, 16, width)]
    return finish_call(
        finish_low_kernel, [(0, first), (1, second)], width, skip, w_qkv, w_proj,
        (fields, grads), (own, own), [(pairs, 48, width)] * 2 + strips,
        [own, own] + [whole(*shape) for shape in strips], {},
    )


def finish_east(arrays, w_qkv, w_proj, skip):
    width = w_proj.shape[0]
    rows = lambda n: pl.BlockSpec((2, skip, n, width), lambda s: (0, s, 0, 0))
    return finish_call(
        finish_east_kernel, [(0, arrays)], width, skip, w_qkv, w_proj, (), (),
        [(2, 2 * skip, 16, width), (2, 2 * skip, 3 * SUB, width)],
        [rows(16), rows(3 * SUB)], {},
    )


def finish_top(arrays, kept, w_qkv, w_proj, fields, grads, skip, into):
    pairs, _, width = fields.shape
    own = pl.BlockSpec((skip, 48, width), lambda s: (s + 1, 0, 0))
    anyw = pl.BlockSpec(memory_space=pl.ANY)
    rows = pl.BlockSpec((2, skip, 3 * SUB, width), lambda s: (0, s, 0, 0))
    return finish_call(
        finish_top_kernel, [(0, arrays)], width, skip, w_qkv, w_proj,
        (fields, grads, *into), (own, own, anyw, anyw), [(pairs, 48, width)] * 2,
        [own, own], {2: 0, 1: 1}, ahead=[(kept, rows)],
    )


def edge_kernel(f_ref, o_ref, r_ref, g_ref, q_ref, out_ref, gout_ref):
    s = lax.broadcasted_iota(jnp.int32, f_ref.shape, 1)
    for i, (f, o, out) in enumerate(((f_ref, o_ref, out_ref), (g_ref, q_ref, gout_ref))):
        total = f[...].astype(F32) + r_ref[i].astype(F32)
        out[...] = jnp.where(s < HALF, total, o[...].astype(F32)).astype(BF16)


def edge(fields, out, back, grads, gout, skip, first):
    _, _, width = fields.shape
    n = back.shape[1] // skip
    at = pl.BlockSpec((skip, SUB, width), lambda i: (i + first, 0, 0))
    strip = pl.BlockSpec((2, skip, SUB, width), lambda i: (0, i, 0, 0))
    return pl.pallas_call(
        edge_kernel,
        grid=(n,),
        in_specs=[at, at, strip, at, at],
        out_specs=[at, at],
        out_shape=(jax.ShapeDtypeStruct(out.shape, BF16),) * 2,
        input_output_aliases={1: 0, 4: 1},
        name="edge",
    )(fields, out, back, grads, gout)


def rim_kernel(f_ref, low_ref, c_ref, g_ref, out_any, gout_any, out_ref, gout_ref):
    for i, (f, out) in enumerate(((f_ref, out_ref), (g_ref, gout_ref))):
        back = low_ref[i].astype(F32)
        corner = c_ref[i].astype(F32)
        s = lax.broadcasted_iota(jnp.int32, corner.shape, 1)
        head = jnp.where(s < HALF, corner, back[:, :SUB])
        back = jnp.concatenate([head, back[:, SUB:]], axis=1)
        out[...] = (f[...].astype(F32) + back).astype(BF16)


def rim(fields, low, corner, grads, out, gout):
    _, skip, cols, width = low.shape
    at = pl.BlockSpec((skip, cols, width), lambda i: (0, 0, 0))
    whole = lambda *shape: pl.BlockSpec(shape, lambda i: (0,) * len(shape))
    anyw = pl.BlockSpec(memory_space=pl.ANY)
    return pl.pallas_call(
        rim_kernel,
        grid=(1,),
        in_specs=[at, whole(2, skip, cols, width), whole(2, skip, SUB, width), at, anyw, anyw],
        out_specs=[at, at],
        out_shape=(jax.ShapeDtypeStruct(out.shape, BF16),) * 2,
        input_output_aliases={4: 0, 5: 1},
        name="rim",
    )(fields, low, corner, grads, out, gout)


def linear(lon, lat, lats):
    return lon * lats + lat


def shift_by(block, step_lon, step_lat):
    lons, lats = lax.axis_size("lon"), lax.axis_size("lat")
    route = [
        (linear((i + step_lon) % lons, (j + step_lat) % lats, lats), linear(i, j, lats))
        for i in range(lons)
        for j in range(lats)
    ]
    return lax.ppermute(block, AXES, route)


def stages():
    lons, lats = lax.axis_size("lon"), lax.axis_size("lat")
    lat_bits = [1 << i for i in range(lats.bit_length() - 1)]
    lon_bits = [lats << i for i in range(lons.bit_length() - 1)]
    assert lats == 1 << len(lat_bits) and lons == 1 << len(lon_bits)
    far = lon_bits[1:]
    groups = [lat_bits[i : i + 2] for i in range(0, len(lat_bits), 2)]
    groups += [far[i : i + 2] for i in range(0, len(far), 2)]
    groups += [lon_bits[:1]]
    return groups, sorted(lat_bits + lon_bits)[::-1]


def swap(block, bit):
    total = lax.axis_size("lon") * lax.axis_size("lat")
    return lax.ppermute(block, AXES, [(i, i ^ bit) for i in range(total)])


def join(mine, other, bit, bits, place):
    high = (place & bit) != 0
    axis = bits.index(bit)
    return jnp.where(
        high,
        jnp.concatenate([other, mine], axis=axis),
        jnp.concatenate([mine, other], axis=axis),
    )


def gather_stage(held, group, bits, place):
    if len(group) == 1:
        return join(held, swap(held, group[0]), group[0], bits, place)
    b1, b2 = group
    o1, o2, o3 = swap(held, b1), swap(held, b2), swap(held, b1 | b2)
    return join(join(held, o1, b1, bits, place), join(o2, o3, b1, bits, place), b2, bits, place)


def part_of(held, bit, bits, index):
    return lax.dynamic_index_in_dim(held, index, bits.index(bit), keepdims=True)


def scatter_stage(held, group, bits, place):
    here = [jnp.where((place & bit) != 0, 1, 0) for bit in group]
    total = held
    for bit, i in zip(group, here):
        total = part_of(total, bit, bits, i)
    total = total.astype(F32)
    for flips in range(1, 1 << len(group)):
        send, mask = held, 0
        for k, (bit, i) in enumerate(zip(group, here)):
            flip = (flips >> k) & 1
            send = part_of(send, bit, bits, 1 - i if flip else i)
            mask |= bit * flip
        total = total + swap(send.astype(BF16), mask).astype(F32)
    return total


def lines_of(grid):
    rows, cols, levels, width = grid.shape
    return grid.transpose(0, 2, 1, 3).reshape(rows * levels, cols, width)


def grid_of(lines, levels):
    count, cols, width = lines.shape
    return lines.reshape(count // levels, levels, cols, width).transpose(0, 2, 1, 3)


def paired(lines):
    *lead, count, cols, width = lines.shape
    return lines.reshape(*lead, count // 2, 2 * cols, width)


def unpaired(pairs):
    *lead, count, cols, width = pairs.shape
    return pairs.reshape(*lead, count * 2, cols // 2, width)


def block(fields, region_ids, w_qkv, w_proj, grad_output):
    rows, cols, levels, width = fields.shape
    skip = HALF * levels // 2
    devices = lax.axis_size("lon") * lax.axis_size("lat")
    factor = float(rows * cols * levels * devices) ** (-0.5)
    place = lax.axis_index(AXES)
    groups, bits = stages()
    share = w_qkv.shape[0]
    f_lines, g_lines = lines_of(fields), lines_of(grad_output)
    f_pairs, g_pairs = paired(f_lines), paired(g_lines)
    held = jnp.concatenate([w_qkv, w_proj], axis=0)
    held = held.reshape((1,) * len(bits) + held.shape)
    for group in groups[:-1]:
        held = gather_stage(held, group, bits, place)
    bit = groups[-1][0]
    other = swap(held, bit)
    w3 = join(held[..., :share, :], other[..., :share, :], bit, bits, place).reshape(3, width, width)
    p_all = join(held[..., share:, :], other[..., share:, :], bit, bits, place).reshape(width, width)
    low, corner, east = pack(f_lines, g_lines, 2 * skip)
    low = shift_by(low, 0, 1)
    east = shift_by(east, 1, 0)
    corner = shift_by(corner, 1, 1)
    low, east, corner = paired(low), paired(east), paired(corner)
    regions = token_regions(region_ids, levels)
    n00, i00, g00 = assemble_own(f_pairs, g_pairs, skip)
    n10, i10, g10 = assemble_below(f_pairs, g_pairs, low, skip)
    a10, q10, *carry = attention(n10, g10, regions[1, :1], w3, p_all)
    n1, i1, g1 = assemble_second(f_pairs, g_pairs, east, low, corner, skip)
    many = width // (GROUP * LANES)
    a1, q1, *carry = attention(n1, g1, regions[:, 1], w3, p_all, carry, many)
    out, gout, r_east1, r_low, r_corner = finish_low(
        (a10, q10, n10, i10), (a1, q1, n1, i1), w3, p_all, f_pairs, g_pairs, skip
    )
    r_low = shift_by(unpaired(r_low), 0, -1)
    r_corner = shift_by(unpaired(r_corner), -1, -1)
    r_east0, kept = finish_east((a1, q1, n1, i1), w3, p_all, skip)
    r_east1 = shift_by(unpaired(r_east1), -1, 0)
    r_east0 = shift_by(unpaired(r_east0), -1, 0)
    a00, q00, grad_w, grad_p = attention(n00, g00, regions[0, :1], w3, p_all, carry, many)
    grads = jnp.concatenate(
        [grad_w.reshape(devices, -1, width), grad_p.reshape(devices, -1, width)], axis=1
    )
    grads = grads.reshape((2,) * len(bits) + grads.shape[1:])
    for group in groups[::-1]:
        grads = scatter_stage(grads, group, bits, place)
    grads = grads.reshape(-1, width) * factor
    out, gout = finish_top(
        (a00, q00, n00, i00), kept, w3, p_all, f_pairs, g_pairs, skip, (out, gout)
    )
    out, gout = unpaired(out), unpaired(gout)
    out, gout = rim(f_lines, r_low, r_corner, g_lines, out, gout)
    out, gout = edge(f_lines, out, r_east1, g_lines, gout, 2 * skip, rows * levels // (2 * skip) - 1)
    out, gout = edge(f_lines, out, r_east0, g_lines, gout, 2 * skip, 1)
    return (grid_of(out, levels), grid_of(gout, levels), grads[:share], grads[share:])


def solution(mesh):
    return jax.shard_map(
        block,
        mesh=mesh,
        in_specs=(
            P("lat", "lon", None, None),
            P("lat"),
            P(AXES, None),
            P(AXES, None),
            P("lat", "lon", None, None),
        ),
        out_specs=(
            P("lat", "lon", None, None),
            P("lat", "lon", None, None),
            P(AXES, None),
            P(AXES, None),
        ),
        check_vma=False,
    )
```

time: 182 us -> 187 us (1.027)
  waiting for transfers between devices: 35.5 us -> 45.3 us
  Pallas kernels: 88.4 us -> 95.3 us
  starting transfers between devices: 30.5 us -> 24.6 us
  other arithmetic: 9.35 us -> 6.45 us
  local copies, waits for them, and re-layouts: 16.4 us -> 13.9 us
    pallas_call x8 -> x10, Pallas kernels: 81.6 us -> 88.5 us  [the longest x3 55.8 us: attention(): pl.pallas_call(functools.partial(attention_kernel, first=first, carried=c...]
    ppermute x7, starting transfers between devices: 10.7 us -> 3.94 us  [shift_by(): return lax.ppermute(block, AXES, route)]
    ppermute x7, waiting for transfers between devices: 10.2 us -> 15.9 us  [shift_by(): return lax.ppermute(block, AXES, route)]
    another operation x7 -> x0, local copies, waits for them, and re-layouts: 5.5 us -> none  [the longest x3 2.69 us: attention(): regions[:, :, None]]
    ppermute x14, waiting for transfers between devices: 25.4 us -> 29.4 us  [swap(): return lax.ppermute(block, AXES, [(i, i ^ bit) for i in range(total)])]
    another operation x3 -> x0, other arithmetic: 2.71 us -> none  [the longest x1 0.99 us: block(): low = shift_by(both([f_lines[:2 * skip], g_lines[:2 * skip]]), 0, 1)]
    convert_element_type x0 -> x1, other arithmetic: none -> 2.69 us  [scatter_stage(): total = total + swap(send.astype(BF16), mask).astype(F32)]
    concatenate x4 -> x5, other arithmetic: 2.58 us -> 0.23 us  [join(): jnp.concatenate([other, mine], axis=axis)]
  transfers between devices with their start and end apart: 21 -> 21, of which waited for: 7 -> 10; matrix products, arithmetic and copies ran while one was open for 9% -> 3% of each run, Pallas kernels for 18% -> 21%
where the time goes in v3:
time: 187 us; the launch traced here: 186 us
  Pallas kernels  95.3 us (51%)
  waiting for transfers between devices  45.3 us (24%)
  starting transfers between devices  24.6 us (13%)
  local copies, waits for them, and re-layouts  13.9 us (7%)
  other arithmetic  6.45 us (3%)
    pallas_call x3, Pallas kernels, attention(): pl.pallas_call(functools.partial(attention_kernel, first=first, carried=c...  55.8 us
    ppermute x14, waiting for transfers between devices, swap(): return lax.ppermute(block, AXES, [(i, i ^ bit) for i in range(total)])  29.4 us
    ppermute x14, starting transfers between devices, swap(): return lax.ppermute(block, AXES, [(i, i ^ bit) for i in range(total)])  20.6 us
    pallas_call x3, Pallas kernels, finish_call(): pl.pallas_call(kernel, grid=(2,), in_specs=ins, out_specs=out_specs, out_...  17.5 us
    ppermute x7, waiting for transfers between devices, shift_by(): return lax.ppermute(block, AXES, route)  15.9 us
    pallas_call x3, Pallas kernels, assembled(): pl.pallas_call(kernel, grid=(2 * windows,), in_specs=specs, out_specs=[ou...  12.4 us
    unnamed x21, local copies, waits for them, and re-layouts  5.35 us
    pallas_call x2, Pallas kernels, edge(): pl.pallas_call(edge_kernel, grid=(n,), in_specs=[at, at, strip, at, at],...  4.24 us
  transfers between devices with their start and end apart: 21, of which 10 were waited for; matrix products, arithmetic and copies ran while one was open for 3% of the time, Pallas kernels for 21%

profile of v3, /device:TPU:0, one launch (start us, length us, event | category | flops | bytes accessed | tf_op | source)
XLA Modules:
  0.0 186.5 jit_solution(15137669385493200893)
XLA Ops:
  2.2 5.1 %collective-permute-start.1 = (bf16[1,1,1,1,1,64,512]{6,5,4,3,2,1,0:T(8,128)(2,1)S(1)}, bf16[1,1,1,1,1,64,512]{6,5,4,3,2,1,0:T(8,128)(2,1)S(1)}, u32[]{:S(2)}, u32[]{:S(2)}) collective-permute-start(bf16[1,1,1,1,1,64,512]{6,5,4,3,2,1,0:T(8,128)(2,1)S(1)} %bitcast.127), channel_id=1, source_target_pairs={{0,3},{1,2},{2,1},{3,0},{4,7},{5,6},{6,5},{7,4},{8,11},{9,10},{10,... | collective-permute-start | bytes 196616 | tf_op jit(solution)/shard_map/ppermute | solution.py:548
  7.8 1.9 %collective-permute-done.1 = bf16[1,1,1,1,1,64,512]{6,5,4,3,2,1,0:T(8,128)(2,1)S(1)} collective-permute-done((bf16[1,1,1,1,1,64,512]{6,5,4,3,2,1,0:T(8,128)(2,1)S(1)}, bf16[1,1,1,1,1,64,512]{6,5,4,3,2,1,0:T(8,128)(2,1)S(1)}, u32[]{:S(2)}, u32[]{:S(2)}) %collective-permute-start.1) | collective-permute-done | bytes 65568 | tf_op jit(solution)/shard_map/ppermute | solution.py:548
  9.7 3.1 %collective-permute-done.2 = bf16[1,1,1,1,1,64,512]{6,5,4,3,2,1,0:T(8,128)(2,1)S(1)} collective-permute-done((bf16[1,1,1,1,1,64,512]{6,5,4,3,2,1,0:T(8,128)(2,1)S(1)}, bf16[1,1,1,1,1,64,512]{6,5,4,3,2,1,0:T(8,128)(2,1)S(1)}, u32[]{:S(2)}, u32[]{:S(2)}) %collective-permute-start.2) | collective-permute-done | bytes 65568 | tf_op jit(solution)/shard_map/ppermute | solution.py:548
  12.9 2.5 %collective-permute-start.4 = (bf16[1,1,1,2,2,64,512]{6,5,4,3,2,1,0:T(8,128)(2,1)S(1)}, bf16[1,1,1,2,2,64,512]{6,5,4,3,2,1,0:T(8,128)(2,1)S(1)}, u32[]{:S(2)}, u32[]{:S(2)}) collective-permute-start(bf16[1,1,1,2,2,64,512]{6,5,4,3,2,1,0:T(8,128)(2,1)S(1)} %maximum_select_fusion.5), channel_id=1, source_target_pairs={{0,24},{1,25},{2,26},{3,27},{4,28},{5,29},{6,30},{7,31},{8,16},{9,... | collective-permute-start | bytes 786440 | tf_op jit(solution)/shard_map/ppermute | solution.py:548
  16.5 6.6 %collective-permute-done.4 = bf16[1,1,1,2,2,64,512]{6,5,4,3,2,1,0:T(8,128)(2,1)S(1)} collective-permute-done((bf16[1,1,1,2,2,64,512]{6,5,4,3,2,1,0:T(8,128)(2,1)S(1)}, bf16[1,1,1,2,2,64,512]{6,5,4,3,2,1,0:T(8,128)(2,1)S(1)}, u32[]{:S(2)}, u32[]{:S(2)}) %collective-permute-start.4) | collective-permute-done | bytes 262176 | tf_op jit(solution)/shard_map/ppermute | solution.py:548
  23.1 4.3 %collective-permute-done.5 = bf16[1,1,1,2,2,64,512]{6,5,4,3,2,1,0:T(8,128)(2,1)S(1)} collective-permute-done((bf16[1,1,1,2,2,64,512]{6,5,4,3,2,1,0:T(8,128)(2,1)S(1)}, bf16[1,1,1,2,2,64,512]{6,5,4,3,2,1,0:T(8,128)(2,1)S(1)}, u32[]{:S(2)}, u32[]{:S(2)}) %collective-permute-start.5) | collective-permute-done | bytes 262176 | tf_op jit(solution)/shard_map/ppermute | solution.py:548
  28.0 2.8 %pack.1 = (bf16[2,18,24,512]{3,2,1,0:T(8,128)(2,1)}, bf16[2,18,8,512]{3,2,1,0:T(8,128)(2,1)}, bf16[2,54,8,512]{3,2,1,0:T(8,128)(2,1)}) custom-call(bf16[72,24,512]{2,1,0:T(8,128)(2,1)} %bitcast.70, bf16[72,24,512]{2,1,0:T(8,128)(2,1)} %bitcast.71, bf16[72,24,512]{2,1,0:T(8,128)(2,1)} %bitcast.80, bf16[72,24,512]{2,1,0:T(8,128)(2,1)} %bitcast.81), custom_call_target="tpu_custom_call" | custom-call | tf_op jit(solution)/shard_map/pack/pallas_call | solution.py:102
  30.8 1.4 collective-permute-start
  32.2 1.6 collective-permute-start.8
  35.3 3.2 %shard_map.89 = (bf16[1,18,24,512]{3,2,1,0:T(8,128)(2,1)}, f32[1,18,24,128]{3,2,1,0:T(8,128)}, bf16[1,18,24,512]{3,2,1,0:T(8,128)(2,1)}) custom-call(bf16[36,48,512]{2,1,0:T(8,128)(2,1)} %bitcast.72, bf16[36,48,512]{2,1,0:T(8,128)(2,1)} %bitcast.82), custom_call_target="tpu_custom_call" | custom-call | flops 11059200 | bytes 1769472 | tf_op jit(solution)/shard_map/pallas_call | solution.py:176
  39.2 14.3 %collective-permute-done = bf16[2,18,24,512]{3,2,1,0:T(8,128)(2,1)S(1)} collective-permute-done((bf16[2,18,24,512]{3,2,1,0:T(8,128)(2,1)}, bf16[2,18,24,512]{3,2,1,0:T(8,128)(2,1)S(1)}, u32[]{:S(2)}, u32[]{:S(2)}) %collective-permute-start) | collective-permute-done | bytes 884768 | tf_op jit(solution)/shard_map/ppermute | solution.py:531
  54.4 3.5 %shard_map.84 = (bf16[1,18,24,512]{3,2,1,0:T(8,128)(2,1)}, f32[1,18,24,128]{3,2,1,0:T(8,128)}, bf16[1,18,24,512]{3,2,1,0:T(8,128)(2,1)}) custom-call(bf16[36,48,512]{2,1,0:T(8,128)(2,1)} %bitcast.73, bf16[36,48,512]{2,1,0:T(8,128)(2,1)} %bitcast.83, bf16[2,9,48,512]{3,2,1,0:T(8,128)(2,1)} %bitcast.113), custom_call_target="tpu_custom_call" | custom-call | flops 11059200 | bytes 1769472 | tf_op jit(solution)/shard_map/pallas_call | solution.py:176
  59.6 5.7 %shard_map.86 = (bf16[2,18,24,512]{3,2,1,0:T(8,128)(2,1)}, f32[2,18,24,128]{3,2,1,0:T(8,128)}, bf16[2,18,24,512]{3,2,1,0:T(8,128)(2,1)}) custom-call(bf16[36,48,512]{2,1,0:T(8,128)(2,1)} %bitcast.74, bf16[36,48,512]{2,1,0:T(8,128)(2,1)} %bitcast.84, bf16[2,27,16,512]{3,2,1,0:T(8,128)(2,1)} %bitcast.31.east_ref, bf16[2,9,48,512]{3,2,1,0:T(8,128)(2,1)} %bitcast.114, ...), custom_call_target="tpu_custom_call" | custom-call | flops 22118400 | bytes 3538944 | tf_op jit(solution)/shard_map/pallas_call | solution.py:176
  68.7 1.3 copy.27
  70.0 14.1 %shard_map.85 = (bf16[1,432,512]{2,1,0:T(8,128)(2,1)}, bf16[1,3,432,512]{3,2,1,0:T(8,128)(2,1)}, f32[3,512,512]{2,1,0:T(8,128)}, f32[512,512]{1,0:T(8,128)}) custom-call(bf16[1,432,512]{2,1,0:T(8,128)(2,1)} %bitcast.117, bf16[1,432,512]{2,1,0:T(8,128)(2,1)} %bitcast.138, s32[1,1,432]{2,1,0:T(1,128)} %get-tuple-element.95.refs_2_, ...), custom_call_target="tpu_custom_call" | custom-call | flops 2958557184 | bytes 2654208 | tf_op jit(solution)/shard_map/pallas_call | solution.py:316
  84.1 26.6 %shard_map.87 = (bf16[2,432,512]{2,1,0:T(8,128)(2,1)}, bf16[2,3,432,512]{3,2,1,0:T(8,128)(2,1)}, f32[3,512,512]{2,1,0:T(8,128)}, f32[512,512]{1,0:T(8,128)}) custom-call(bf16[2,432,512]{2,1,0:T(8,128)(2,1)} %bitcast.110, bf16[2,432,512]{2,1,0:T(8,128)(2,1)} %bitcast.135, s32[2,1,432]{2,1,0:T(1,128)} %slice.65.refs_2_, ...), custom_call_target="tpu_custom_call", output_to_operand_aliasing={{2}: (5, {}), {3}: (6, {})} | custom-call | flops 5917114368 | bytes 5308416 | tf_op jit(solution)/shard_map/pallas_call | solution.py:316
  110.7 15.1 %shard_map.90 = (bf16[1,432,512]{2,1,0:T(8,128)(2,1)}, bf16[1,3,432,512]{3,2,1,0:T(8,128)(2,1)}, f32[3,512,512]{2,1,0:T(8,128)}, f32[512,512]{1,0:T(8,128)}) custom-call(bf16[1,432,512]{2,1,0:T(8,128)(2,1)} %bitcast.119, bf16[1,432,512]{2,1,0:T(8,128)(2,1)} %bitcast.137, ...), custom_call_target="tpu_custom_call", output_to_operand_aliasing={{2}: (5, {}), {3}: (6, {})} | custom-call | flops 2958557184 | bytes 2654208 | tf_op jit(solution)/shard_map/pallas_call | solution.py:316
  125.8 2.7 %fusion.1 = bf16[2,2,1,2,2,64,512]{6,5,4,3,2,1,0:T(8,128)(2,1)} fusion(s32[]{:T(128)S(6)} %select_n.340, f32[2,2,2,2,2,48,512]{6,5,4,3,2,1,0:T(8,128)} %bitcast.100, f32[2,2,2,2,2,16,512]{6,5,4,3,2,1,0:T(8,128)} %bitcast.108), kind=kLoop, calls=%fused_computation.5 | loop fusion | flops 2097152 | bytes 5242884 | tf_op jit(solution)/shard_map/convert_element_type | solution.py:585
  128.5 1.2 collective-permute-start.14
  129.8 7.4 %shard_map.88 = (bf16[36,48,512]{2,1,0:T(8,128)(2,1)}, bf16[36,48,512]{2,1,0:T(8,128)(2,1)}, bf16[2,9,16,512]{3,2,1,0:T(8,128)(2,1)}, bf16[2,9,48,512]{3,2,1,0:T(8,128)(2,1)}, bf16[2,9,16,512]{3,2,1,0:T(8,128)(2,1)}) custom-call(bf16[1,432,512]{2,1,0:T(8,128)(2,1)} %get-tuple-element.46.refs_0_, bf16[1,3,432,512]{3,2,1,0:T(8,128)(2,1)} %get-tuple-element.47.refs_1_, ...), custom_call_target="tpu_custom_call" | custom-call | flops 1811939328 | bytes 14155776 | tf_op jit(solution)/shard_map/pallas_call | solution.py:422
  137.2 1.8 fusion.3
  139.0 1.3 copy-done.1
  140.5 1.5 collective-permute-start.15
  142.5 1.5 collective-permute-start.17
  144.0 4.6 %shard_map.91 = (bf16[2,18,16,512]{3,2,1,0:T(8,128)(2,1)}, bf16[2,18,24,512]{3,2,1,0:T(8,128)(2,1)}) custom-call(bf16[2,432,512]{2,1,0:T(8,128)(2,1)} %get-tuple-element.55.refs_4_.att, bf16[2,3,432,512]{3,2,1,0:T(8,128)(2,1)} %get-tuple-element.56.refs_5_.gqkv, bf16[2,432,512]{2,1,0:T(8,128)(2,1)} %bitcast.112, f32[2,432,128]{2,1,0:T(8,128)} %bitcast.116, ...), custom_call_target="tpu_custom_call" | custom-call | flops 905969664 | bytes 7077888 | tf_op jit(solution)/shard_map/pallas_call | solution.py:422
  150.6 12.4 %collective-permute-done.16 = bf16[1,1,1,2,2,64,512]{6,5,4,3,2,1,0:T(8,128)(2,1)S(1)} collective-permute-done((bf16[1,1,1,2,2,64,512]{6,5,4,3,2,1,0:T(8,128)(2,1)S(1)}, bf16[1,1,1,2,2,64,512]{6,5,4,3,2,1,0:T(8,128)(2,1)S(1)}, u32[]{:S(2)}, u32[]{:S(2)}) %collective-permute-start.16) | collective-permute-done | bytes 262176 | tf_op jit(solution)/shard_map/ppermute | solution.py:548
  164.2 2.3 %collective-permute-start.18 = (bf16[1,1,1,1,1,64,512]{6,5,4,3,2,1,0:T(8,128)(2,1)S(1)}, bf16[1,1,1,1,1,64,512]{6,5,4,3,2,1,0:T(8,128)(2,1)S(1)}, u32[]{:S(2)}, u32[]{:S(2)}) collective-permute-start(bf16[1,1,1,1,1,64,512]{6,5,4,3,2,1,0:T(8,128)(2,1)S(1)} %get-tuple-element.87), channel_id=1, source_target_pairs={{0,1},{1,0},{2,3},{3,2},{4,5},{5,4},{6,7},{7,6},{8,9},{9,8},{10,11... | collective-permute-start | bytes 196616 | tf_op jit(solution)/shard_map/ppermute | solution.py:548
  167.1 3.3 %collective-permute-start.19 = (bf16[1,1,1,1,1,64,512]{6,5,4,3,2,1,0:T(8,128)(2,1)S(1)}, bf16[1,1,1,1,1,64,512]{6,5,4,3,2,1,0:T(8,128)(2,1)S(1)}, u32[]{:S(2)}, u32[]{:S(2)}) collective-permute-start(bf16[1,1,1,1,1,64,512]{6,5,4,3,2,1,0:T(8,128)(2,1)S(1)} %get-tuple-element.89), channel_id=1, source_target_pairs={{0,2},{1,3},{2,0},{3,1},{4,6},{5,7},{6,4},{7,5},{8,10},{9,11},{10,... | collective-permute-start | bytes 196616 | tf_op jit(solution)/shard_map/ppermute | solution.py:548
  171.4 5.5 %shard_map.92 = (bf16[36,48,512]{2,1,0:T(8,128)(2,1)}, bf16[36,48,512]{2,1,0:T(8,128)(2,1)}) custom-call(bf16[1,432,512]{2,1,0:T(8,128)(2,1)} %get-tuple-element.64.att, bf16[1,3,432,512]{3,2,1,0:T(8,128)(2,1)} %get-tuple-element.65.gqkv, bf16[1,432,512]{2,1,0:T(8,128)(2,1)} %bitcast.120, ...), custom_call_target="tpu_custom_call", output_to_operand_aliasing={{0}: (9, {}), {1}: (10, {})} | custom-call | flops 905969664 | bytes 7077888 | tf_op jit(solution)/shard_map/pallas_call | solution.py:422
  176.8 2.5 %rim.1 = (bf16[72,24,512]{2,1,0:T(8,128)(2,1)}, bf16[72,24,512]{2,1,0:T(8,128)(2,1)}) custom-call(bf16[72,24,512]{2,1,0:T(8,128)(2,1)} %bitcast.77, bf16[2,18,24,512]{3,2,1,0:T(8,128)(2,1)} %collective-permute-done.10.low_ref, bf16[2,18,8,512]{3,2,1,0:T(8,128)(2,1)} %copy-done.6, ...), custom_call_target="tpu_custom_call", output_to_operand_aliasing={{0}: (4, {}), {1}: (5, {})} | custom-call | tf_op jit(solution)/shard_map/rim/pallas_call | solution.py:509
  180.1 2.0 %edge.2 = (bf16[72,24,512]{2,1,0:T(8,128)(2,1)}, bf16[72,24,512]{2,1,0:T(8,128)(2,1)}) custom-call(bf16[72,24,512]{2,1,0:T(8,128)(2,1)} %bitcast.78, bf16[72,24,512]{2,1,0:T(8,128)(2,1)} %get-tuple-element.72.o_ref, bf16[2,18,8,512]{3,2,1,0:T(8,128)(2,1)} %copy-done.5, bf16[72,24,512]{2,1,0:T(8,128)(2,1)} %bitcast.88, ...), custom_call_target="tpu_custom_call", output_to_operand_aliasing={{0}: (1, {}), {1}: (4, {})} | custom-call | tf_op jit(solution)/shard_map/edge/pallas_call | solution.py:483
  182.9 2.3 %edge.3 = (bf16[72,24,512]{2,1,0:T(8,128)(2,1)}, bf16[72,24,512]{2,1,0:T(8,128)(2,1)}) custom-call(bf16[72,24,512]{2,1,0:T(8,128)(2,1)} %bitcast.79, bf16[72,24,512]{2,1,0:T(8,128)(2,1)} %get-tuple-element.75.o_ref, bf16[2,36,8,512]{3,2,1,0:T(8,128)(2,1)} %copy-done.3, bf16[72,24,512]{2,1,0:T(8,128)(2,1)} %bitcast.89, ...), custom_call_target="tpu_custom_call", output_to_operand_aliasing={{0}: (1, {}), {1}: (4, {})} | custom-call | tf_op jit(solution)/shard_map/edge/pallas_call | solution.py:483
  (84 shorter events, 20.1 us)
Async XLA Ops:
  2.2 7.6 %collective-permute-start.1 = (bf16[1,1,1,1,1,64,512]{6,5,4,3,2,1,0:T(8,128)(2,1)S(1)}, bf16[1,1,1,1,1,64,512]{6,5,4,3,2,1,0:T(8,128)(2,1)S(1)}, u32[]{:S(2)}, u32[]{:S(2)}) collective-permute-start(bf16[1,1,1,1,1,64,512]{6,5,4,3,2,1,0:T(8,128)(2,1)S(1)} %bitcast.127), channel_id=1, source_target_pairs={{0,3},{1,2},{2,1},{3,0},{4,7},{5,6},{6,5},{7,4},{8,11},{9,10},{10,... | collective-permute-start | bytes 196616 | tf_op jit(solution)/shard_map/ppermute | solution.py:548
  7.2 5.6 %collective-permute-start.2 = (bf16[1,1,1,1,1,64,512]{6,5,4,3,2,1,0:T(8,128)(2,1)S(1)}, bf16[1,1,1,1,1,64,512]{6,5,4,3,2,1,0:T(8,128)(2,1)S(1)}, u32[]{:S(2)}, u32[]{:S(2)}) collective-permute-start(bf16[1,1,1,1,1,64,512]{6,5,4,3,2,1,0:T(8,128)(2,1)S(1)} %bitcast.128), channel_id=1, source_target_pairs={{0,2},{1,3},{2,0},{3,1},{4,6},{5,7},{6,4},{7,5},{8,10},{9,11},{10,... | collective-permute-start | bytes 196616 | tf_op jit(solution)/shard_map/ppermute | solution.py:548
  7.2 5.6 %collective-permute-start.3 = (bf16[1,1,1,1,1,64,512]{6,5,4,3,2,1,0:T(8,128)(2,1)S(1)}, bf16[1,1,1,1,1,64,512]{6,5,4,3,2,1,0:T(8,128)(2,1)S(1)}, u32[]{:S(2)}, u32[]{:S(2)}) collective-permute-start(bf16[1,1,1,1,1,64,512]{6,5,4,3,2,1,0:T(8,128)(2,1)S(1)} %bitcast.129), channel_id=1, source_target_pairs={{0,1},{1,0},{2,3},{3,2},{4,5},{5,4},{6,7},{7,6},{8,9},{9,8},{10,11... | collective-permute-start | bytes 196616 | tf_op jit(solution)/shard_map/ppermute | solution.py:548
  12.9 10.2 %collective-permute-start.4 = (bf16[1,1,1,2,2,64,512]{6,5,4,3,2,1,0:T(8,128)(2,1)S(1)}, bf16[1,1,1,2,2,64,512]{6,5,4,3,2,1,0:T(8,128)(2,1)S(1)}, u32[]{:S(2)}, u32[]{:S(2)}) collective-permute-start(bf16[1,1,1,2,2,64,512]{6,5,4,3,2,1,0:T(8,128)(2,1)S(1)} %maximum_select_fusion.5), channel_id=1, source_target_pairs={{0,24},{1,25},{2,26},{3,27},{4,28},{5,29},{6,30},{7,31},{8,16},{9,... | collective-permute-start | bytes 786440 | tf_op jit(solution)/shard_map/ppermute | solution.py:548
  15.4 11.9 %collective-permute-start.5 = (bf16[1,1,1,2,2,64,512]{6,5,4,3,2,1,0:T(8,128)(2,1)S(1)}, bf16[1,1,1,2,2,64,512]{6,5,4,3,2,1,0:T(8,128)(2,1)S(1)}, u32[]{:S(2)}, u32[]{:S(2)}) collective-permute-start(bf16[1,1,1,2,2,64,512]{6,5,4,3,2,1,0:T(8,128)(2,1)S(1)} %maximum_select_fusion.5), channel_id=1, source_target_pairs={{0,16},{1,17},{2,18},{3,19},{4,20},{5,21},{6,22},{7,23},{8,24},{9,... | collective-permute-start | bytes 786440 | tf_op jit(solution)/shard_map/ppermute | solution.py:548
  16.0 11.7 %collective-permute-start.6 = (bf16[1,1,1,2,2,64,512]{6,5,4,3,2,1,0:T(8,128)(2,1)S(1)}, bf16[1,1,1,2,2,64,512]{6,5,4,3,2,1,0:T(8,128)(2,1)S(1)}, u32[]{:S(2)}, u32[]{:S(2)}) collective-permute-start(bf16[1,1,1,2,2,64,512]{6,5,4,3,2,1,0:T(8,128)(2,1)S(1)} %maximum_select_fusion.5), channel_id=1, source_target_pairs={{0,8},{1,9},{2,10},{3,11},{4,12},{5,13},{6,14},{7,15},{8,0},{9,1},... | collective-permute-start | bytes 786440 | tf_op jit(solution)/shard_map/ppermute | solution.py:548
  27.9 37.5 %collective-permute-start.7 = (bf16[2,2,1,2,2,64,512]{6,5,4,3,1,2,0:T(8,128)(2,1)S(1)}, bf16[2,2,1,2,2,64,512]{6,5,4,3,1,2,0:T(8,128)(2,1)}, u32[]{:S(2)}, u32[]{:S(2)}) collective-permute-start(bf16[2,2,1,2,2,64,512]{6,5,4,3,1,2,0:T(8,128)(2,1)S(1)} %maximum_select_fusion.1), channel_id=1, source_target_pairs={{0,4},{1,5},{2,6},{3,7},{4,0},{5,1},{6,2},{7,3},{8,12},{9,13},{10,... | collective-permute-start | bytes 3145736 | tf_op jit(solution)/shard_map/ppermute | solution.py:548
  28.0 5.8 %copy-start.7 = (s32[24]{0:T(128)S(1)}, s32[24]{0:T(128)}, u32[]{:S(2)}) copy-start(s32[24]{0:T(128)} %param.6) | copy-start | bytes 292
  30.8 22.7 %collective-permute-start = (bf16[2,18,24,512]{3,2,1,0:T(8,128)(2,1)}, bf16[2,18,24,512]{3,2,1,0:T(8,128)(2,1)S(1)}, u32[]{:S(2)}, u32[]{:S(2)}) collective-permute-start(bf16[2,18,24,512]{3,2,1,0:T(8,128)(2,1)} %get-tuple-element.43), channel_id=1, source_target_pairs={{1,0},{2,1},{3,2},{0,3},{5,4},{6,5},{7,6},{4,7},{9,8},{10,9},{11,1... | collective-permute-start | bytes 2654216 | tf_op jit(solution)/shard_map/ppermute | solution.py:531
  32.2 26.7 %collective-permute-start.8 = (bf16[2,54,8,512]{3,2,1,0:T(8,128)(2,1)}, bf16[2,54,8,512]{3,2,1,0:T(8,128)(2,1)}, u32[]{:S(2)}, u32[]{:S(2)}) collective-permute-start(bf16[2,54,8,512]{3,2,1,0:T(8,128)(2,1)} %get-tuple-element.49), channel_id=1, source_target_pairs={{4,0},{5,1},{6,2},{7,3},{8,4},{9,5},{10,6},{11,7},{12,8},{13,9},{1... | collective-permute-start | bytes 2654216 | tf_op jit(solution)/shard_map/ppermute | solution.py:531
  33.8 25.1 %collective-permute-start.9 = (bf16[2,18,8,512]{3,2,1,0:T(8,128)(2,1)}, bf16[2,18,8,512]{3,2,1,0:T(8,128)(2,1)S(1)}, u32[]{:S(2)}, u32[]{:S(2)}) collective-permute-start(bf16[2,18,8,512]{3,2,1,0:T(8,128)(2,1)} %get-tuple-element.50), channel_id=1, source_target_pairs={{5,0},{6,1},{7,2},{4,3},{9,4},{10,5},{11,6},{8,7},{13,8},{14,9},{1... | collective-permute-start | bytes 884744 | tf_op jit(solution)/shard_map/ppermute | solution.py:531
  53.5 0.9 copy-start.2
  58.9 0.7 copy-start.4
  128.5 8.7 %collective-permute-start.14 = (bf16[2,2,1,2,2,64,512]{6,5,4,3,2,1,0:T(8,128)(2,1)}, bf16[2,2,1,2,2,64,512]{6,5,4,3,2,1,0:T(8,128)(2,1)}, u32[]{:S(2)}, u32[]{:S(2)}) collective-permute-start(bf16[2,2,1,2,2,64,512]{6,5,4,3,2,1,0:T(8,128)(2,1)} %fusion.1), channel_id=1, source_target_pairs={{0,4},{1,5},{2,6},{3,7},{4,0},{5,1},{6,2},{7,3},{8,12},{9,13},{10,... | collective-permute-start | bytes 3145736 | tf_op jit(solution)/shard_map/ppermute | solution.py:548
  129.8 7.4 %copy-start = (f32[3,512,512]{2,1,0:T(8,128)S(1)}, f32[3,512,512]{2,1,0:T(8,128)}, u32[]{:S(2)}) copy-start(f32[3,512,512]{2,1,0:T(8,128)} %get-tuple-element.80) | copy-start | bytes 9437188
  137.1 33.3 %collective-permute-start.10 = (bf16[2,18,24,512]{3,2,1,0:T(8,128)(2,1)}, bf16[2,18,24,512]{3,2,1,0:T(8,128)(2,1)}, u32[]{:S(2)}, u32[]{:S(2)}) collective-permute-start(bf16[2,18,24,512]{3,2,1,0:T(8,128)(2,1)} %bitcast.134), channel_id=1, source_target_pairs={{3,0},{0,1},{1,2},{2,3},{7,4},{4,5},{5,6},{6,7},{11,8},{8,9},{9,10... | collective-permute-start | bytes 2654216 | tf_op jit(solution)/shard_map/ppermute | solution.py:531
  139.0 1.3 copy-start.1
  140.5 9.2 %collective-permute-start.15 = (bf16[1,1,1,2,2,64,512]{6,5,4,3,2,1,0:T(8,128)(2,1)S(1)}, bf16[1,1,1,2,2,64,512]{6,5,4,3,2,1,0:T(8,128)(2,1)S(1)}, u32[]{:S(2)}, u32[]{:S(2)}) collective-permute-start(bf16[1,1,1,2,2,64,512]{6,5,4,3,2,1,0:T(8,128)(2,1)S(1)} %get-tuple-element.84), channel_id=1, source_target_pairs={{0,8},{1,9},{2,10},{3,11},{4,12},{5,13},{6,14},{7,15},{8,0},{9,1},... | collective-permute-start | bytes 786440 | tf_op jit(solution)/shard_map/ppermute | solution.py:548
  142.0 21.0 %collective-permute-start.16 = (bf16[1,1,1,2,2,64,512]{6,5,4,3,2,1,0:T(8,128)(2,1)S(1)}, bf16[1,1,1,2,2,64,512]{6,5,4,3,2,1,0:T(8,128)(2,1)S(1)}, u32[]{:S(2)}, u32[]{:S(2)}) collective-permute-start(bf16[1,1,1,2,2,64,512]{6,5,4,3,2,1,0:T(8,128)(2,1)S(1)} %get-tuple-element.86), channel_id=1, source_target_pairs={{0,16},{1,17},{2,18},{3,19},{4,20},{5,21},{6,22},{7,23},{8,24},{9,... | collective-permute-start | bytes 786440 | tf_op jit(solution)/shard_map/ppermute | solution.py:548
  142.5 7.2 %copy-start.9 = (bf16[2,9,16,512]{3,2,1,0:T(8,128)(2,1)S(1)}, bf16[2,9,16,512]{3,2,1,0:T(8,128)(2,1)}, u32[]{:S(2)}) copy-start(bf16[2,9,16,512]{3,2,1,0:T(8,128)(2,1)} %get-tuple-element.59) | copy-start | bytes 884740
  142.5 20.5 %copy-start.8 = (bf16[2,9,16,512]{3,2,1,0:T(8,128)(2,1)S(1)}, bf16[2,9,16,512]{3,2,1,0:T(8,128)(2,1)}, u32[]{:S(2)}) copy-start(bf16[2,9,16,512]{3,2,1,0:T(8,128)(2,1)} %get-tuple-element.73) | copy-start | bytes 884740
  142.5 20.5 %collective-permute-start.17 = (bf16[1,1,1,2,2,64,512]{6,5,4,3,2,1,0:T(8,128)(2,1)S(1)}, bf16[1,1,1,2,2,64,512]{6,5,4,3,2,1,0:T(8,128)(2,1)S(1)}, u32[]{:S(2)}, u32[]{:S(2)}) collective-permute-start(bf16[1,1,1,2,2,64,512]{6,5,4,3,2,1,0:T(8,128)(2,1)S(1)} %get-tuple-element.85), channel_id=1, source_target_pairs={{0,24},{1,25},{2,26},{3,27},{4,28},{5,29},{6,30},{7,31},{8,16},{9,... | collective-permute-start | bytes 786440 | tf_op jit(solution)/shard_map/ppermute | solution.py:548
  148.7 33.4 %collective-permute-start.13 = (bf16[2,36,8,512]{3,2,1,0:T(8,128)(2,1)}, bf16[2,36,8,512]{3,2,1,0:T(8,128)(2,1)S(1)}, u32[]{:S(2)}, u32[]{:S(2)}) collective-permute-start(bf16[2,36,8,512]{3,2,1,0:T(8,128)(2,1)} %bitcast.136), channel_id=1, source_target_pairs={{28,0},{29,1},{30,2},{31,3},{0,4},{1,5},{2,6},{3,7},{4,8},{5,9},{6... | collective-permute-start | bytes 1769480 | tf_op jit(solution)/shard_map/ppermute | solution.py:531
  149.7 17.4 %collective-permute-start.11 = (bf16[2,18,8,512]{3,2,1,0:T(8,128)(2,1)S(1)}, bf16[2,18,8,512]{3,2,1,0:T(8,128)(2,1)S(1)}, u32[]{:S(2)}, u32[]{:S(2)}) collective-permute-start(bf16[2,18,8,512]{3,2,1,0:T(8,128)(2,1)S(1)} %bitcast.140), channel_id=1, source_target_pairs={{31,0},{28,1},{29,2},{30,3},{3,4},{0,5},{1,6},{2,7},{7,8},{4,9},{5... | collective-permute-start | bytes 884744 | tf_op jit(solution)/shard_map/ppermute | solution.py:531
  163.0 16.4 %collective-permute-start.12 = (bf16[2,18,8,512]{3,2,1,0:T(8,128)(2,1)S(1)}, bf16[2,18,8,512]{3,2,1,0:T(8,128)(2,1)S(1)}, u32[]{:S(2)}, u32[]{:S(2)}) collective-permute-start(bf16[2,18,8,512]{3,2,1,0:T(8,128)(2,1)S(1)} %bitcast.139), channel_id=1, source_target_pairs={{28,0},{29,1},{30,2},{31,3},{0,4},{1,5},{2,6},{3,7},{4,8},{5,9},{6... | collective-permute-start | bytes 884744 | tf_op jit(solution)/shard_map/ppermute | solution.py:531
  164.2 20.9 %collective-permute-start.18 = (bf16[1,1,1,1,1,64,512]{6,5,4,3,2,1,0:T(8,128)(2,1)S(1)}, bf16[1,1,1,1,1,64,512]{6,5,4,3,2,1,0:T(8,128)(2,1)S(1)}, u32[]{:S(2)}, u32[]{:S(2)}) collective-permute-start(bf16[1,1,1,1,1,64,512]{6,5,4,3,2,1,0:T(8,128)(2,1)S(1)} %get-tuple-element.87), channel_id=1, source_target_pairs={{0,1},{1,0},{2,3},{3,2},{4,5},{5,4},{6,7},{7,6},{8,9},{9,8},{10,11... | collective-permute-start | bytes 196616 | tf_op jit(solution)/shard_map/ppermute | solution.py:548
  167.1 9.7 %copy-start.6 = (bf16[2,18,8,512]{3,2,1,0:T(8,128)(2,1)}, bf16[2,18,8,512]{3,2,1,0:T(8,128)(2,1)S(1)}, u32[]{:S(2)}) copy-start(bf16[2,18,8,512]{3,2,1,0:T(8,128)(2,1)S(1)} %collective-permute-done.11.c_ref) | copy-start | bytes 884740
  167.1 18.0 %collective-permute-start.19 = (bf16[1,1,1,1,1,64,512]{6,5,4,3,2,1,0:T(8,128)(2,1)S(1)}, bf16[1,1,1,1,1,64,512]{6,5,4,3,2,1,0:T(8,128)(2,1)S(1)}, u32[]{:S(2)}, u32[]{:S(2)}) collective-permute-start(bf16[1,1,1,1,1,64,512]{6,5,4,3,2,1,0:T(8,128)(2,1)S(1)} %get-tuple-element.89), channel_id=1, source_target_pairs={{0,2},{1,3},{2,0},{3,1},{4,6},{5,7},{6,4},{7,5},{8,10},{9,11},{10,... | collective-permute-start | bytes 196616 | tf_op jit(solution)/shard_map/ppermute | solution.py:548
  170.4 14.7 %collective-permute-start.20 = (bf16[1,1,1,1,1,64,512]{6,5,4,3,2,1,0:T(8,128)(2,1)S(1)}, bf16[1,1,1,1,1,64,512]{6,5,4,3,2,1,0:T(8,128)(2,1)S(1)}, u32[]{:S(2)}, u32[]{:S(2)}) collective-permute-start(bf16[1,1,1,1,1,64,512]{6,5,4,3,2,1,0:T(8,128)(2,1)S(1)} %get-tuple-element.88), channel_id=1, source_target_pairs={{0,3},{1,2},{2,1},{3,0},{4,7},{5,6},{6,5},{7,4},{8,11},{9,10},{10,... | collective-permute-start | bytes 196616 | tf_op jit(solution)/shard_map/ppermute | solution.py:548
  179.4 0.7 copy-start.5
  182.1 0.8 copy-start.3

commit v4 on v3

--- a/solution.py
+++ b/solution.py
@@ -218,14 +218,14 @@
     )
 
 
-def attention_kernel(*refs, first, carried, into):
-    normed_ref, gs_ref, reg_ref, w_ref, wp_ref = refs[:5]
-    refs = refs[5:]
+def attention_kernel(*refs, carried, last):
+    normed_ref, inv_ref, gs_ref, reg_ref, w_ref, wp_ref = refs[:6]
+    refs = refs[6:]
     if carried:
         gw_in, gp_in = refs[:2]
-        refs = refs[2 + (2 if into else 0):]
-    att_ref, gqkv_ref, gw_ref, gp_ref = refs
-    group = pl.program_id(0) + first
+        refs = refs[2:]
+    back_ref, gw_ref, gp_ref, branch_acc, pre_acc = refs
+    group = pl.program_id(0)
     window = pl.program_id(1)
     scale = HEAD ** (-0.5)
     normed = normed_ref[window]
@@ -276,22 +276,50 @@
     grad_q_t = jnp.concatenate(grad_q_t, axis=0)
     grad_k = jnp.concatenate(grad_ks, axis=1)
     grad_v = jnp.concatenate(grad_vs, axis=1)
-    att_ref[0] = att_t.T.astype(BF16)
-    gqkv_ref[0, 0] = grad_q_t.T.astype(BF16)
-    gqkv_ref[0, 1] = grad_k.astype(BF16)
-    gqkv_ref[0, 2] = grad_v.astype(BF16)
+    att = att_t.T.astype(BF16)
+    grad_qkv = jnp.concatenate(
+        [grad_q_t.T.astype(BF16), grad_k.astype(BF16), grad_v.astype(BF16)], axis=1
+    )
+    branch = nt(att, wp_ref[...])
+    grad_normed = nn(grad_qkv, weights)
+
+    @pl.when(group == 0)
+    def _():
+        branch_acc[window] = branch
+        pre_acc[window] = grad_normed
+
+    @pl.when(group > 0)
+    def _():
+        branch_acc[window] += branch
+        pre_acc[window] += grad_normed
+
+    @pl.when(group == pl.num_programs(0) - 1)
+    def _():
+        back_ref[0, 0] = branch_acc[window].astype(BF16)
+        total = pre_acc[window]
+        normal = normed_ref[window].astype(F32)
+        mean = jnp.mean(total, axis=-1, keepdims=True)
+        along = jnp.mean(total * normal, axis=-1, keepdims=True)
+        pre = inv_ref[window][:, :1] * (total - mean - normal * along)
+        back_ref[0, 1] = pre.astype(BF16)
+
     turned = [grad_q_t.astype(BF16), grad_k.T.astype(BF16), grad_v.T.astype(BF16)]
     grad_w = nn(jnp.concatenate(turned, axis=0), normed).reshape(3, wide, grads.shape[1])
     grad_p = nn(att_t.astype(BF16), grads).T
-
-    def start(add):
-        gw_ref[...] = grad_w + gw_in[...] if add else grad_w
-        gp_ref[...] = grad_p + gp_in[...] if add else grad_p
-
-    opening = window == 0
+    kind = gw_ref.dtype
     if carried:
-        pl.when(opening & (group < carried))(lambda: start(True))
-    pl.when(opening & (group >= carried))(lambda: start(False))
+        first_w, first_p = grad_w + gw_in[...], grad_p + gp_in[...]
+    else:
+        first_w, first_p = grad_w, grad_p
+    if last:
+        gw_ref[...] = first_w.astype(kind)
+        gp_ref[...] = first_p.astype(kind)
+        return
+
+    @pl.when(window == 0)
+    def _():
+        gw_ref[...] = first_w
+        gp_ref[...] = first_p
 
     @pl.when(window > 0)
     def _():
@@ -299,173 +327,117 @@
         gp_ref[...] += grad_p
 
 
-def attention(normed, gs, regions, w_qkv, w_proj, carry=(), carried=0, groups=None, into=()):
+def attention(normed, inv, gs, regions, w_qkv, w_proj, carry=(), last=False):
     windows, count, width = normed.shape
+    assert not last or windows == 1
     wide = GROUP * LANES
-    first, number = groups or (0, width // wide)
+    number = width // wide
     whole = lambda *shape: pl.BlockSpec(shape, lambda p, w: (0,) * len(shape))
-    rows3 = pl.BlockSpec((3, wide, width), lambda p, w: (0, p + first, 0))
-    cols1 = pl.BlockSpec((width, wide), lambda p, w: (0, p + first))
-    anyw = pl.BlockSpec(memory_space=pl.ANY)
-    args = [normed, gs, regions[:, None, :], w_qkv, w_proj, *carry, *into]
-    alias = {}
-    if carry:
-        alias = {5: 2, 6: 3}
-    if into:
-        alias |= {7: 0, 8: 1}
+    rows3 = pl.BlockSpec((3, wide, width), lambda p, w: (0, p, 0))
+    cols1 = pl.BlockSpec((width, wide), lambda p, w: (0, p))
+    kind = BF16 if last else F32
     return pl.pallas_call(
-        functools.partial(attention_kernel, first=first, carried=carried, into=bool(into)),
+        functools.partial(attention_kernel, carried=bool(carry), last=last),
         grid=(number, windows),
         in_specs=[
             whole(windows, count, width),
+            whole(windows, count, LANES),
             whole(windows, count, width),
             whole(windows, 1, count),
             rows3,
             cols1,
         ]
-        + ([rows3, cols1] if carry else [])
-        + ([anyw, anyw] if into else []),
+        + ([rows3, cols1] if carry else []),
         out_specs=[
-            pl.BlockSpec((1, count, wide), lambda p, w: (w, 0, p + first)),
-            pl.BlockSpec((1, 3, count, wide), lambda p, w: (w, 0, 0, p + first)),
+            pl.BlockSpec(
+                (1, 2, count, width), lambda p, w: (jnp.where(p == number - 1, w, 0), 0, 0, 0)
+            ),
             rows3,
             cols1,
         ],
         out_shape=(
-            jax.ShapeDtypeStruct((windows, count, width), BF16),
-            jax.ShapeDtypeStruct((windows, 3, count, width), BF16),
-            jax.ShapeDtypeStruct((3, width, width), F32),
-            jax.ShapeDtypeStruct((width, width), F32),
+            jax.ShapeDtypeStruct((windows, 2, count, width), BF16),
+            jax.ShapeDtypeStruct((3, width, width), kind),
+            jax.ShapeDtypeStruct((width, width), kind),
         ),
-        input_output_aliases=alias,
+        scratch_shapes=[pltpu.VMEM((windows, count, width), F32)] * 2,
+        input_output_aliases={6: 1, 7: 2} if carry and not last else {},
         cost_estimate=pl.CostEstimate(
-            flops=windows * count * number * wide * (16 * width + 12 * count), transcendentals=0,
-            bytes_accessed=windows * count * number * wide * 12),
-    )(*args)
-
-
-def back(att, gqkv, normed, inv, w_ref, wp_ref, scr):
-    shape = scr.shape[1:]
-    branch = nt(att[0], wp_ref[...])
-    scr[0] = branch.astype(BF16).astype(F32).reshape(shape)
-    grad_normed = nn(gqkv[0, 0], w_ref[0]) + nn(gqkv[0, 1], w_ref[1]) + nn(gqkv[0, 2], w_ref[2])
-    normal = normed[0].astype(F32)
-    mean = jnp.mean(grad_normed, axis=-1, keepdims=True)
-    along = jnp.mean(grad_normed * normal, axis=-1, keepdims=True)
-    pre = inv[0][:, :1] * (grad_normed - mean - normal * along)
-    scr[1] = pre.astype(BF16).astype(F32).reshape(shape)
-
-
-def finish_low_kernel(*refs):
-    ins, (w_ref, wp_ref, f_ref, g_ref) = refs[:8], refs[8:12]
-    out_ref, gout_ref, east_ref, low_ref, corner_ref, first, second = refs[12:]
-    back(*ins[:4], w_ref, wp_ref, first)
-    back(*ins[4:], w_ref, wp_ref, second)
+            flops=windows * count * width * (20 * width + 12 * count), transcendentals=0,
+            bytes_accessed=windows * count * width * 12),
+    )(normed, inv, gs, regions[:, None, :], w_qkv, w_proj, *carry)
+
+
+def send_kernel(below, second, east, f_ref, g_ref, out_ref, gout_ref, east0, east1, low_ref,
+                corner_ref):
     n = f_ref.shape[0]
+
+    @pl.loop(0, n, unroll=3)
+    def _(p):
+        for i in range(2):
+            tokens = east[0, i, p].astype(F32)
+            east0[i, p] = unpick(tokens, tokens)[1].astype(BF16)
 
     @pl.when(pl.program_id(0) == 0)
     def _():
         @pl.loop(0, n, unroll=3)
         def _(p):
             for i, (x, o) in enumerate(((f_ref, out_ref), (g_ref, gout_ref))):
-                add, strip = unpick(first[i, p], second[i, p])
+                add, strip = unpick(below[0, i, p].astype(F32), second[0, i, p].astype(F32))
                 o[p] = (x[p].astype(F32) + add).astype(BF16)
-                east_ref[i, p] = strip.astype(BF16)
+                east1[i, p] = strip.astype(BF16)
 
     @pl.when(pl.program_id(0) == 1)
     def _():
         @pl.loop(0, n, unroll=3)
         def _(p):
             for i in range(2):
-                add, strip = unpick(first[i, p], second[i, p])
+                add, strip = unpick(below[0, i, p].astype(F32), second[0, i, p].astype(F32))
                 low_ref[i, p] = add.astype(BF16)
                 corner_ref[i, p] = strip.astype(BF16)
 
 
-def finish_east_kernel(att, gqkv, normed, inv, w_ref, wp_ref, east_ref, kept_ref, second):
-    back(att, gqkv, normed, inv, w_ref, wp_ref, second)
-    kept_ref[...] = second[...].astype(BF16)
-
-    @pl.loop(0, second.shape[1], unroll=3)
-    def _(p):
-        for i in range(2):
-            _, strip = unpick(second[i, p], second[i, p])
-            east_ref[i, p] = strip.astype(BF16)
-
-
-def finish_top_kernel(att, gqkv, normed, inv, kept_ref, w_ref, wp_ref, f_ref, g_ref, any0, any1,
-                      out_ref, gout_ref, first):
-    back(att, gqkv, normed, inv, w_ref, wp_ref, first)
-
+def send(below, second, fields, grads, skip):
+    pairs, _, width = fields.shape
+    last = pairs // skip - 1
+    own = pl.BlockSpec((skip, 48, width), lambda s: (last, 0, 0))
+    half = lambda at: pl.BlockSpec((1, 2, skip, 3 * SUB, width), lambda s: (at, 0, s, 0, 0))
+    whole = lambda *shape: pl.BlockSpec(shape, lambda s: (0,) * len(shape))
+    strips = [(2, skip, 16, width), (2, skip, 48, width), (2, skip, 16, width)]
+    outs = [(pairs, 48, width)] * 2 + [(2, 2 * skip, 16, width)] + strips
+    return pl.pallas_call(
+        send_kernel,
+        grid=(2,),
+        in_specs=[half(0), half(1), half(0), own, own],
+        out_specs=[own, own, pl.BlockSpec((2, skip, 16, width), lambda s: (0, s, 0, 0))]
+        + [whole(*shape) for shape in strips],
+        out_shape=tuple(jax.ShapeDtypeStruct(shape, BF16) for shape in outs),
+        name="send",
+    )(below, second, second, fields, grads)
+
+
+def finish_kernel(first, second, f_ref, g_ref, any0, any1, out_ref, gout_ref):
     @pl.loop(0, f_ref.shape[0], unroll=3)
     def _(p):
         for i, (x, o) in enumerate(((f_ref, out_ref), (g_ref, gout_ref))):
-            add, _ = unpick(first[i, p], kept_ref[i, p].astype(F32))
+            add, _ = unpick(first[0, i, p].astype(F32), second[0, i, p].astype(F32))
             o[p] = (x[p].astype(F32) + add).astype(BF16)
 
 
-def finish_call(kernel, sets, width, skip, w_qkv, w_proj, more, specs, outs, out_specs, alias,
-                ahead=()):
-    part = skip * 3 * SUB
-    whole = lambda *shape: pl.BlockSpec(shape, lambda s: (0,) * len(shape))
-    ins, args = [], []
-    for at, arrays in sets:
-        ins += [
-            pl.BlockSpec((1, part, width), lambda s, at=at: (at, s, 0)),
-            pl.BlockSpec((1, 3, part, width), lambda s, at=at: (at, 0, s, 0)),
-            pl.BlockSpec((1, part, width), lambda s, at=at: (at, s, 0)),
-            pl.BlockSpec((1, part, LANES), lambda s, at=at: (at, s, 0)),
-        ]
-        args += arrays
-    args += [x for x, _ in ahead] + [w_qkv, w_proj] + list(more)
-    ins += [x for _, x in ahead] + [whole(3, width, width), whole(width, width)] + list(specs)
-    return pl.pallas_call(
-        kernel,
-        grid=(2,),
-        in_specs=ins,
-        out_specs=out_specs,
-        out_shape=tuple(jax.ShapeDtypeStruct(shape, BF16) for shape in outs),
-        scratch_shapes=[pltpu.VMEM((2, skip, 3 * SUB, width), F32)] * len(sets),
-        input_output_aliases={len(args) - back_at: at for back_at, at in alias.items()},
-        cost_estimate=pl.CostEstimate(
-            flops=2 * len(sets) * part * 8 * width * width, transcendentals=0,
-            bytes_accessed=4 * len(sets) * part * width * 16),
-    )(*args)
-
-
-def finish_low(first, second, w_qkv, w_proj, fields, grads, skip):
-    pairs, _, width = fields.shape
-    last = pairs // skip - 1
-    own = pl.BlockSpec((skip, 48, width), lambda s: (last, 0, 0))
-    whole = lambda *shape: pl.BlockSpec(shape, lambda s: (0,) * len(shape))
-    strips = [(2, skip, 16, width), (2, skip, 48, width), (2, skip, 16, width)]
-    return finish_call(
-        finish_low_kernel, [(0, first), (1, second)], width, skip, w_qkv, w_proj,
-        (fields, grads), (own, own), [(pairs, 48, width)] * 2 + strips,
-        [own, own] + [whole(*shape) for shape in strips], {},
-    )
-
-
-def finish_east(arrays, w_qkv, w_proj, skip):
-    width = w_proj.shape[0]
-    rows = lambda n: pl.BlockSpec((2, skip, n, width), lambda s: (0, s, 0, 0))
-    return finish_call(
-        finish_east_kernel, [(0, arrays)], width, skip, w_qkv, w_proj, (), (),
-        [(2, 2 * skip, 16, width), (2, 2 * skip, 3 * SUB, width)],
-        [rows(16), rows(3 * SUB)], {},
-    )
-
-
-def finish_top(arrays, kept, w_qkv, w_proj, fields, grads, skip, into):
+def finish(first, second, fields, grads, skip, out, gout):
     pairs, _, width = fields.shape
     own = pl.BlockSpec((skip, 48, width), lambda s: (s + 1, 0, 0))
     anyw = pl.BlockSpec(memory_space=pl.ANY)
-    rows = pl.BlockSpec((2, skip, 3 * SUB, width), lambda s: (0, s, 0, 0))
-    return finish_call(
-        finish_top_kernel, [(0, arrays)], width, skip, w_qkv, w_proj,
-        (fields, grads, *into), (own, own, anyw, anyw), [(pairs, 48, width)] * 2,
-        [own, own], {2: 0, 1: 1}, ahead=[(kept, rows)],
-    )
+    half = pl.BlockSpec((1, 2, skip, 3 * SUB, width), lambda s: (0, 0, s, 0, 0))
+    return pl.pallas_call(
+        finish_kernel,
+        grid=(2,),
+        in_specs=[half, half, own, own, anyw, anyw],
+        out_specs=[own, own],
+        out_shape=(jax.ShapeDtypeStruct((pairs, 48, width), BF16),) * 2,
+        input_output_aliases={4: 0, 5: 1},
+        name="finish",
+    )(first, second, fields, grads, out, gout)
 
 
 def edge_kernel(f_ref, o_ref, r_ref, g_ref, q_ref, out_ref, gout_ref):
@@ -632,19 +604,17 @@
     regions = token_regions(region_ids, levels)
     n00, i00, g00 = assemble_own(f_pairs, g_pairs, skip)
     n10, i10, g10 = assemble_below(f_pairs, g_pairs, low, skip)
-    a10, q10, *carry = attention(n10, g10, regions[1, :1], w3, p_all)
+    b10, *carry = attention(n10, i10, g10, regions[1, :1], w3, p_all)
     n1, i1, g1 = assemble_second(f_pairs, g_pairs, east, low, corner, skip)
-    many = width // (GROUP * LANES)
-    a1, q1, *carry = attention(n1, g1, regions[:, 1], w3, p_all, carry, many)
-    out, gout, r_east1, r_low, r_corner = finish_low(
-        (a10, q10, n10, i10), (a1, q1, n1, i1), w3, p_all, f_pairs, g_pairs, skip
-    )
+    b1, *carry = attention(n1, i1, g1, regions[:, 1], w3, p_all, carry)
+    b10, b1 = [x.reshape(-1, 2, 2 * skip, 3 * SUB, width) for x in (b10, b1)]
+    out, gout, r_east0, r_east1, r_low, r_corner = send(b10, b1, f_pairs, g_pairs, skip)
     r_low = shift_by(unpaired(r_low), 0, -1)
     r_corner = shift_by(unpaired(r_corner), -1, -1)
-    r_east0, kept = finish_east((a1, q1, n1, i1), w3, p_all, skip)
     r_east1 = shift_by(unpaired(r_east1), -1, 0)
     r_east0 = shift_by(unpaired(r_east0), -1, 0)
-    a00, q00, grad_w, grad_p = attention(n00, g00, regions[0, :1], w3, p_all, carry, many)
+    b00, grad_w, grad_p = attention(n00, i00, g00, regions[0, :1], w3, p_all, carry, True)
+    b00 = b00.reshape(-1, 2, 2 * skip, 3 * SUB, width)
     grads = jnp.concatenate(
         [grad_w.reshape(devices, -1, width), grad_p.reshape(devices, -1, width)], axis=1
     )
@@ -652,9 +622,7 @@
     for group in groups[::-1]:
         grads = scatter_stage(grads, group, bits, place)
     grads = grads.reshape(-1, width) * factor
-    out, gout = finish_top(
-        (a00, q00, n00, i00), kept, w3, p_all, f_pairs, g_pairs, skip, (out, gout)
-    )
+    out, gout = finish(b00, b1, f_pairs, g_pairs, skip, out, gout)
     out, gout = unpaired(out), unpaired(gout)
     out, gout = rim(f_lines, r_low, r_corner, g_lines, out, gout)
     out, gout = edge(f_lines, out, r_east1, g_lines, gout, 2 * skip, rows * levels // (2 * skip) - 1)

time: 187 us -> 187 us (level)
  waiting for transfers between devices: 45.3 us -> 51.1 us
  Pallas kernels: 95.3 us -> 91.6 us
    ppermute x14, waiting for transfers between devices: 29.4 us -> 34.9 us  [swap(): return lax.ppermute(block, AXES, [(i, i ^ bit) for i in range(total)])]
    pallas_call x6 -> x5, Pallas kernels: 73.3 us -> 69.6 us  [the longest x3 62.6 us: attention(): pl.pallas_call(functools.partial(attention_kernel, carried=bool(carry), l...]
    convert_element_type x1 -> x0, other arithmetic: 2.69 us -> none  [scatter_stage(): total = total + swap(send.astype(BF16), mask).astype(F32)]
  transfers between devices with their start and end apart: 21 -> 21, of which waited for: 10 -> 10; matrix products, arithmetic and copies ran while one was open for 3% -> 3% of each run, Pallas kernels for 21% -> 14%
where the time goes in v4:
time: 187 us; the launch traced here: 186 us
  Pallas kernels  91.6 us (49%)
  waiting for transfers between devices  51.1 us (27%)
  starting transfers between devices  23.5 us (13%)
  local copies, waits for them, and re-layouts  14 us (7%)
  other arithmetic  4.84 us (3%)
    pallas_call x3, Pallas kernels, attention(): pl.pallas_call(functools.partial(attention_kernel, carried=bool(carry), l...  62.6 us
    ppermute x14, waiting for transfers between devices, swap(): return lax.ppermute(block, AXES, [(i, i ^ bit) for i in range(total)])  34.9 us
    ppermute x14, starting transfers between devices, swap(): return lax.ppermute(block, AXES, [(i, i ^ bit) for i in range(total)])  20.5 us
    ppermute x7, waiting for transfers between devices, shift_by(): return lax.ppermute(block, AXES, route)  16.3 us
    pallas_call x3, Pallas kernels, assembled(): pl.pallas_call(kernel, grid=(2 * windows,), in_specs=specs, out_specs=[ou...  12.4 us
    unnamed x21, local copies, waits for them, and re-layouts  5.36 us
    pallas_call x2, Pallas kernels, edge(): pl.pallas_call(edge_kernel, grid=(n,), in_specs=[at, at, strip, at, at],...  4.24 us
    pallas_call x1, Pallas kernels, send(): pl.pallas_call(send_kernel, grid=(2,), in_specs=[half(0), half(1), half(0...  3.93 us
  transfers between devices with their start and end apart: 21, of which 10 were waited for; matrix products, arithmetic and copies ran while one was open for 3% of the time, Pallas kernels for 14%

profile of v4, /device:TPU:0, one launch (start us, length us, event | category | flops | bytes accessed | tf_op | source)
XLA Modules:
  0.0 186.0 jit_solution(9361432292641690000)
XLA Ops:
  2.2 5.1 %collective-permute-start.1 = (bf16[1,1,1,1,1,64,512]{6,5,4,3,2,1,0:T(8,128)(2,1)S(1)}, bf16[1,1,1,1,1,64,512]{6,5,4,3,2,1,0:T(8,128)(2,1)S(1)}, u32[]{:S(2)}, u32[]{:S(2)}) collective-permute-start(bf16[1,1,1,1,1,64,512]{6,5,4,3,2,1,0:T(8,128)(2,1)S(1)} %bitcast.118), channel_id=1, source_target_pairs={{0,3},{1,2},{2,1},{3,0},{4,7},{5,6},{6,5},{7,4},{8,11},{9,10},{10,... | collective-permute-start | bytes 196616 | tf_op jit(solution)/shard_map/ppermute | solution.py:520
  7.8 1.9 %collective-permute-done.1 = bf16[1,1,1,1,1,64,512]{6,5,4,3,2,1,0:T(8,128)(2,1)S(1)} collective-permute-done((bf16[1,1,1,1,1,64,512]{6,5,4,3,2,1,0:T(8,128)(2,1)S(1)}, bf16[1,1,1,1,1,64,512]{6,5,4,3,2,1,0:T(8,128)(2,1)S(1)}, u32[]{:S(2)}, u32[]{:S(2)}) %collective-permute-start.1) | collective-permute-done | bytes 65568 | tf_op jit(solution)/shard_map/ppermute | solution.py:520
  9.7 3.1 %collective-permute-done.2 = bf16[1,1,1,1,1,64,512]{6,5,4,3,2,1,0:T(8,128)(2,1)S(1)} collective-permute-done((bf16[1,1,1,1,1,64,512]{6,5,4,3,2,1,0:T(8,128)(2,1)S(1)}, bf16[1,1,1,1,1,64,512]{6,5,4,3,2,1,0:T(8,128)(2,1)S(1)}, u32[]{:S(2)}, u32[]{:S(2)}) %collective-permute-start.2) | collective-permute-done | bytes 65568 | tf_op jit(solution)/shard_map/ppermute | solution.py:520
  12.9 2.5 %collective-permute-start.4 = (bf16[1,1,1,2,2,64,512]{6,5,4,3,2,1,0:T(8,128)(2,1)S(1)}, bf16[1,1,1,2,2,64,512]{6,5,4,3,2,1,0:T(8,128)(2,1)S(1)}, u32[]{:S(2)}, u32[]{:S(2)}) collective-permute-start(bf16[1,1,1,2,2,64,512]{6,5,4,3,2,1,0:T(8,128)(2,1)S(1)} %maximum_select_fusion.5), channel_id=1, source_target_pairs={{0,24},{1,25},{2,26},{3,27},{4,28},{5,29},{6,30},{7,31},{8,16},{9,... | collective-permute-start | bytes 786440 | tf_op jit(solution)/shard_map/ppermute | solution.py:520
  16.5 6.6 %collective-permute-done.4 = bf16[1,1,1,2,2,64,512]{6,5,4,3,2,1,0:T(8,128)(2,1)S(1)} collective-permute-done((bf16[1,1,1,2,2,64,512]{6,5,4,3,2,1,0:T(8,128)(2,1)S(1)}, bf16[1,1,1,2,2,64,512]{6,5,4,3,2,1,0:T(8,128)(2,1)S(1)}, u32[]{:S(2)}, u32[]{:S(2)}) %collective-permute-start.4) | collective-permute-done | bytes 262176 | tf_op jit(solution)/shard_map/ppermute | solution.py:520
  23.1 4.3 %collective-permute-done.5 = bf16[1,1,1,2,2,64,512]{6,5,4,3,2,1,0:T(8,128)(2,1)S(1)} collective-permute-done((bf16[1,1,1,2,2,64,512]{6,5,4,3,2,1,0:T(8,128)(2,1)S(1)}, bf16[1,1,1,2,2,64,512]{6,5,4,3,2,1,0:T(8,128)(2,1)S(1)}, u32[]{:S(2)}, u32[]{:S(2)}) %collective-permute-start.5) | collective-permute-done | bytes 262176 | tf_op jit(solution)/shard_map/ppermute | solution.py:520
  28.0 2.8 %pack.1 = (bf16[2,18,24,512]{3,2,1,0:T(8,128)(2,1)}, bf16[2,18,8,512]{3,2,1,0:T(8,128)(2,1)}, bf16[2,54,8,512]{3,2,1,0:T(8,128)(2,1)}) custom-call(bf16[72,24,512]{2,1,0:T(8,128)(2,1)} %bitcast.73, bf16[72,24,512]{2,1,0:T(8,128)(2,1)} %bitcast.74, bf16[72,24,512]{2,1,0:T(8,128)(2,1)} %bitcast.83, bf16[72,24,512]{2,1,0:T(8,128)(2,1)} %bitcast.84), custom_call_target="tpu_custom_call" | custom-call | tf_op jit(solution)/shard_map/pack/pallas_call | solution.py:102
  30.8 1.4 collective-permute-start
  32.2 1.6 collective-permute-start.8
  35.3 3.2 %shard_map.88 = (bf16[1,18,24,512]{3,2,1,0:T(8,128)(2,1)}, f32[1,18,24,128]{3,2,1,0:T(8,128)}, bf16[1,18,24,512]{3,2,1,0:T(8,128)(2,1)}) custom-call(bf16[36,48,512]{2,1,0:T(8,128)(2,1)} %bitcast.75, bf16[36,48,512]{2,1,0:T(8,128)(2,1)} %bitcast.85), custom_call_target="tpu_custom_call" | custom-call | flops 11059200 | bytes 1769472 | tf_op jit(solution)/shard_map/pallas_call | solution.py:176
  39.2 14.3 %collective-permute-done = bf16[2,18,24,512]{3,2,1,0:T(8,128)(2,1)S(1)} collective-permute-done((bf16[2,18,24,512]{3,2,1,0:T(8,128)(2,1)}, bf16[2,18,24,512]{3,2,1,0:T(8,128)(2,1)S(1)}, u32[]{:S(2)}, u32[]{:S(2)}) %collective-permute-start) | collective-permute-done | bytes 884768 | tf_op jit(solution)/shard_map/ppermute | solution.py:503
  54.4 3.5 %shard_map.84 = (bf16[1,18,24,512]{3,2,1,0:T(8,128)(2,1)}, f32[1,18,24,128]{3,2,1,0:T(8,128)}, bf16[1,18,24,512]{3,2,1,0:T(8,128)(2,1)}) custom-call(bf16[36,48,512]{2,1,0:T(8,128)(2,1)} %bitcast.76, bf16[36,48,512]{2,1,0:T(8,128)(2,1)} %bitcast.86, bf16[2,9,48,512]{3,2,1,0:T(8,128)(2,1)} %bitcast.102), custom_call_target="tpu_custom_call" | custom-call | flops 11059200 | bytes 1769472 | tf_op jit(solution)/shard_map/pallas_call | solution.py:176
  59.6 5.7 %shard_map.86 = (bf16[2,18,24,512]{3,2,1,0:T(8,128)(2,1)}, f32[2,18,24,128]{3,2,1,0:T(8,128)}, bf16[2,18,24,512]{3,2,1,0:T(8,128)(2,1)}) custom-call(bf16[36,48,512]{2,1,0:T(8,128)(2,1)} %bitcast.77, bf16[36,48,512]{2,1,0:T(8,128)(2,1)} %bitcast.87, bf16[2,27,16,512]{3,2,1,0:T(8,128)(2,1)} %bitcast.32.east_ref, bf16[2,9,48,512]{3,2,1,0:T(8,128)(2,1)} %bitcast.103, ...), custom_call_target="tpu_custom_call" | custom-call | flops 22118400 | bytes 3538944 | tf_op jit(solution)/shard_map/pallas_call | solution.py:176
  68.7 1.3 copy.25
  70.0 15.6 %shard_map.85 = (bf16[1,2,432,512]{3,2,1,0:T(8,128)(2,1)}, f32[3,512,512]{2,1,0:T(8,128)}, f32[512,512]{1,0:T(8,128)}) custom-call(bf16[1,432,512]{2,1,0:T(8,128)(2,1)} %bitcast.130, f32[1,432,128]{2,1,0:T(8,128)} %bitcast.136, bf16[1,432,512]{2,1,0:T(8,128)(2,1)} %bitcast.131, s32[1,1,432]{2,1,0:T(1,128)} %get-tuple-element.87.refs_3_, ...), custom_call_target="tpu_custom_call" | custom-call | flops 3411542016 | bytes 2654208 | tf_op jit(solution)/shard_map/pallas_call | solution.py:339
  85.6 30.8 %shard_map.87 = (bf16[2,2,432,512]{3,2,1,0:T(8,128)(2,1)}, f32[3,512,512]{2,1,0:T(8,128)}, f32[512,512]{1,0:T(8,128)}) custom-call(bf16[2,432,512]{2,1,0:T(8,128)(2,1)} %bitcast.126, f32[2,432,128]{2,1,0:T(8,128)} %bitcast.132, bf16[2,432,512]{2,1,0:T(8,128)(2,1)} %bitcast.127, ...), custom_call_target="tpu_custom_call", output_to_operand_aliasing={{1}: (6, {}), {2}: (7, {})} | custom-call | flops 6823084032 | bytes 5308416 | tf_op jit(solution)/shard_map/pallas_call | solution.py:339
  116.4 16.1 %shard_map.89 = (bf16[1,2,432,512]{3,2,1,0:T(8,128)(2,1)}, bf16[3,512,512]{2,1,0:T(8,128)(2,1)}, bf16[512,512]{1,0:T(8,128)(2,1)}) custom-call(bf16[1,432,512]{2,1,0:T(8,128)(2,1)} %bitcast.128, f32[1,432,128]{2,1,0:T(8,128)} %bitcast.135, bf16[1,432,512]{2,1,0:T(8,128)(2,1)} %bitcast.129, s32[1,1,432]{2,1,0:T(1,128)} %get-tuple-element.86.refs_3_, ...), custom_call_target="tpu_custom_call" | custom-call | flops 3411542016 | bytes 2654208 | tf_op jit(solution)/shard_map/pallas_call | solution.py:339
  132.6 1.3 fusion
  133.9 1.3 collective-permute-start.14
  135.2 3.9 %send.1 = (bf16[36,48,512]{2,1,0:T(8,128)(2,1)}, bf16[36,48,512]{2,1,0:T(8,128)(2,1)}, bf16[2,18,16,512]{3,2,1,0:T(8,128)(2,1)}, bf16[2,9,16,512]{3,2,1,0:T(8,12...) custom-call(bf16[1,2,18,24,512]{4,3,2,1,0:T(8,128)(2,1)} %bitcast.110, ...), custom_call_target="tpu_custom_call" | custom-call | tf_op jit(solution)/shard_map/send/pallas_call | solution.py:408
  139.2 1.6 convert_add_fusion
  140.8 1.3 copy-done.1
  142.2 1.6 collective-permute-start.15
  144.3 1.5 collective-permute-start.17
  145.8 5.7 %collective-permute-done.15 = bf16[1,1,1,2,2,64,512]{6,5,4,3,2,1,0:T(8,128)(2,1)S(1)} collective-permute-done((bf16[1,1,1,2,2,64,512]{6,5,4,3,2,1,0:T(8,128)(2,1)S(1)}, bf16[1,1,1,2,2,64,512]{6,5,4,3,2,1,0:T(8,128)(2,1)S(1)}, u32[]{:S(2)}, u32[]{:S(2)}) %collective-permute-start.15) | collective-permute-done | bytes 262176 | tf_op jit(solution)/shard_map/ppermute | solution.py:520
  151.5 13.1 %collective-permute-done.16 = bf16[1,1,1,2,2,64,512]{6,5,4,3,2,1,0:T(8,128)(2,1)S(1)} collective-permute-done((bf16[1,1,1,2,2,64,512]{6,5,4,3,2,1,0:T(8,128)(2,1)S(1)}, bf16[1,1,1,2,2,64,512]{6,5,4,3,2,1,0:T(8,128)(2,1)S(1)}, u32[]{:S(2)}, u32[]{:S(2)}) %collective-permute-start.16) | collective-permute-done | bytes 262176 | tf_op jit(solution)/shard_map/ppermute | solution.py:520
  165.9 2.3 %collective-permute-start.18 = (bf16[1,1,1,1,1,64,512]{6,5,4,3,2,1,0:T(8,128)(2,1)S(1)}, bf16[1,1,1,1,1,64,512]{6,5,4,3,2,1,0:T(8,128)(2,1)S(1)}, u32[]{:S(2)}, u32[]{:S(2)}) collective-permute-start(bf16[1,1,1,1,1,64,512]{6,5,4,3,2,1,0:T(8,128)(2,1)S(1)} %get-tuple-element.79), channel_id=1, source_target_pairs={{0,1},{1,0},{2,3},{3,2},{4,5},{5,4},{6,7},{7,6},{8,9},{9,8},{10,11... | collective-permute-start | bytes 196616 | tf_op jit(solution)/shard_map/ppermute | solution.py:520
  169.2 3.0 %collective-permute-start.19 = (bf16[1,1,1,1,1,64,512]{6,5,4,3,2,1,0:T(8,128)(2,1)S(1)}, bf16[1,1,1,1,1,64,512]{6,5,4,3,2,1,0:T(8,128)(2,1)S(1)}, u32[]{:S(2)}, u32[]{:S(2)}) collective-permute-start(bf16[1,1,1,1,1,64,512]{6,5,4,3,2,1,0:T(8,128)(2,1)S(1)} %get-tuple-element.81), channel_id=1, source_target_pairs={{0,2},{1,3},{2,0},{3,1},{4,6},{5,7},{6,4},{7,5},{8,10},{9,11},{10,... | collective-permute-start | bytes 196616 | tf_op jit(solution)/shard_map/ppermute | solution.py:520
  173.2 3.1 %finish.1 = (bf16[36,48,512]{2,1,0:T(8,128)(2,1)}, bf16[36,48,512]{2,1,0:T(8,128)(2,1)}) custom-call(bf16[1,2,18,24,512]{4,3,2,1,0:T(8,128)(2,1)} %bitcast.109, bf16[2,2,18,24,512]{4,3,2,1,0:T(8,128)(2,1)} %bitcast.99, bf16[36,48,512]{2,1,0:T(8,128)(2,1)} %bitcast.79, bf16[36,48,512]{2,1,0:T(8,128)(2,1)} %bitcast.89, ...), custom_call_target="tpu_custom_call", output_to_operand_aliasing={{0}: (4, {}), {1}: (5, {})} | custom-call | tf_op jit(solution)/shard_map/finish/pallas_call | solution.py:432
  176.3 2.5 %rim.1 = (bf16[72,24,512]{2,1,0:T(8,128)(2,1)}, bf16[72,24,512]{2,1,0:T(8,128)(2,1)}) custom-call(bf16[72,24,512]{2,1,0:T(8,128)(2,1)} %bitcast.80, bf16[2,18,24,512]{3,2,1,0:T(8,128)(2,1)} %collective-permute-done.10.low_ref, bf16[2,18,8,512]{3,2,1,0:T(8,128)(2,1)} %copy-done.7, ...), custom_call_target="tpu_custom_call", output_to_operand_aliasing={{0}: (4, {}), {1}: (5, {})} | custom-call | tf_op jit(solution)/shard_map/rim/pallas_call | solution.py:481
  179.6 2.0 %edge.2 = (bf16[72,24,512]{2,1,0:T(8,128)(2,1)}, bf16[72,24,512]{2,1,0:T(8,128)(2,1)}) custom-call(bf16[72,24,512]{2,1,0:T(8,128)(2,1)} %bitcast.81, bf16[72,24,512]{2,1,0:T(8,128)(2,1)} %get-tuple-element.64.o_ref, bf16[2,18,8,512]{3,2,1,0:T(8,128)(2,1)} %copy-done.6, bf16[72,24,512]{2,1,0:T(8,128)(2,1)} %bitcast.91, ...), custom_call_target="tpu_custom_call", output_to_operand_aliasing={{0}: (1, {}), {1}: (4, {})} | custom-call | tf_op jit(solution)/shard_map/edge/pallas_call | solution.py:455
  182.4 2.3 %edge.3 = (bf16[72,24,512]{2,1,0:T(8,128)(2,1)}, bf16[72,24,512]{2,1,0:T(8,128)(2,1)}) custom-call(bf16[72,24,512]{2,1,0:T(8,128)(2,1)} %bitcast.82, bf16[72,24,512]{2,1,0:T(8,128)(2,1)} %get-tuple-element.67.o_ref, bf16[2,36,8,512]{3,2,1,0:T(8,128)(2,1)} %copy-done.4, bf16[72,24,512]{2,1,0:T(8,128)(2,1)} %bitcast.92, ...), custom_call_target="tpu_custom_call", output_to_operand_aliasing={{0}: (1, {}), {1}: (4, {})} | custom-call | tf_op jit(solution)/shard_map/edge/pallas_call | solution.py:455
  (83 shorter events, 18.7 us)
Async XLA Ops:
  2.2 7.6 %collective-permute-start.1 = (bf16[1,1,1,1,1,64,512]{6,5,4,3,2,1,0:T(8,128)(2,1)S(1)}, bf16[1,1,1,1,1,64,512]{6,5,4,3,2,1,0:T(8,128)(2,1)S(1)}, u32[]{:S(2)}, u32[]{:S(2)}) collective-permute-start(bf16[1,1,1,1,1,64,512]{6,5,4,3,2,1,0:T(8,128)(2,1)S(1)} %bitcast.118), channel_id=1, source_target_pairs={{0,3},{1,2},{2,1},{3,0},{4,7},{5,6},{6,5},{7,4},{8,11},{9,10},{10,... | collective-permute-start | bytes 196616 | tf_op jit(solution)/shard_map/ppermute | solution.py:520
  7.2 5.6 %collective-permute-start.2 = (bf16[1,1,1,1,1,64,512]{6,5,4,3,2,1,0:T(8,128)(2,1)S(1)}, bf16[1,1,1,1,1,64,512]{6,5,4,3,2,1,0:T(8,128)(2,1)S(1)}, u32[]{:S(2)}, u32[]{:S(2)}) collective-permute-start(bf16[1,1,1,1,1,64,512]{6,5,4,3,2,1,0:T(8,128)(2,1)S(1)} %bitcast.119), channel_id=1, source_target_pairs={{0,2},{1,3},{2,0},{3,1},{4,6},{5,7},{6,4},{7,5},{8,10},{9,11},{10,... | collective-permute-start | bytes 196616 | tf_op jit(solution)/shard_map/ppermute | solution.py:520
  7.2 5.6 %collective-permute-start.3 = (bf16[1,1,1,1,1,64,512]{6,5,4,3,2,1,0:T(8,128)(2,1)S(1)}, bf16[1,1,1,1,1,64,512]{6,5,4,3,2,1,0:T(8,128)(2,1)S(1)}, u32[]{:S(2)}, u32[]{:S(2)}) collective-permute-start(bf16[1,1,1,1,1,64,512]{6,5,4,3,2,1,0:T(8,128)(2,1)S(1)} %bitcast.120), channel_id=1, source_target_pairs={{0,1},{1,0},{2,3},{3,2},{4,5},{5,4},{6,7},{7,6},{8,9},{9,8},{10,11... | collective-permute-start | bytes 196616 | tf_op jit(solution)/shard_map/ppermute | solution.py:520
  12.9 10.2 %collective-permute-start.4 = (bf16[1,1,1,2,2,64,512]{6,5,4,3,2,1,0:T(8,128)(2,1)S(1)}, bf16[1,1,1,2,2,64,512]{6,5,4,3,2,1,0:T(8,128)(2,1)S(1)}, u32[]{:S(2)}, u32[]{:S(2)}) collective-permute-start(bf16[1,1,1,2,2,64,512]{6,5,4,3,2,1,0:T(8,128)(2,1)S(1)} %maximum_select_fusion.5), channel_id=1, source_target_pairs={{0,24},{1,25},{2,26},{3,27},{4,28},{5,29},{6,30},{7,31},{8,16},{9,... | collective-permute-start | bytes 786440 | tf_op jit(solution)/shard_map/ppermute | solution.py:520
  15.4 11.9 %collective-permute-start.5 = (bf16[1,1,1,2,2,64,512]{6,5,4,3,2,1,0:T(8,128)(2,1)S(1)}, bf16[1,1,1,2,2,64,512]{6,5,4,3,2,1,0:T(8,128)(2,1)S(1)}, u32[]{:S(2)}, u32[]{:S(2)}) collective-permute-start(bf16[1,1,1,2,2,64,512]{6,5,4,3,2,1,0:T(8,128)(2,1)S(1)} %maximum_select_fusion.5), channel_id=1, source_target_pairs={{0,16},{1,17},{2,18},{3,19},{4,20},{5,21},{6,22},{7,23},{8,24},{9,... | collective-permute-start | bytes 786440 | tf_op jit(solution)/shard_map/ppermute | solution.py:520
  16.0 11.7 %collective-permute-start.6 = (bf16[1,1,1,2,2,64,512]{6,5,4,3,2,1,0:T(8,128)(2,1)S(1)}, bf16[1,1,1,2,2,64,512]{6,5,4,3,2,1,0:T(8,128)(2,1)S(1)}, u32[]{:S(2)}, u32[]{:S(2)}) collective-permute-start(bf16[1,1,1,2,2,64,512]{6,5,4,3,2,1,0:T(8,128)(2,1)S(1)} %maximum_select_fusion.5), channel_id=1, source_target_pairs={{0,8},{1,9},{2,10},{3,11},{4,12},{5,13},{6,14},{7,15},{8,0},{9,1},... | collective-permute-start | bytes 786440 | tf_op jit(solution)/shard_map/ppermute | solution.py:520
  27.9 37.5 %collective-permute-start.7 = (bf16[2,2,1,2,2,64,512]{6,5,4,3,1,2,0:T(8,128)(2,1)S(1)}, bf16[2,2,1,2,2,64,512]{6,5,4,3,1,2,0:T(8,128)(2,1)}, u32[]{:S(2)}, u32[]{:S(2)}) collective-permute-start(bf16[2,2,1,2,2,64,512]{6,5,4,3,1,2,0:T(8,128)(2,1)S(1)} %maximum_select_fusion.1), channel_id=1, source_target_pairs={{0,4},{1,5},{2,6},{3,7},{4,0},{5,1},{6,2},{7,3},{8,12},{9,13},{10,... | collective-permute-start | bytes 3145736 | tf_op jit(solution)/shard_map/ppermute | solution.py:520
  28.0 5.8 %copy-start.8 = (s32[24]{0:T(128)S(1)}, s32[24]{0:T(128)}, u32[]{:S(2)}) copy-start(s32[24]{0:T(128)} %param.6) | copy-start | bytes 292
  30.8 22.7 %collective-permute-start = (bf16[2,18,24,512]{3,2,1,0:T(8,128)(2,1)}, bf16[2,18,24,512]{3,2,1,0:T(8,128)(2,1)S(1)}, u32[]{:S(2)}, u32[]{:S(2)}) collective-permute-start(bf16[2,18,24,512]{3,2,1,0:T(8,128)(2,1)} %get-tuple-element.39), channel_id=1, source_target_pairs={{1,0},{2,1},{3,2},{0,3},{5,4},{6,5},{7,6},{4,7},{9,8},{10,9},{11,1... | collective-permute-start | bytes 2654216 | tf_op jit(solution)/shard_map/ppermute | solution.py:503
  32.2 26.7 %collective-permute-start.8 = (bf16[2,54,8,512]{3,2,1,0:T(8,128)(2,1)}, bf16[2,54,8,512]{3,2,1,0:T(8,128)(2,1)}, u32[]{:S(2)}, u32[]{:S(2)}) collective-permute-start(bf16[2,54,8,512]{3,2,1,0:T(8,128)(2,1)} %get-tuple-element.44), channel_id=1, source_target_pairs={{4,0},{5,1},{6,2},{7,3},{8,4},{9,5},{10,6},{11,7},{12,8},{13,9},{1... | collective-permute-start | bytes 2654216 | tf_op jit(solution)/shard_map/ppermute | solution.py:503
  33.8 25.1 %collective-permute-start.9 = (bf16[2,18,8,512]{3,2,1,0:T(8,128)(2,1)}, bf16[2,18,8,512]{3,2,1,0:T(8,128)(2,1)S(1)}, u32[]{:S(2)}, u32[]{:S(2)}) collective-permute-start(bf16[2,18,8,512]{3,2,1,0:T(8,128)(2,1)} %get-tuple-element.45), channel_id=1, source_target_pairs={{5,0},{6,1},{7,2},{4,3},{9,4},{10,5},{11,6},{8,7},{13,8},{14,9},{1... | collective-permute-start | bytes 884744 | tf_op jit(solution)/shard_map/ppermute | solution.py:503
  53.5 0.9 copy-start.2
  58.9 0.7 copy-start.5
  133.9 5.3 %collective-permute-start.14 = (bf16[2,2,1,2,2,64,512]{6,5,4,3,2,1,0:T(8,128)(2,1)S(1)}, bf16[2,2,1,2,2,64,512]{6,5,4,3,2,1,0:T(8,128)(2,1)}, u32[]{:S(2)}, u32[]{:S(2)}) collective-permute-start(bf16[2,2,1,2,2,64,512]{6,5,4,3,2,1,0:T(8,128)(2,1)S(1)} %fusion), channel_id=1, source_target_pairs={{0,4},{1,5},{2,6},{3,7},{4,0},{5,1},{6,2},{7,3},{8,12},{9,13},{10,... | collective-permute-start | bytes 3145736 | tf_op jit(solution)/shard_map/ppermute | solution.py:520
  135.2 4.0 %copy-start = (bf16[3,512,512]{2,1,0:T(8,128)(2,1)S(1)}, bf16[3,512,512]{2,1,0:T(8,128)(2,1)}, u32[]{:S(2)}) copy-start(bf16[3,512,512]{2,1,0:T(8,128)(2,1)} %get-tuple-element.72) | copy-start | bytes 4718596
  135.2 4.0 %copy-start.3 = (bf16[512,512]{1,0:T(8,128)(2,1)S(1)}, bf16[512,512]{1,0:T(8,128)(2,1)}, u32[]{:S(2)}) copy-start(bf16[512,512]{1,0:T(8,128)(2,1)} %get-tuple-element.73) | copy-start | bytes 1572868
  139.1 25.5 %copy-start.9 = (bf16[2,9,16,512]{3,2,1,0:T(8,128)(2,1)S(1)}, bf16[2,9,16,512]{3,2,1,0:T(8,128)(2,1)}, u32[]{:S(2)}) copy-start(bf16[2,9,16,512]{3,2,1,0:T(8,128)(2,1)} %get-tuple-element.65) | copy-start | bytes 884740
  139.1 33.1 %collective-permute-start.10 = (bf16[2,18,24,512]{3,2,1,0:T(8,128)(2,1)}, bf16[2,18,24,512]{3,2,1,0:T(8,128)(2,1)}, u32[]{:S(2)}, u32[]{:S(2)}) collective-permute-start(bf16[2,18,24,512]{3,2,1,0:T(8,128)(2,1)} %bitcast.125), channel_id=1, source_target_pairs={{3,0},{0,1},{1,2},{2,3},{7,4},{4,5},{5,6},{6,7},{11,8},{8,9},{9,10... | collective-permute-start | bytes 2654216 | tf_op jit(solution)/shard_map/ppermute | solution.py:503
  140.8 1.4 copy-start.1
  142.2 9.2 %collective-permute-start.15 = (bf16[1,1,1,2,2,64,512]{6,5,4,3,2,1,0:T(8,128)(2,1)S(1)}, bf16[1,1,1,2,2,64,512]{6,5,4,3,2,1,0:T(8,128)(2,1)S(1)}, u32[]{:S(2)}, u32[]{:S(2)}) collective-permute-start(bf16[1,1,1,2,2,64,512]{6,5,4,3,2,1,0:T(8,128)(2,1)S(1)} %get-tuple-element.76), channel_id=1, source_target_pairs={{0,8},{1,9},{2,10},{3,11},{4,12},{5,13},{6,14},{7,15},{8,0},{9,1},... | collective-permute-start | bytes 786440 | tf_op jit(solution)/shard_map/ppermute | solution.py:520
  143.8 20.8 %collective-permute-start.16 = (bf16[1,1,1,2,2,64,512]{6,5,4,3,2,1,0:T(8,128)(2,1)S(1)}, bf16[1,1,1,2,2,64,512]{6,5,4,3,2,1,0:T(8,128)(2,1)S(1)}, u32[]{:S(2)}, u32[]{:S(2)}) collective-permute-start(bf16[1,1,1,2,2,64,512]{6,5,4,3,2,1,0:T(8,128)(2,1)S(1)} %get-tuple-element.78), channel_id=1, source_target_pairs={{0,16},{1,17},{2,18},{3,19},{4,20},{5,21},{6,22},{7,23},{8,24},{9,... | collective-permute-start | bytes 786440 | tf_op jit(solution)/shard_map/ppermute | solution.py:520
  144.3 20.3 %collective-permute-start.17 = (bf16[1,1,1,2,2,64,512]{6,5,4,3,2,1,0:T(8,128)(2,1)S(1)}, bf16[1,1,1,2,2,64,512]{6,5,4,3,2,1,0:T(8,128)(2,1)S(1)}, u32[]{:S(2)}, u32[]{:S(2)}) collective-permute-start(bf16[1,1,1,2,2,64,512]{6,5,4,3,2,1,0:T(8,128)(2,1)S(1)} %get-tuple-element.77), channel_id=1, source_target_pairs={{0,24},{1,25},{2,26},{3,27},{4,28},{5,29},{6,30},{7,31},{8,16},{9,... | collective-permute-start | bytes 786440 | tf_op jit(solution)/shard_map/ppermute | solution.py:520
  145.8 35.8 %collective-permute-start.13 = (bf16[2,36,8,512]{3,2,1,0:T(8,128)(2,1)}, bf16[2,36,8,512]{3,2,1,0:T(8,128)(2,1)S(1)}, u32[]{:S(2)}, u32[]{:S(2)}) collective-permute-start(bf16[2,36,8,512]{3,2,1,0:T(8,128)(2,1)} %bitcast.47), channel_id=1, source_target_pairs={{28,0},{29,1},{30,2},{31,3},{0,4},{1,5},{2,6},{3,7},{4,8},{5,9},{6... | collective-permute-start | bytes 1769480 | tf_op jit(solution)/shard_map/ppermute | solution.py:503
  151.5 17.7 %collective-permute-start.11 = (bf16[2,18,8,512]{3,2,1,0:T(8,128)(2,1)}, bf16[2,18,8,512]{3,2,1,0:T(8,128)(2,1)S(1)}, u32[]{:S(2)}, u32[]{:S(2)}) collective-permute-start(bf16[2,18,8,512]{3,2,1,0:T(8,128)(2,1)} %bitcast.134), channel_id=1, source_target_pairs={{31,0},{28,1},{29,2},{30,3},{3,4},{0,5},{1,6},{2,7},{7,8},{4,9},{5... | collective-permute-start | bytes 884744 | tf_op jit(solution)/shard_map/ppermute | solution.py:503
  164.6 14.2 %collective-permute-start.12 = (bf16[2,18,8,512]{3,2,1,0:T(8,128)(2,1)S(1)}, bf16[2,18,8,512]{3,2,1,0:T(8,128)(2,1)S(1)}, u32[]{:S(2)}, u32[]{:S(2)}) collective-permute-start(bf16[2,18,8,512]{3,2,1,0:T(8,128)(2,1)S(1)} %bitcast.133), channel_id=1, source_target_pairs={{28,0},{29,1},{30,2},{31,3},{0,4},{1,5},{2,6},{3,7},{4,8},{5,9},{6... | collective-permute-start | bytes 884744 | tf_op jit(solution)/shard_map/ppermute | solution.py:503
  165.9 18.8 %collective-permute-start.18 = (bf16[1,1,1,1,1,64,512]{6,5,4,3,2,1,0:T(8,128)(2,1)S(1)}, bf16[1,1,1,1,1,64,512]{6,5,4,3,2,1,0:T(8,128)(2,1)S(1)}, u32[]{:S(2)}, u32[]{:S(2)}) collective-permute-start(bf16[1,1,1,1,1,64,512]{6,5,4,3,2,1,0:T(8,128)(2,1)S(1)} %get-tuple-element.79), channel_id=1, source_target_pairs={{0,1},{1,0},{2,3},{3,2},{4,5},{5,4},{6,7},{7,6},{8,9},{9,8},{10,11... | collective-permute-start | bytes 196616 | tf_op jit(solution)/shard_map/ppermute | solution.py:520
  169.2 7.2 %copy-start.7 = (bf16[2,18,8,512]{3,2,1,0:T(8,128)(2,1)}, bf16[2,18,8,512]{3,2,1,0:T(8,128)(2,1)S(1)}, u32[]{:S(2)}) copy-start(bf16[2,18,8,512]{3,2,1,0:T(8,128)(2,1)S(1)} %collective-permute-done.11.c_ref) | copy-start | bytes 884740
  169.2 15.5 %collective-permute-start.19 = (bf16[1,1,1,1,1,64,512]{6,5,4,3,2,1,0:T(8,128)(2,1)S(1)}, bf16[1,1,1,1,1,64,512]{6,5,4,3,2,1,0:T(8,128)(2,1)S(1)}, u32[]{:S(2)}, u32[]{:S(2)}) collective-permute-start(bf16[1,1,1,1,1,64,512]{6,5,4,3,2,1,0:T(8,128)(2,1)S(1)} %get-tuple-element.81), channel_id=1, source_target_pairs={{0,2},{1,3},{2,0},{3,1},{4,6},{5,7},{6,4},{7,5},{8,10},{9,11},{10,... | collective-permute-start | bytes 196616 | tf_op jit(solution)/shard_map/ppermute | solution.py:520
  172.2 12.5 %collective-permute-start.20 = (bf16[1,1,1,1,1,64,512]{6,5,4,3,2,1,0:T(8,128)(2,1)S(1)}, bf16[1,1,1,1,1,64,512]{6,5,4,3,2,1,0:T(8,128)(2,1)S(1)}, u32[]{:S(2)}, u32[]{:S(2)}) collective-permute-start(bf16[1,1,1,1,1,64,512]{6,5,4,3,2,1,0:T(8,128)(2,1)S(1)} %get-tuple-element.80), channel_id=1, source_target_pairs={{0,3},{1,2},{2,1},{3,0},{4,7},{5,6},{6,5},{7,4},{8,11},{9,10},{10,... | collective-permute-start | bytes 196616 | tf_op jit(solution)/shard_map/ppermute | solution.py:520
  178.9 0.7 copy-start.6
  181.6 0.8 copy-start.4

commit v5 on v4

--- a/solution.py
+++ b/solution.py
@@ -123,7 +123,7 @@
 
 
 def assemble_own_kernel(f_ref, g_ref, *outs):
-    @pl.loop(0, f_ref.shape[0], unroll=3)
+    @pl.loop(0, f_ref.shape[0], unroll=9)
     def _(p):
         put(0, p, pick_first(f_ref[p].astype(F32)), pick_first(g_ref[p].astype(F32)), *outs)
 
@@ -131,13 +131,13 @@
 def assemble_below_kernel(f_ref, g_ref, low_ref, *outs):
     @pl.when(pl.program_id(0) == 0)
     def _():
-        @pl.loop(0, f_ref.shape[0], unroll=3)
+        @pl.loop(0, f_ref.shape[0], unroll=9)
         def _(p):
             put(0, p, pick_first(f_ref[p].astype(F32)), pick_first(g_ref[p].astype(F32)), *outs)
 
     @pl.when(pl.program_id(0) == 1)
     def _():
-        @pl.loop(0, f_ref.shape[0], unroll=3)
+        @pl.loop(0, f_ref.shape[0], unroll=9)
         def _(p):
             put(0, p, pick_first(low_ref[0, p].astype(F32)), pick_first(low_ref[1, p].astype(F32)), *outs)
 
@@ -147,7 +147,7 @@
 
     @pl.when(pl.program_id(0) < last)
     def _():
-        @pl.loop(0, f_ref.shape[0], unroll=3)
+        @pl.loop(0, f_ref.shape[0], unroll=9)
         def _(p):
             put(
                 0,
@@ -159,7 +159,7 @@
 
     @pl.when(pl.program_id(0) == last)
     def _():
-        @pl.loop(0, f_ref.shape[0], unroll=3)
+        @pl.loop(0, f_ref.shape[0], unroll=9)
         def _(p):
             put(
                 0,
@@ -221,6 +221,7 @@
 def attention_kernel(*refs, carried, last):
     normed_ref, inv_ref, gs_ref, reg_ref, w_ref, wp_ref = refs[:6]
     refs = refs[6:]
+    gw_in = gp_in = None
     if carried:
         gw_in, gp_in = refs[:2]
         refs = refs[2:]
@@ -245,86 +246,104 @@
     allowed = spread == region
     lane = lax.broadcasted_iota(jnp.int32, (count, LANES), 1)
     zero = jnp.zeros((), BF16)
-    att_t, grad_q_t, grad_ks, grad_vs = [], [], [], []
-    for pair in range(GROUP):
+    heads = GROUP * LANES // HEAD
+    pairs = LANES // HEAD
+
+    def inputs(h):
+        pair, k = divmod(h, pairs)
         cols = slice(pair * LANES, (pair + 1) * LANES)
-        query, keys, values = queries[:, cols], all_keys[:, cols], all_values[:, cols]
-        keys_t, values_t = all_keys_t[cols], all_values_t[cols]
-        grad_att = grad_att_all[:, cols]
-        grad_k = grad_v = None
-        for h in range(LANES // HEAD):
-            mine = (lane >= h * HEAD) & (lane < (h + 1) * HEAD)
-            rows = slice(h * HEAD, (h + 1) * HEAD)
-            scores = nt(jnp.where(mine, keys, zero), query)
-            scores = jnp.where(allowed, scores, -1e30)
-            peak = jnp.max(scores, axis=0, keepdims=True)
-            expo = jnp.exp(scores - peak)
-            ratio = 1.0 / jnp.sum(expo, axis=0, keepdims=True)
-            rounded = (expo * ratio).astype(BF16)
-            grad_probs = nt(jnp.where(mine, values, zero), grad_att)
-            att_t.append(nn(values_t[rows], rounded))
-            inner = jnp.sum(grad_probs * expo, axis=0, keepdims=True) * ratio
-            grad_scores = (expo * (grad_probs - inner) * ratio).astype(BF16)
-            grad_q_t.append(nn(keys_t[rows], grad_scores))
-            part_v = nn(rounded, jnp.where(mine, grad_att, zero))
-            part_k = nn(grad_scores, jnp.where(mine, query, zero))
-            grad_k = part_k if grad_k is None else grad_k + part_k
-            grad_v = part_v if grad_v is None else grad_v + part_v
-        grad_ks.append(grad_k)
-        grad_vs.append(grad_v)
-    att_t = jnp.concatenate(att_t, axis=0)
-    grad_q_t = jnp.concatenate(grad_q_t, axis=0)
-    grad_k = jnp.concatenate(grad_ks, axis=1)
-    grad_v = jnp.concatenate(grad_vs, axis=1)
-    att = att_t.T.astype(BF16)
-    grad_qkv = jnp.concatenate(
-        [grad_q_t.T.astype(BF16), grad_k.astype(BF16), grad_v.astype(BF16)], axis=1
-    )
+        mine = (lane >= k * HEAD) & (lane < (k + 1) * HEAD)
+        return cols, lambda x: jnp.where(mine, x[:, cols], zero)
+
+    def products(h):
+        cols, only = inputs(h)
+        scores = nt(only(all_keys), queries[:, cols])
+        return jnp.where(allowed, scores, -1e30), nt(only(all_values), grad_att_all[:, cols])
+
+    def softmax(scores, grad_probs):
+        peak = jnp.max(scores, axis=0, keepdims=True)
+        expo = jnp.exp(scores - peak)
+        ratio = 1.0 / jnp.sum(expo, axis=0, keepdims=True)
+        rounded = (expo * ratio).astype(BF16)
+        inner = jnp.sum(grad_probs * expo, axis=0, keepdims=True) * ratio
+        return rounded, (expo * (grad_probs - inner) * ratio).astype(BF16)
+
+    def gradients(h, rounded, grad_scores):
+        _, only = inputs(h)
+        rows = slice(h * HEAD, (h + 1) * HEAD)
+        return (
+            nn(all_values_t[rows], rounded),
+            nn(all_keys_t[rows], grad_scores),
+            nn(grad_scores, only(queries)),
+            nn(rounded, only(grad_att_all)),
+        )
+
+    def joined(k, first, number):
+        return jnp.concatenate([d[k] for d in done[first * pairs : (first + number) * pairs]], axis=0)
+
+    def att_rows(first, number):
+        return joined(0, first, number).T.astype(BF16)
+
+    def back_to_rows(first, number):
+        return joined(1, first, number).T.astype(BF16)
+
+    def key_and_value(first, number, turned=False):
+        out = []
+        for k in (2, 3):
+            both = [
+                sum(d[k] for d in done[p * pairs : (p + 1) * pairs]) for p in range(first, first + number)
+            ]
+            if turned:
+                out.append(jnp.concatenate([x.T.astype(BF16) for x in both], axis=0))
+            else:
+                out.append(jnp.concatenate([x.astype(BF16) for x in both], axis=1))
+        return out
+
+    def sums(first, number):
+        turned = [joined(1, first, number).astype(BF16), *key_and_value(first, number, True)]
+        grad_w = nn(jnp.concatenate(turned, axis=0), normed)
+        grad_w = grad_w.reshape(3, number * LANES, grad_w.shape[1])
+        return grad_w, nn(joined(0, first, number).astype(BF16), grads).T, first
+
+    ahead, weights_of, done = {0: products(0)}, {}, []
+    parts = [(0, GROUP)]
+    early = {}
+    for h in range(heads + 1):
+        if h + 1 < heads:
+            ahead[h + 1] = products(h + 1)
+        if h < heads:
+            weights_of[h] = softmax(*ahead.pop(h))
+        if h > 0:
+            done.append(gradients(h - 1, *weights_of.pop(h - 1)))
+    att = att_rows(0, GROUP)
+    grad_qkv = jnp.concatenate([back_to_rows(0, GROUP), *key_and_value(0, GROUP)], axis=1)
     branch = nt(att, wp_ref[...])
     grad_normed = nn(grad_qkv, weights)
-
-    @pl.when(group == 0)
-    def _():
-        branch_acc[window] = branch
-        pre_acc[window] = grad_normed
-
-    @pl.when(group > 0)
-    def _():
-        branch_acc[window] += branch
-        pre_acc[window] += grad_normed
-
-    @pl.when(group == pl.num_programs(0) - 1)
-    def _():
-        back_ref[0, 0] = branch_acc[window].astype(BF16)
-        total = pre_acc[window]
-        normal = normed_ref[window].astype(F32)
-        mean = jnp.mean(total, axis=-1, keepdims=True)
-        along = jnp.mean(total * normal, axis=-1, keepdims=True)
-        pre = inv_ref[window][:, :1] * (total - mean - normal * along)
-        back_ref[0, 1] = pre.astype(BF16)
-
-    turned = [grad_q_t.astype(BF16), grad_k.T.astype(BF16), grad_v.T.astype(BF16)]
-    grad_w = nn(jnp.concatenate(turned, axis=0), normed).reshape(3, wide, grads.shape[1])
-    grad_p = nn(att_t.astype(BF16), grads).T
+    started = group > 0
+    branch += jnp.where(started, branch_acc[window], 0.0)
+    grad_normed += jnp.where(started, pre_acc[window], 0.0)
+    branch_acc[window] = branch
+    pre_acc[window] = grad_normed
+    back_ref[0, 0] = branch.astype(BF16)
+    normal = normed.astype(F32)
+    mean = jnp.mean(grad_normed, axis=-1, keepdims=True)
+    along = jnp.mean(grad_normed * normal, axis=-1, keepdims=True)
+    pre = inv_ref[window][:, :1] * (grad_normed - mean - normal * along)
+    back_ref[0, 1] = pre.astype(BF16)
+    opening = window == 0
     kind = gw_ref.dtype
-    if carried:
-        first_w, first_p = grad_w + gw_in[...], grad_p + gp_in[...]
-    else:
-        first_w, first_p = grad_w, grad_p
-    if last:
-        gw_ref[...] = first_w.astype(kind)
-        gp_ref[...] = first_p.astype(kind)
-        return
-
-    @pl.when(window == 0)
-    def _():
-        gw_ref[...] = first_w
-        gp_ref[...] = first_p
-
-    @pl.when(window > 0)
-    def _():
-        gw_ref[...] += grad_w
-        gp_ref[...] += grad_p
+    for pairs_of in parts:
+        grad_w, grad_p, at = sums(*pairs_of) if pairs_of not in early else early[pairs_of]
+        cols = pl.ds(at * LANES, grad_p.shape[1])
+        for ref, mine, carry, where in (
+            (gw_ref, grad_w, gw_in, (slice(None), cols)),
+            (gp_ref, grad_p, gp_in, (slice(None), cols)),
+        ):
+            if last:
+                ref[where] = (mine + carry[where] if carried else mine).astype(kind)
+            else:
+                base = carry[where] if carried else 0.0
+                ref[where] = mine + jnp.where(opening, base, ref[where])
 
 
 def attention(normed, inv, gs, regions, w_qkv, w_proj, carry=(), last=False):
@@ -558,6 +577,31 @@
     return total
 
 
+def last_join_kernel(place_ref, mine_ref, other_ref, w_ref, p_ref):
+    share = w_ref.shape[3]
+    for own, ref in ((True, mine_ref), (False, other_ref)):
+        at = place_ref[0] if own else 1 - place_ref[0]
+        w_ref[:, at] = ref[:, :, :share]
+        p_ref[:, at] = ref[:, :, share:]
+
+
+def last_join(mine, other, place, share):
+    far, near, rows, width = mine.shape
+    whole = lambda *shape: pl.BlockSpec(shape, lambda i, p: (0,) * len(shape))
+    shapes = [(far, 2, near, share, width), (far, 2, near, rows - share, width)]
+    return pl.pallas_call(
+        last_join_kernel,
+        grid_spec=pltpu.PrefetchScalarGridSpec(
+            num_scalar_prefetch=1,
+            grid=(1,),
+            in_specs=[whole(*mine.shape)] * 2,
+            out_specs=[whole(*shape) for shape in shapes],
+        ),
+        out_shape=tuple(jax.ShapeDtypeStruct(shape, BF16) for shape in shapes),
+        name="last_join",
+    )(place, mine, other)
+
+
 def lines_of(grid):
     rows, cols, levels, width = grid.shape
     return grid.transpose(0, 2, 1, 3).reshape(rows * levels, cols, width)
@@ -594,8 +638,10 @@
         held = gather_stage(held, group, bits, place)
     bit = groups[-1][0]
     other = swap(held, bit)
-    w3 = join(held[..., :share, :], other[..., :share, :], bit, bits, place).reshape(3, width, width)
-    p_all = join(held[..., share:, :], other[..., share:, :], bit, bits, place).reshape(width, width)
+    near = bit
+    halves = [x.reshape(-1, near, held.shape[-2], width) for x in (held, other)]
+    w3, p_all = last_join(*halves, jnp.where((place & bit) != 0, 1, 0).reshape(1), share)
+    w3, p_all = w3.reshape(3, width, width), p_all.reshape(width, width)
     low, corner, east = pack(f_lines, g_lines, 2 * skip)
     low = shift_by(low, 0, 1)
     east = shift_by(east, 1, 0)

time: 187 us -> 165 us (0.88)
  waiting for transfers between devices: 51.1 us -> 39.9 us
  Pallas kernels: 91.6 us -> 83.3 us
  local copies, waits for them, and re-layouts: 14 us -> 10.5 us
  other arithmetic: 4.84 us -> 7.77 us
    ppermute x7, waiting for transfers between devices: 16.3 us -> 3.69 us  [shift_by(): return lax.ppermute(block, AXES, route)]
    pallas_call x3, Pallas kernels: 62.6 us -> 53.3 us  [attention(): pl.pallas_call(functools.partial(attention_kernel, carried=bool(carry), l...]
    ppermute x14, starting transfers between devices: 20.5 us -> 17 us  [swap(): return lax.ppermute(block, AXES, [(i, i ^ bit) for i in range(total)])]
    pallas_call x0 -> x1, Pallas kernels: none -> 3.02 us  [last_join(): pl.pallas_call(last_join_kernel, grid_spec=pltpu.PrefetchScalarGridSpec(n...]
    slice x4 -> x0, local copies, waits for them, and re-layouts: 2.26 us -> none  [the longest x1 1.2 us: block(): other[..., :share, :]]
    select_n x4 -> x5, other arithmetic: 0.51 us -> 2.73 us  [join(): jnp.where(high, jnp.concatenate([other, mine], axis=axis), jnp.concatenat...]
    pallas_call x3, Pallas kernels: 12.4 us -> 10.2 us  [assembled(): pl.pallas_call(kernel, grid=(2 * windows,), in_specs=specs, out_specs=[ou...]
    select_n x2 -> x0, local copies, waits for them, and re-layouts: 2.17 us -> none  [join(): jnp.where(high, jnp.concatenate([other, mine], axis=axis), jnp.concatenat...]
  transfers between devices with their start and end apart: 21 -> 21, of which waited for: 10 -> 7; matrix products, arithmetic and copies ran while one was open for 3% -> 5% of each run, Pallas kernels for 14% -> 14%
where the time goes in v5:
time: 165 us; the launch traced here: 164 us
  Pallas kernels  83.3 us (50%)
  waiting for transfers between devices  39.9 us (24%)
  starting transfers between devices  21.8 us (13%)
  local copies, waits for them, and re-layouts  10.5 us (6%)
  other arithmetic  7.77 us (5%)
    pallas_call x3, Pallas kernels, attention(): pl.pallas_call(functools.partial(attention_kernel, carried=bool(carry), l...  53.3 us
    ppermute x14, waiting for transfers between devices, swap(): return lax.ppermute(block, AXES, [(i, i ^ bit) for i in range(total)])  36.2 us
    ppermute x14, starting transfers between devices, swap(): return lax.ppermute(block, AXES, [(i, i ^ bit) for i in range(total)])  17 us
    pallas_call x3, Pallas kernels, assembled(): pl.pallas_call(kernel, grid=(2 * windows,), in_specs=specs, out_specs=[ou...  10.2 us
    unnamed x23, local copies, waits for them, and re-layouts  6.31 us
    ppermute x7, starting transfers between devices, shift_by(): return lax.ppermute(block, AXES, route)  4.8 us
    pallas_call x2, Pallas kernels, edge(): pl.pallas_call(edge_kernel, grid=(n,), in_specs=[at, at, strip, at, at],...  4.24 us
    pallas_call x1, Pallas kernels, send(): pl.pallas_call(send_kernel, grid=(2,), in_specs=[half(0), half(1), half(0...  3.9 us
  transfers between devices with their start and end apart: 21, of which 7 were waited for; matrix products, arithmetic and copies ran while one was open for 5% of the time, Pallas kernels for 14%

profile of v5, /device:TPU:0, one launch (start us, length us, event | category | flops | bytes accessed | tf_op | source)
XLA Modules:
  0.0 164.2 jit_solution(6997590198321313920)
XLA Ops:
  2.2 5.1 %collective-permute-start.1 = (bf16[1,1,1,1,1,64,512]{6,5,4,3,2,1,0:T(8,128)(2,1)S(1)}, bf16[1,1,1,1,1,64,512]{6,5,4,3,2,1,0:T(8,128)(2,1)S(1)}, u32[]{:S(2)}, u32[]{:S(2)}) collective-permute-start(bf16[1,1,1,1,1,64,512]{6,5,4,3,2,1,0:T(8,128)(2,1)S(1)} %bitcast.120), channel_id=1, source_target_pairs={{0,3},{1,2},{2,1},{3,0},{4,7},{5,6},{6,5},{7,4},{8,11},{9,10},{10,... | collective-permute-start | bytes 196616 | tf_op jit(solution)/shard_map/ppermute | solution.py:539
  7.8 1.9 %collective-permute-done.1 = bf16[1,1,1,1,1,64,512]{6,5,4,3,2,1,0:T(8,128)(2,1)S(1)} collective-permute-done((bf16[1,1,1,1,1,64,512]{6,5,4,3,2,1,0:T(8,128)(2,1)S(1)}, bf16[1,1,1,1,1,64,512]{6,5,4,3,2,1,0:T(8,128)(2,1)S(1)}, u32[]{:S(2)}, u32[]{:S(2)}) %collective-permute-start.1) | collective-permute-done | bytes 65568 | tf_op jit(solution)/shard_map/ppermute | solution.py:539
  9.7 3.1 %collective-permute-done.2 = bf16[1,1,1,1,1,64,512]{6,5,4,3,2,1,0:T(8,128)(2,1)S(1)} collective-permute-done((bf16[1,1,1,1,1,64,512]{6,5,4,3,2,1,0:T(8,128)(2,1)S(1)}, bf16[1,1,1,1,1,64,512]{6,5,4,3,2,1,0:T(8,128)(2,1)S(1)}, u32[]{:S(2)}, u32[]{:S(2)}) %collective-permute-start.2) | collective-permute-done | bytes 65568 | tf_op jit(solution)/shard_map/ppermute | solution.py:539
  12.9 2.5 %collective-permute-start.4 = (bf16[1,1,1,2,2,64,512]{6,5,4,3,2,1,0:T(8,128)(2,1)S(1)}, bf16[1,1,1,2,2,64,512]{6,5,4,3,2,1,0:T(8,128)(2,1)S(1)}, u32[]{:S(2)}, u32[]{:S(2)}) collective-permute-start(bf16[1,1,1,2,2,64,512]{6,5,4,3,2,1,0:T(8,128)(2,1)S(1)} %maximum_select_fusion.5), channel_id=1, source_target_pairs={{0,24},{1,25},{2,26},{3,27},{4,28},{5,29},{6,30},{7,31},{8,16},{9,... | collective-permute-start | bytes 786440 | tf_op jit(solution)/shard_map/ppermute | solution.py:539
  16.0 2.9 %pack.1 = (bf16[2,18,24,512]{3,2,1,0:T(8,128)(2,1)}, bf16[2,18,8,512]{3,2,1,0:T(8,128)(2,1)}, bf16[2,54,8,512]{3,2,1,0:T(8,128)(2,1)}) custom-call(bf16[72,24,512]{2,1,0:T(8,128)(2,1)} %bitcast.80, bf16[72,24,512]{2,1,0:T(8,128)(2,1)} %bitcast.81, bf16[72,24,512]{2,1,0:T(8,128)(2,1)} %bitcast.90, bf16[72,24,512]{2,1,0:T(8,128)(2,1)} %bitcast.91), custom_call_target="tpu_custom_call" | custom-call | tf_op jit(solution)/shard_map/pack/pallas_call | solution.py:102
  18.8 2.6 %collective-permute-start = (bf16[2,18,24,512]{3,2,1,0:T(8,128)(2,1)}, bf16[2,18,24,512]{3,2,1,0:T(8,128)(2,1)S(1)}, u32[]{:S(2)}, u32[]{:S(2)}) collective-permute-start(bf16[2,18,24,512]{3,2,1,0:T(8,128)(2,1)} %get-tuple-element.41), channel_id=1, source_target_pairs={{1,0},{2,1},{3,2},{0,3},{5,4},{6,5},{7,6},{4,7},{9,8},{10,9},{11,1... | collective-permute-start | bytes 2654216 | tf_op jit(solution)/shard_map/ppermute | solution.py:522
  23.4 2.1 %collective-permute-start.9 = (bf16[2,18,8,512]{3,2,1,0:T(8,128)(2,1)}, bf16[2,18,8,512]{3,2,1,0:T(8,128)(2,1)}, u32[]{:S(2)}, u32[]{:S(2)}) collective-permute-start(bf16[2,18,8,512]{3,2,1,0:T(8,128)(2,1)} %get-tuple-element.49), channel_id=1, source_target_pairs={{5,0},{6,1},{7,2},{4,3},{9,4},{10,5},{11,6},{8,7},{13,8},{14,9},{1... | collective-permute-start | bytes 884744 | tf_op jit(solution)/shard_map/ppermute | solution.py:522
  25.5 1.9 %collective-permute-done.5 = bf16[1,1,1,2,2,64,512]{6,5,4,3,2,1,0:T(8,128)(2,1)S(1)} collective-permute-done((bf16[1,1,1,2,2,64,512]{6,5,4,3,2,1,0:T(8,128)(2,1)S(1)}, bf16[1,1,1,2,2,64,512]{6,5,4,3,2,1,0:T(8,128)(2,1)S(1)}, u32[]{:S(2)}, u32[]{:S(2)}) %collective-permute-start.5) | collective-permute-done | bytes 262176 | tf_op jit(solution)/shard_map/ppermute | solution.py:539
  27.5 11.4 %collective-permute-done.6 = bf16[1,1,1,2,2,64,512]{6,5,4,3,2,1,0:T(8,128)(2,1)S(1)} collective-permute-done((bf16[1,1,1,2,2,64,512]{6,5,4,3,2,1,0:T(8,128)(2,1)S(1)}, bf16[1,1,1,2,2,64,512]{6,5,4,3,2,1,0:T(8,128)(2,1)S(1)}, u32[]{:S(2)}, u32[]{:S(2)}) %collective-permute-start.6) | collective-permute-done | bytes 262176 | tf_op jit(solution)/shard_map/ppermute | solution.py:539
  40.8 2.5 %shard_map.88 = (bf16[1,18,24,512]{3,2,1,0:T(8,128)(2,1)}, f32[1,18,24,128]{3,2,1,0:T(8,128)}, bf16[1,18,24,512]{3,2,1,0:T(8,128)(2,1)}) custom-call(bf16[36,48,512]{2,1,0:T(8,128)(2,1)} %bitcast.82, bf16[36,48,512]{2,1,0:T(8,128)(2,1)} %bitcast.92), custom_call_target="tpu_custom_call" | custom-call | flops 11059200 | bytes 1769472 | tf_op jit(solution)/shard_map/pallas_call | solution.py:176
  43.9 1.3 maximum_select_fusion.2
  47.3 2.8 %shard_map.84 = (bf16[1,18,24,512]{3,2,1,0:T(8,128)(2,1)}, f32[1,18,24,128]{3,2,1,0:T(8,128)}, bf16[1,18,24,512]{3,2,1,0:T(8,128)(2,1)}) custom-call(bf16[36,48,512]{2,1,0:T(8,128)(2,1)} %bitcast.83, bf16[36,48,512]{2,1,0:T(8,128)(2,1)} %bitcast.93, bf16[2,9,48,512]{3,2,1,0:T(8,128)(2,1)} %bitcast.110), custom_call_target="tpu_custom_call" | custom-call | flops 11059200 | bytes 1769472 | tf_op jit(solution)/shard_map/pallas_call | solution.py:176
  50.1 4.9 %shard_map.86 = (bf16[2,18,24,512]{3,2,1,0:T(8,128)(2,1)}, f32[2,18,24,128]{3,2,1,0:T(8,128)}, bf16[2,18,24,512]{3,2,1,0:T(8,128)(2,1)}) custom-call(bf16[36,48,512]{2,1,0:T(8,128)(2,1)} %bitcast.84, bf16[36,48,512]{2,1,0:T(8,128)(2,1)} %bitcast.94, bf16[2,27,16,512]{3,2,1,0:T(8,128)(2,1)} %bitcast.37.east_ref, bf16[2,9,48,512]{3,2,1,0:T(8,128)(2,1)} %bitcast.111, ...), custom_call_target="tpu_custom_call" | custom-call | flops 22118400 | bytes 3538944 | tf_op jit(solution)/shard_map/pallas_call | solution.py:176
  56.0 3.0 %last_join.1 = (bf16[4,2,4,48,512]{4,3,2,1,0:T(8,128)(2,1)}, bf16[4,2,4,16,512]{4,3,2,1,0:T(8,128)(2,1)}) custom-call(s32[1]{0:T(128)} %bitcast.12.place_ref, bf16[4,4,64,512]{3,2,1,0:T(8,128)(2,1)} %bitcast.109, bf16[4,4,64,512]{3,2,1,0:T(8,128)(2,1)} %bitcast.114), custom_call_target="tpu_custom_call" | custom-call | tf_op jit(solution)/shard_map/last_join/pallas_call | solution.py:592
  59.1 13.6 %shard_map.85 = (bf16[1,2,432,512]{3,2,1,0:T(8,128)(2,1)}, f32[3,512,512]{2,1,0:T(8,128)}, f32[512,512]{1,0:T(8,128)}) custom-call(bf16[1,432,512]{2,1,0:T(8,128)(2,1)} %bitcast.138, f32[1,432,128]{2,1,0:T(8,128)} %bitcast.144, bf16[1,432,512]{2,1,0:T(8,128)(2,1)} %bitcast.139, s32[1,1,432]{2,1,0:T(1,128)} %get-tuple-element.93.refs_3_, ...), custom_call_target="tpu_custom_call" | custom-call | flops 3411542016 | bytes 2654208 | tf_op jit(solution)/shard_map/pallas_call | solution.py:358
  72.7 25.6 %shard_map.87 = (bf16[2,2,432,512]{3,2,1,0:T(8,128)(2,1)}, f32[3,512,512]{2,1,0:T(8,128)}, f32[512,512]{1,0:T(8,128)}) custom-call(bf16[2,432,512]{2,1,0:T(8,128)(2,1)} %bitcast.131, f32[2,432,128]{2,1,0:T(8,128)} %bitcast.140, bf16[2,432,512]{2,1,0:T(8,128)(2,1)} %bitcast.132, ...), custom_call_target="tpu_custom_call", output_to_operand_aliasing={{1}: (6, {}), {2}: (7, {})} | custom-call | flops 6823084032 | bytes 5308416 | tf_op jit(solution)/shard_map/pallas_call | solution.py:358
  98.2 14.2 %shard_map.89 = (bf16[1,2,432,512]{3,2,1,0:T(8,128)(2,1)}, bf16[3,512,512]{2,1,0:T(8,128)(2,1)}, bf16[512,512]{1,0:T(8,128)(2,1)}) custom-call(bf16[1,432,512]{2,1,0:T(8,128)(2,1)} %bitcast.136, f32[1,432,128]{2,1,0:T(8,128)} %bitcast.143, bf16[1,432,512]{2,1,0:T(8,128)(2,1)} %bitcast.137, s32[1,1,432]{2,1,0:T(1,128)} %get-tuple-element.92.refs_3_, ...), custom_call_target="tpu_custom_call" | custom-call | flops 3411542016 | bytes 2654208 | tf_op jit(solution)/shard_map/pallas_call | solution.py:358
  112.4 1.3 fusion
  114.3 3.9 %send.1 = (bf16[36,48,512]{2,1,0:T(8,128)(2,1)}, bf16[36,48,512]{2,1,0:T(8,128)(2,1)}, bf16[2,18,16,512]{3,2,1,0:T(8,128)(2,1)}, bf16[2,9,16,512]{3,2,1,0:T(8,12...) custom-call(bf16[1,2,18,24,512]{4,3,2,1,0:T(8,128)(2,1)} %bitcast.119, ...), custom_call_target="tpu_custom_call" | custom-call | tf_op jit(solution)/shard_map/send/pallas_call | solution.py:427
  118.3 1.6 convert_add_fusion
  119.8 1.4 copy-done.1
  121.3 1.6 collective-permute-start.15
  122.9 1.5 collective-permute-start.16
  124.9 5.7 %collective-permute-done.15 = bf16[1,1,1,2,2,64,512]{6,5,4,3,2,1,0:T(8,128)(2,1)S(1)} collective-permute-done((bf16[1,1,1,2,2,64,512]{6,5,4,3,2,1,0:T(8,128)(2,1)S(1)}, bf16[1,1,1,2,2,64,512]{6,5,4,3,2,1,0:T(8,128)(2,1)S(1)}, u32[]{:S(2)}, u32[]{:S(2)}) %collective-permute-start.15) | collective-permute-done | bytes 262176 | tf_op jit(solution)/shard_map/ppermute | solution.py:539
  130.6 12.2 %collective-permute-done.16 = bf16[1,1,1,2,2,64,512]{6,5,4,3,2,1,0:T(8,128)(2,1)S(1)} collective-permute-done((bf16[1,1,1,2,2,64,512]{6,5,4,3,2,1,0:T(8,128)(2,1)S(1)}, bf16[1,1,1,2,2,64,512]{6,5,4,3,2,1,0:T(8,128)(2,1)S(1)}, u32[]{:S(2)}, u32[]{:S(2)}) %collective-permute-start.16) | collective-permute-done | bytes 262176 | tf_op jit(solution)/shard_map/ppermute | solution.py:539
  144.0 1.5 collective-permute-start.18
  145.5 3.7 %collective-permute-done.11.c_ref = bf16[2,18,8,512]{3,2,1,0:T(8,128)(2,1)S(1)} collective-permute-done((bf16[2,18,8,512]{3,2,1,0:T(8,128)(2,1)}, bf16[2,18,8,512]{3,2,1,0:T(8,128)(2,1)S(1)}, u32[]{:S(2)}, u32[]{:S(2)}) %collective-permute-start.11) | collective-permute-done | bytes 294944 | tf_op jit(solution)/shard_map/ppermute | solution.py:522
  149.2 2.1 %collective-permute-start.19 = (bf16[1,1,1,1,1,64,512]{6,5,4,3,2,1,0:T(8,128)(2,1)S(1)}, bf16[1,1,1,1,1,64,512]{6,5,4,3,2,1,0:T(8,128)(2,1)S(1)}, u32[]{:S(2)}, u32[]{:S(2)}) collective-permute-start(bf16[1,1,1,1,1,64,512]{6,5,4,3,2,1,0:T(8,128)(2,1)S(1)} %get-tuple-element.85), channel_id=1, source_target_pairs={{0,2},{1,3},{2,0},{3,1},{4,6},{5,7},{6,4},{7,5},{8,10},{9,11},{10,... | collective-permute-start | bytes 196616 | tf_op jit(solution)/shard_map/ppermute | solution.py:539
  151.4 3.2 %finish.1 = (bf16[36,48,512]{2,1,0:T(8,128)(2,1)}, bf16[36,48,512]{2,1,0:T(8,128)(2,1)}) custom-call(bf16[1,2,18,24,512]{4,3,2,1,0:T(8,128)(2,1)} %bitcast.118, bf16[2,2,18,24,512]{4,3,2,1,0:T(8,128)(2,1)} %bitcast.106, bf16[36,48,512]{2,1,0:T(8,128)(2,1)} %bitcast.86, bf16[36,48,512]{2,1,0:T(8,128)(2,1)} %bitcast.96, ...), custom_call_target="tpu_custom_call", output_to_operand_aliasing={{0}: (4, {}), {1}: (5, {})} | custom-call | tf_op jit(solution)/shard_map/finish/pallas_call | solution.py:451
  154.5 2.5 %rim.1 = (bf16[72,24,512]{2,1,0:T(8,128)(2,1)}, bf16[72,24,512]{2,1,0:T(8,128)(2,1)}) custom-call(bf16[72,24,512]{2,1,0:T(8,128)(2,1)} %bitcast.87, bf16[2,18,24,512]{3,2,1,0:T(8,128)(2,1)} %collective-permute-done.10.low_ref, bf16[2,18,8,512]{3,2,1,0:T(8,128)(2,1)} %copy-done.8, ...), custom_call_target="tpu_custom_call", output_to_operand_aliasing={{0}: (4, {}), {1}: (5, {})} | custom-call | tf_op jit(solution)/shard_map/rim/pallas_call | solution.py:500
  157.8 2.0 %edge.2 = (bf16[72,24,512]{2,1,0:T(8,128)(2,1)}, bf16[72,24,512]{2,1,0:T(8,128)(2,1)}) custom-call(bf16[72,24,512]{2,1,0:T(8,128)(2,1)} %bitcast.88, bf16[72,24,512]{2,1,0:T(8,128)(2,1)} %get-tuple-element.68.o_ref, bf16[2,18,8,512]{3,2,1,0:T(8,128)(2,1)} %copy-done.7, bf16[72,24,512]{2,1,0:T(8,128)(2,1)} %bitcast.98, ...), custom_call_target="tpu_custom_call", output_to_operand_aliasing={{0}: (1, {}), {1}: (4, {})} | custom-call | tf_op jit(solution)/shard_map/edge/pallas_call | solution.py:474
  160.6 2.3 %edge.3 = (bf16[72,24,512]{2,1,0:T(8,128)(2,1)}, bf16[72,24,512]{2,1,0:T(8,128)(2,1)}) custom-call(bf16[72,24,512]{2,1,0:T(8,128)(2,1)} %bitcast.89, bf16[72,24,512]{2,1,0:T(8,128)(2,1)} %get-tuple-element.71.o_ref, bf16[2,36,8,512]{3,2,1,0:T(8,128)(2,1)} %copy-done.6, bf16[72,24,512]{2,1,0:T(8,128)(2,1)} %bitcast.99, ...), custom_call_target="tpu_custom_call", output_to_operand_aliasing={{0}: (1, {}), {1}: (4, {})} | custom-call | tf_op jit(solution)/shard_map/edge/pallas_call | solution.py:474
  (81 shorter events, 15.6 us)
Async XLA Ops:
  2.2 7.6 %collective-permute-start.1 = (bf16[1,1,1,1,1,64,512]{6,5,4,3,2,1,0:T(8,128)(2,1)S(1)}, bf16[1,1,1,1,1,64,512]{6,5,4,3,2,1,0:T(8,128)(2,1)S(1)}, u32[]{:S(2)}, u32[]{:S(2)}) collective-permute-start(bf16[1,1,1,1,1,64,512]{6,5,4,3,2,1,0:T(8,128)(2,1)S(1)} %bitcast.120), channel_id=1, source_target_pairs={{0,3},{1,2},{2,1},{3,0},{4,7},{5,6},{6,5},{7,4},{8,11},{9,10},{10,... | collective-permute-start | bytes 196616 | tf_op jit(solution)/shard_map/ppermute | solution.py:539
  7.2 5.6 %collective-permute-start.2 = (bf16[1,1,1,1,1,64,512]{6,5,4,3,2,1,0:T(8,128)(2,1)S(1)}, bf16[1,1,1,1,1,64,512]{6,5,4,3,2,1,0:T(8,128)(2,1)S(1)}, u32[]{:S(2)}, u32[]{:S(2)}) collective-permute-start(bf16[1,1,1,1,1,64,512]{6,5,4,3,2,1,0:T(8,128)(2,1)S(1)} %bitcast.121), channel_id=1, source_target_pairs={{0,2},{1,3},{2,0},{3,1},{4,6},{5,7},{6,4},{7,5},{8,10},{9,11},{10,... | collective-permute-start | bytes 196616 | tf_op jit(solution)/shard_map/ppermute | solution.py:539
  7.2 5.6 %collective-permute-start.3 = (bf16[1,1,1,1,1,64,512]{6,5,4,3,2,1,0:T(8,128)(2,1)S(1)}, bf16[1,1,1,1,1,64,512]{6,5,4,3,2,1,0:T(8,128)(2,1)S(1)}, u32[]{:S(2)}, u32[]{:S(2)}) collective-permute-start(bf16[1,1,1,1,1,64,512]{6,5,4,3,2,1,0:T(8,128)(2,1)S(1)} %bitcast.122), channel_id=1, source_target_pairs={{0,1},{1,0},{2,3},{3,2},{4,5},{5,4},{6,7},{7,6},{8,9},{9,8},{10,11... | collective-permute-start | bytes 196616 | tf_op jit(solution)/shard_map/ppermute | solution.py:539
  12.9 10.5 %collective-permute-start.4 = (bf16[1,1,1,2,2,64,512]{6,5,4,3,2,1,0:T(8,128)(2,1)S(1)}, bf16[1,1,1,2,2,64,512]{6,5,4,3,2,1,0:T(8,128)(2,1)S(1)}, u32[]{:S(2)}, u32[]{:S(2)}) collective-permute-start(bf16[1,1,1,2,2,64,512]{6,5,4,3,2,1,0:T(8,128)(2,1)S(1)} %maximum_select_fusion.5), channel_id=1, source_target_pairs={{0,24},{1,25},{2,26},{3,27},{4,28},{5,29},{6,30},{7,31},{8,16},{9,... | collective-permute-start | bytes 786440 | tf_op jit(solution)/shard_map/ppermute | solution.py:539
  15.4 11.9 %collective-permute-start.5 = (bf16[1,1,1,2,2,64,512]{6,5,4,3,2,1,0:T(8,128)(2,1)S(1)}, bf16[1,1,1,2,2,64,512]{6,5,4,3,2,1,0:T(8,128)(2,1)S(1)}, u32[]{:S(2)}, u32[]{:S(2)}) collective-permute-start(bf16[1,1,1,2,2,64,512]{6,5,4,3,2,1,0:T(8,128)(2,1)S(1)} %maximum_select_fusion.5), channel_id=1, source_target_pairs={{0,16},{1,17},{2,18},{3,19},{4,20},{5,21},{6,22},{7,23},{8,24},{9,... | collective-permute-start | bytes 786440 | tf_op jit(solution)/shard_map/ppermute | solution.py:539
  16.0 5.5 %copy-start.9 = (s32[24]{0:T(128)S(1)}, s32[24]{0:T(128)}, u32[]{:S(2)}) copy-start(s32[24]{0:T(128)} %param.6) | copy-start | bytes 292
  18.8 27.6 %collective-permute-start = (bf16[2,18,24,512]{3,2,1,0:T(8,128)(2,1)}, bf16[2,18,24,512]{3,2,1,0:T(8,128)(2,1)S(1)}, u32[]{:S(2)}, u32[]{:S(2)}) collective-permute-start(bf16[2,18,24,512]{3,2,1,0:T(8,128)(2,1)} %get-tuple-element.41), channel_id=1, source_target_pairs={{1,0},{2,1},{3,2},{0,3},{5,4},{6,5},{7,6},{4,7},{9,8},{10,9},{11,1... | collective-permute-start | bytes 2654216 | tf_op jit(solution)/shard_map/ppermute | solution.py:522
  21.5 28.7 %collective-permute-start.8 = (bf16[2,54,8,512]{3,2,1,0:T(8,128)(2,1)}, bf16[2,54,8,512]{3,2,1,0:T(8,128)(2,1)}, u32[]{:S(2)}, u32[]{:S(2)}) collective-permute-start(bf16[2,54,8,512]{3,2,1,0:T(8,128)(2,1)} %get-tuple-element.48), channel_id=1, source_target_pairs={{4,0},{5,1},{6,2},{7,3},{8,4},{9,5},{10,6},{11,7},{12,8},{13,9},{1... | collective-permute-start | bytes 2654216 | tf_op jit(solution)/shard_map/ppermute | solution.py:522
  21.6 17.2 %collective-permute-start.6 = (bf16[1,1,1,2,2,64,512]{6,5,4,3,2,1,0:T(8,128)(2,1)S(1)}, bf16[1,1,1,2,2,64,512]{6,5,4,3,2,1,0:T(8,128)(2,1)S(1)}, u32[]{:S(2)}, u32[]{:S(2)}) collective-permute-start(bf16[1,1,1,2,2,64,512]{6,5,4,3,2,1,0:T(8,128)(2,1)S(1)} %maximum_select_fusion.5), channel_id=1, source_target_pairs={{0,8},{1,9},{2,10},{3,11},{4,12},{5,13},{6,14},{7,15},{8,0},{9,1},... | collective-permute-start | bytes 786440 | tf_op jit(solution)/shard_map/ppermute | solution.py:539
  23.4 26.7 %collective-permute-start.9 = (bf16[2,18,8,512]{3,2,1,0:T(8,128)(2,1)}, bf16[2,18,8,512]{3,2,1,0:T(8,128)(2,1)}, u32[]{:S(2)}, u32[]{:S(2)}) collective-permute-start(bf16[2,18,8,512]{3,2,1,0:T(8,128)(2,1)} %get-tuple-element.49), channel_id=1, source_target_pairs={{5,0},{6,1},{7,2},{4,3},{9,4},{10,5},{11,6},{8,7},{13,8},{14,9},{1... | collective-permute-start | bytes 884744 | tf_op jit(solution)/shard_map/ppermute | solution.py:522
  38.8 0.7 copy-start.5
  39.8 15.2 %collective-permute-start.7 = (bf16[2,2,1,2,2,64,512]{6,5,4,3,1,2,0:T(8,128)(2,1)S(1)}, bf16[2,2,1,2,2,64,512]{6,5,4,3,1,2,0:T(8,128)(2,1)S(1)}, u32[]{:S(2)}, u32[]{:S(2)}) collective-permute-start(bf16[2,2,1,2,2,64,512]{6,5,4,3,1,2,0:T(8,128)(2,1)S(1)} %bitcast_select_fusion), channel_id=1, source_target_pairs={{0,4},{1,5},{2,6},{3,7},{4,0},{5,1},{6,2},{7,3},{8,12},{9,13},{10,... | collective-permute-start | bytes 3145736 | tf_op jit(solution)/shard_map/ppermute | solution.py:539
  46.4 0.9 copy-start.2
  55.1 1.0 copy-start.4
  113.7 4.5 %collective-permute-start.14 = (bf16[2,2,1,2,2,64,512]{6,5,4,3,2,1,0:T(8,128)(2,1)S(1)}, bf16[2,2,1,2,2,64,512]{6,5,4,3,2,1,0:T(8,128)(2,1)}, u32[]{:S(2)}, u32[]{:S(2)}) collective-permute-start(bf16[2,2,1,2,2,64,512]{6,5,4,3,2,1,0:T(8,128)(2,1)S(1)} %fusion), channel_id=1, source_target_pairs={{0,4},{1,5},{2,6},{3,7},{4,0},{5,1},{6,2},{7,3},{8,12},{9,13},{10,... | collective-permute-start | bytes 3145736 | tf_op jit(solution)/shard_map/ppermute | solution.py:539
  114.3 4.0 %copy-start = (bf16[3,512,512]{2,1,0:T(8,128)(2,1)S(1)}, bf16[3,512,512]{2,1,0:T(8,128)(2,1)}, u32[]{:S(2)}) copy-start(bf16[3,512,512]{2,1,0:T(8,128)(2,1)} %get-tuple-element.76) | copy-start | bytes 4718596
  114.3 4.0 %copy-start.3 = (bf16[512,512]{1,0:T(8,128)(2,1)S(1)}, bf16[512,512]{1,0:T(8,128)(2,1)}, u32[]{:S(2)}) copy-start(bf16[512,512]{1,0:T(8,128)(2,1)} %get-tuple-element.77) | copy-start | bytes 1572868
  118.2 24.6 %copy-start.10 = (bf16[2,9,16,512]{3,2,1,0:T(8,128)(2,1)S(1)}, bf16[2,9,16,512]{3,2,1,0:T(8,128)(2,1)}, u32[]{:S(2)}) copy-start(bf16[2,9,16,512]{3,2,1,0:T(8,128)(2,1)} %get-tuple-element.69) | copy-start | bytes 884740
  118.2 33.2 %collective-permute-start.10 = (bf16[2,18,24,512]{3,2,1,0:T(8,128)(2,1)}, bf16[2,18,24,512]{3,2,1,0:T(8,128)(2,1)}, u32[]{:S(2)}, u32[]{:S(2)}) collective-permute-start(bf16[2,18,24,512]{3,2,1,0:T(8,128)(2,1)} %bitcast.130), channel_id=1, source_target_pairs={{3,0},{0,1},{1,2},{2,3},{7,4},{4,5},{5,6},{6,7},{11,8},{8,9},{9,10... | collective-permute-start | bytes 2654216 | tf_op jit(solution)/shard_map/ppermute | solution.py:522
  119.8 1.4 copy-start.1
  121.3 9.2 %collective-permute-start.15 = (bf16[1,1,1,2,2,64,512]{6,5,4,3,2,1,0:T(8,128)(2,1)S(1)}, bf16[1,1,1,2,2,64,512]{6,5,4,3,2,1,0:T(8,128)(2,1)S(1)}, u32[]{:S(2)}, u32[]{:S(2)}) collective-permute-start(bf16[1,1,1,2,2,64,512]{6,5,4,3,2,1,0:T(8,128)(2,1)S(1)} %get-tuple-element.80), channel_id=1, source_target_pairs={{0,8},{1,9},{2,10},{3,11},{4,12},{5,13},{6,14},{7,15},{8,0},{9,1},... | collective-permute-start | bytes 786440 | tf_op jit(solution)/shard_map/ppermute | solution.py:539
  122.9 19.9 %collective-permute-start.16 = (bf16[1,1,1,2,2,64,512]{6,5,4,3,2,1,0:T(8,128)(2,1)S(1)}, bf16[1,1,1,2,2,64,512]{6,5,4,3,2,1,0:T(8,128)(2,1)S(1)}, u32[]{:S(2)}, u32[]{:S(2)}) collective-permute-start(bf16[1,1,1,2,2,64,512]{6,5,4,3,2,1,0:T(8,128)(2,1)S(1)} %get-tuple-element.82), channel_id=1, source_target_pairs={{0,16},{1,17},{2,18},{3,19},{4,20},{5,21},{6,22},{7,23},{8,24},{9,... | collective-permute-start | bytes 786440 | tf_op jit(solution)/shard_map/ppermute | solution.py:539
  124.4 18.4 %collective-permute-start.17 = (bf16[1,1,1,2,2,64,512]{6,5,4,3,2,1,0:T(8,128)(2,1)S(1)}, bf16[1,1,1,2,2,64,512]{6,5,4,3,2,1,0:T(8,128)(2,1)S(1)}, u32[]{:S(2)}, u32[]{:S(2)}) collective-permute-start(bf16[1,1,1,2,2,64,512]{6,5,4,3,2,1,0:T(8,128)(2,1)S(1)} %get-tuple-element.81), channel_id=1, source_target_pairs={{0,24},{1,25},{2,26},{3,27},{4,28},{5,29},{6,30},{7,31},{8,16},{9,... | collective-permute-start | bytes 786440 | tf_op jit(solution)/shard_map/ppermute | solution.py:539
  124.9 34.9 %collective-permute-start.13 = (bf16[2,36,8,512]{3,2,1,0:T(8,128)(2,1)}, bf16[2,36,8,512]{3,2,1,0:T(8,128)(2,1)S(1)}, u32[]{:S(2)}, u32[]{:S(2)}) collective-permute-start(bf16[2,36,8,512]{3,2,1,0:T(8,128)(2,1)} %bitcast.52), channel_id=1, source_target_pairs={{28,0},{29,1},{30,2},{31,3},{0,4},{1,5},{2,6},{3,7},{4,8},{5,9},{6... | collective-permute-start | bytes 1769480 | tf_op jit(solution)/shard_map/ppermute | solution.py:522
  130.6 18.7 %collective-permute-start.11 = (bf16[2,18,8,512]{3,2,1,0:T(8,128)(2,1)}, bf16[2,18,8,512]{3,2,1,0:T(8,128)(2,1)S(1)}, u32[]{:S(2)}, u32[]{:S(2)}) collective-permute-start(bf16[2,18,8,512]{3,2,1,0:T(8,128)(2,1)} %bitcast.142), channel_id=1, source_target_pairs={{31,0},{28,1},{29,2},{30,3},{3,4},{0,5},{1,6},{2,7},{7,8},{4,9},{5... | collective-permute-start | bytes 884744 | tf_op jit(solution)/shard_map/ppermute | solution.py:522
  142.8 14.3 %collective-permute-start.12 = (bf16[2,18,8,512]{3,2,1,0:T(8,128)(2,1)S(1)}, bf16[2,18,8,512]{3,2,1,0:T(8,128)(2,1)S(1)}, u32[]{:S(2)}, u32[]{:S(2)}) collective-permute-start(bf16[2,18,8,512]{3,2,1,0:T(8,128)(2,1)S(1)} %bitcast.141), channel_id=1, source_target_pairs={{28,0},{29,1},{30,2},{31,3},{0,4},{1,5},{2,6},{3,7},{4,8},{5,9},{6... | collective-permute-start | bytes 884744 | tf_op jit(solution)/shard_map/ppermute | solution.py:522
  144.0 18.8 %collective-permute-start.18 = (bf16[1,1,1,1,1,64,512]{6,5,4,3,2,1,0:T(8,128)(2,1)S(1)}, bf16[1,1,1,1,1,64,512]{6,5,4,3,2,1,0:T(8,128)(2,1)S(1)}, u32[]{:S(2)}, u32[]{:S(2)}) collective-permute-start(bf16[1,1,1,1,1,64,512]{6,5,4,3,2,1,0:T(8,128)(2,1)S(1)} %get-tuple-element.83), channel_id=1, source_target_pairs={{0,1},{1,0},{2,3},{3,2},{4,5},{5,4},{6,7},{7,6},{8,9},{9,8},{10,11... | collective-permute-start | bytes 196616 | tf_op jit(solution)/shard_map/ppermute | solution.py:539
  149.2 5.3 %copy-start.8 = (bf16[2,18,8,512]{3,2,1,0:T(8,128)(2,1)}, bf16[2,18,8,512]{3,2,1,0:T(8,128)(2,1)S(1)}, u32[]{:S(2)}) copy-start(bf16[2,18,8,512]{3,2,1,0:T(8,128)(2,1)S(1)} %collective-permute-done.11.c_ref) | copy-start | bytes 884740
  149.2 13.6 %collective-permute-start.19 = (bf16[1,1,1,1,1,64,512]{6,5,4,3,2,1,0:T(8,128)(2,1)S(1)}, bf16[1,1,1,1,1,64,512]{6,5,4,3,2,1,0:T(8,128)(2,1)S(1)}, u32[]{:S(2)}, u32[]{:S(2)}) collective-permute-start(bf16[1,1,1,1,1,64,512]{6,5,4,3,2,1,0:T(8,128)(2,1)S(1)} %get-tuple-element.85), channel_id=1, source_target_pairs={{0,2},{1,3},{2,0},{3,1},{4,6},{5,7},{6,4},{7,5},{8,10},{9,11},{10,... | collective-permute-start | bytes 196616 | tf_op jit(solution)/shard_map/ppermute | solution.py:539
  151.4 11.5 %collective-permute-start.20 = (bf16[1,1,1,1,1,64,512]{6,5,4,3,2,1,0:T(8,128)(2,1)S(1)}, bf16[1,1,1,1,1,64,512]{6,5,4,3,2,1,0:T(8,128)(2,1)S(1)}, u32[]{:S(2)}, u32[]{:S(2)}) collective-permute-start(bf16[1,1,1,1,1,64,512]{6,5,4,3,2,1,0:T(8,128)(2,1)S(1)} %get-tuple-element.84), channel_id=1, source_target_pairs={{0,3},{1,2},{2,1},{3,0},{4,7},{5,6},{6,5},{7,4},{8,11},{9,10},{10,... | collective-permute-start | bytes 196616 | tf_op jit(solution)/shard_map/ppermute | solution.py:539
  157.1 0.7 copy-start.7
  159.8 0.8 copy-start.6

commit v6 on v5

--- a/solution.py
+++ b/solution.py
@@ -19,6 +19,10 @@
 
 F32 = jnp.float32
 BF16 = jnp.bfloat16
+
+
+def grant(mib):
+    return pltpu.CompilerParams(vmem_limit_bytes=mib << 20 if mib else None)
 
 
 def nt(a, b):
@@ -186,6 +190,7 @@
         cost_estimate=pl.CostEstimate(
             flops=windows * skip * 3 * SUB * width * 100, transcendentals=0,
             bytes_accessed=windows * skip * 3 * SUB * width * 16),
+        compiler_params=grant(30 if windows > 1 else None),
     )(*args)
     count = 2 * skip * 3 * SUB
     return [x.reshape(windows, count, x.shape[-1]) for x in outs]
@@ -384,6 +389,7 @@
         cost_estimate=pl.CostEstimate(
             flops=windows * count * width * (20 * width + 12 * count), transcendentals=0,
             bytes_accessed=windows * count * width * 12),
+        compiler_params=grant(30),
     )(normed, inv, gs, regions[:, None, :], w_qkv, w_proj, *carry)
 
 
@@ -431,6 +437,7 @@
         out_specs=[own, own, pl.BlockSpec((2, skip, 16, width), lambda s: (0, s, 0, 0))]
         + [whole(*shape) for shape in strips],
         out_shape=tuple(jax.ShapeDtypeStruct(shape, BF16) for shape in outs),
+        compiler_params=grant(20),
         name="send",
     )(below, second, second, fields, grads)
 
@@ -455,6 +462,7 @@
         out_specs=[own, own],
         out_shape=(jax.ShapeDtypeStruct((pairs, 48, width), BF16),) * 2,
         input_output_aliases={4: 0, 5: 1},
+        compiler_params=grant(20),
         name="finish",
     )(first, second, fields, grads, out, gout)
 
@@ -561,20 +569,20 @@
     return lax.dynamic_index_in_dim(held, index, bits.index(bit), keepdims=True)
 
 
-def scatter_stage(held, group, bits, place):
+def scatter_terms(held, group, bits, place):
     here = [jnp.where((place & bit) != 0, 1, 0) for bit in group]
-    total = held
+    own = held
     for bit, i in zip(group, here):
-        total = part_of(total, bit, bits, i)
-    total = total.astype(F32)
+        own = part_of(own, bit, bits, i)
+    terms = [own]
     for flips in range(1, 1 << len(group)):
         send, mask = held, 0
         for k, (bit, i) in enumerate(zip(group, here)):
             flip = (flips >> k) & 1
             send = part_of(send, bit, bits, 1 - i if flip else i)
             mask |= bit * flip
-        total = total + swap(send.astype(BF16), mask).astype(F32)
-    return total
+        terms.append(swap(send.astype(BF16), mask))
+    return terms
 
 
 def last_join_kernel(place_ref, mine_ref, other_ref, w_ref, p_ref):
@@ -637,6 +645,7 @@
     for group in groups[:-1]:
         held = gather_stage(held, group, bits, place)
     bit = groups[-1][0]
+    held = lax.optimization_barrier(held)
     other = swap(held, bit)
     near = bit
     halves = [x.reshape(-1, near, held.shape[-2], width) for x in (held, other)]
@@ -665,15 +674,19 @@
         [grad_w.reshape(devices, -1, width), grad_p.reshape(devices, -1, width)], axis=1
     )
     grads = grads.reshape((2,) * len(bits) + grads.shape[1:])
-    for group in groups[::-1]:
-        grads = scatter_stage(grads, group, bits, place)
-    grads = grads.reshape(-1, width) * factor
+    for i, group in enumerate(groups[::-1]):
+        terms = scatter_terms(grads, group, bits, place)
+        if i + 1 < len(groups):
+            grads = sum(x.astype(F32) for x in terms)
+    terms = [x.reshape(-1, width) for x in terms]
+    grad_w = sum(x[:share].astype(F32) for x in terms) * factor
+    grad_p = sum(x[share:].astype(F32) for x in terms) * factor
     out, gout = finish(b00, b1, f_pairs, g_pairs, skip, out, gout)
     out, gout = unpaired(out), unpaired(gout)
     out, gout = rim(f_lines, r_low, r_corner, g_lines, out, gout)
     out, gout = edge(f_lines, out, r_east1, g_lines, gout, 2 * skip, rows * levels // (2 * skip) - 1)
     out, gout = edge(f_lines, out, r_east0, g_lines, gout, 2 * skip, 1)
-    return (grid_of(out, levels), grid_of(gout, levels), grads[:share], grads[share:])
+    return (grid_of(out, levels), grid_of(gout, levels), grad_w, grad_p)
 
 
 def solution(mesh):

time: 165 us -> 182 us (1.10)
  local copies, waits for them, and re-layouts: 10.5 us -> 24.3 us
  waiting for transfers between devices: 39.9 us -> 53.6 us
  Pallas kernels: 83.3 us -> 69.7 us
    unnamed x23 -> x73, local copies, waits for them, and re-layouts: 6.31 us -> 21 us
    ppermute x7, waiting for transfers between devices: 3.69 us -> 17.9 us  [shift_by(): return lax.ppermute(block, AXES, route)]
    pallas_call x3, Pallas kernels: 53.3 us -> 45 us  [attention(): pl.pallas_call(functools.partial(attention_kernel, carried=bool(carry), l...]
    ppermute x14, starting transfers between devices: 17 us -> 20.4 us  [swap(): return lax.ppermute(block, AXES, [(i, i ^ bit) for i in range(total)])]
    mul x1 -> x2, other arithmetic: 0.04 us -> 3.01 us  [the longest x1 1.6 us: block(): grad_w = sum((x[:share].astype(F32) for x in terms)) * factor]
    pallas_call x3, Pallas kernels: 10.2 us -> 8.28 us  [assembled(): pl.pallas_call(kernel, grid=(2 * windows,), in_specs=specs, out_specs=[ou...]
  transfers between devices with their start and end apart: 21 -> 21, of which waited for: 7 -> 9; matrix products, arithmetic and copies ran while one was open for 5% -> 3% of each run, Pallas kernels for 14% -> 11%
where the time goes in v6:
time: 182 us; the launch traced here: 181 us
  Pallas kernels  69.7 us (38%)
  waiting for transfers between devices  53.6 us (29%)
  local copies, waits for them, and re-layouts  24.3 us (13%)
  starting transfers between devices  23.5 us (13%)
  other arithmetic  8.62 us (5%)
    pallas_call x3, Pallas kernels, attention(): pl.pallas_call(functools.partial(attention_kernel, carried=bool(carry), l...  45 us
    ppermute x14, waiting for transfers between devices, swap(): return lax.ppermute(block, AXES, [(i, i ^ bit) for i in range(total)])  35.7 us
    unnamed x73, local copies, waits for them, and re-layouts  21 us
    ppermute x14, starting transfers between devices, swap(): return lax.ppermute(block, AXES, [(i, i ^ bit) for i in range(total)])  20.4 us
    ppermute x7, waiting for transfers between devices, shift_by(): return lax.ppermute(block, AXES, route)  17.9 us
    pallas_call x3, Pallas kernels, assembled(): pl.pallas_call(kernel, grid=(2 * windows,), in_specs=specs, out_specs=[ou...  8.28 us
    pallas_call x2, Pallas kernels, edge(): pl.pallas_call(edge_kernel, grid=(n,), in_specs=[at, at, strip, at, at],...  4.26 us
  transfers between devices with their start and end apart: 21, of which 9 were waited for; matrix products, arithmetic and copies ran while one was open for 3% of the time, Pallas kernels for 11%

profile of v6, /device:TPU:0, one launch (start us, length us, event | category | flops | bytes accessed | tf_op | source)
XLA Modules:
  0.0 180.8 jit_solution(12593345296421198355)
XLA Ops:
  2.2 5.1 %collective-permute-start.1 = (bf16[1,1,1,1,1,64,512]{6,5,4,3,2,1,0:T(8,128)(2,1)S(1)}, bf16[1,1,1,1,1,64,512]{6,5,4,3,2,1,0:T(8,128)(2,1)S(1)}, u32[]{:S(2)}, u32[]{:S(2)}) collective-permute-start(bf16[1,1,1,1,1,64,512]{6,5,4,3,2,1,0:T(8,128)(2,1)S(1)} %bitcast.131), channel_id=1, source_target_pairs={{0,3},{1,2},{2,1},{3,0},{4,7},{5,6},{6,5},{7,4},{8,11},{9,10},{10,... | collective-permute-start | bytes 196616 | tf_op jit(solution)/shard_map/ppermute | solution.py:547
  7.8 1.9 %collective-permute-done.1 = bf16[1,1,1,1,1,64,512]{6,5,4,3,2,1,0:T(8,128)(2,1)S(1)} collective-permute-done((bf16[1,1,1,1,1,64,512]{6,5,4,3,2,1,0:T(8,128)(2,1)S(1)}, bf16[1,1,1,1,1,64,512]{6,5,4,3,2,1,0:T(8,128)(2,1)S(1)}, u32[]{:S(2)}, u32[]{:S(2)}) %collective-permute-start.1) | collective-permute-done | bytes 65568 | tf_op jit(solution)/shard_map/ppermute | solution.py:547
  9.7 3.1 %collective-permute-done.2 = bf16[1,1,1,1,1,64,512]{6,5,4,3,2,1,0:T(8,128)(2,1)S(1)} collective-permute-done((bf16[1,1,1,1,1,64,512]{6,5,4,3,2,1,0:T(8,128)(2,1)S(1)}, bf16[1,1,1,1,1,64,512]{6,5,4,3,2,1,0:T(8,128)(2,1)S(1)}, u32[]{:S(2)}, u32[]{:S(2)}) %collective-permute-start.2) | collective-permute-done | bytes 65568 | tf_op jit(solution)/shard_map/ppermute | solution.py:547
  12.9 2.5 %collective-permute-start.4 = (bf16[1,1,1,2,2,64,512]{6,5,4,3,2,1,0:T(8,128)(2,1)S(1)}, bf16[1,1,1,2,2,64,512]{6,5,4,3,2,1,0:T(8,128)(2,1)S(1)}, u32[]{:S(2)}, u32[]{:S(2)}) collective-permute-start(bf16[1,1,1,2,2,64,512]{6,5,4,3,2,1,0:T(8,128)(2,1)S(1)} %maximum_select_fusion.3), channel_id=1, source_target_pairs={{0,24},{1,25},{2,26},{3,27},{4,28},{5,29},{6,30},{7,31},{8,16},{9,... | collective-permute-start | bytes 786440 | tf_op jit(solution)/shard_map/ppermute | solution.py:547
  16.5 6.6 %collective-permute-done.4 = bf16[1,1,1,2,2,64,512]{6,5,4,3,2,1,0:T(8,128)(2,1)S(1)} collective-permute-done((bf16[1,1,1,2,2,64,512]{6,5,4,3,2,1,0:T(8,128)(2,1)S(1)}, bf16[1,1,1,2,2,64,512]{6,5,4,3,2,1,0:T(8,128)(2,1)S(1)}, u32[]{:S(2)}, u32[]{:S(2)}) %collective-permute-start.4) | collective-permute-done | bytes 262176 | tf_op jit(solution)/shard_map/ppermute | solution.py:547
  23.1 4.3 %collective-permute-done.5 = bf16[1,1,1,2,2,64,512]{6,5,4,3,2,1,0:T(8,128)(2,1)S(1)} collective-permute-done((bf16[1,1,1,2,2,64,512]{6,5,4,3,2,1,0:T(8,128)(2,1)S(1)}, bf16[1,1,1,2,2,64,512]{6,5,4,3,2,1,0:T(8,128)(2,1)S(1)}, u32[]{:S(2)}, u32[]{:S(2)}) %collective-permute-start.5) | collective-permute-done | bytes 262176 | tf_op jit(solution)/shard_map/ppermute | solution.py:547
  28.8 2.8 %pack.1 = (bf16[2,18,24,512]{3,2,1,0:T(8,128)(2,1)}, bf16[2,18,8,512]{3,2,1,0:T(8,128)(2,1)}, bf16[2,54,8,512]{3,2,1,0:T(8,128)(2,1)}) custom-call(bf16[72,24,512]{2,1,0:T(8,128)(2,1)} %bitcast.76, bf16[72,24,512]{2,1,0:T(8,128)(2,1)} %bitcast.77, bf16[72,24,512]{2,1,0:T(8,128)(2,1)} %bitcast.86, bf16[72,24,512]{2,1,0:T(8,128)(2,1)} %bitcast.87), custom_call_target="tpu_custom_call" | custom-call | tf_op jit(solution)/shard_map/pack/pallas_call | solution.py:106
  33.1 1.6 collective-permute-start.8
  35.6 2.5 %shard_map.88 = (bf16[1,18,24,512]{3,2,1,0:T(8,128)(2,1)}, f32[1,18,24,128]{3,2,1,0:T(8,128)}, bf16[1,18,24,512]{3,2,1,0:T(8,128)(2,1)}) custom-call(bf16[36,48,512]{2,1,0:T(8,128)(2,1)} %bitcast.78, bf16[36,48,512]{2,1,0:T(8,128)(2,1)} %bitcast.88), custom_call_target="tpu_custom_call" | custom-call | flops 11059200 | bytes 1769472 | tf_op jit(solution)/shard_map/pallas_call | solution.py:180
  38.1 16.3 %collective-permute-done = bf16[2,18,24,512]{3,2,1,0:T(8,128)(2,1)S(1)} collective-permute-done((bf16[2,18,24,512]{3,2,1,0:T(8,128)(2,1)}, bf16[2,18,24,512]{3,2,1,0:T(8,128)(2,1)S(1)}, u32[]{:S(2)}, u32[]{:S(2)}) %collective-permute-start) | collective-permute-done | bytes 884768 | tf_op jit(solution)/shard_map/ppermute | solution.py:530
  55.3 3.0 %shard_map.84 = (bf16[1,18,24,512]{3,2,1,0:T(8,128)(2,1)}, f32[1,18,24,128]{3,2,1,0:T(8,128)}, bf16[1,18,24,512]{3,2,1,0:T(8,128)(2,1)}) custom-call(bf16[36,48,512]{2,1,0:T(8,128)(2,1)} %bitcast.79, bf16[36,48,512]{2,1,0:T(8,128)(2,1)} %bitcast.89, bf16[2,9,48,512]{3,2,1,0:T(8,128)(2,1)} %bitcast.101), custom_call_target="tpu_custom_call" | custom-call | flops 11059200 | bytes 1769472 | tf_op jit(solution)/shard_map/pallas_call | solution.py:180
  58.3 1.6 collective-permute-done.9
  61.1 2.8 %shard_map.86 = (bf16[2,18,24,512]{3,2,1,0:T(8,128)(2,1)S(1)}, f32[2,18,24,128]{3,2,1,0:T(8,128)S(1)}, bf16[2,18,24,512]{3,2,1,0:T(8,128)(2,1)S(1)}) custom-call(bf16[36,48,512]{2,1,0:T(8,128)(2,1)S(1)} %bitcast.83, bf16[36,48,512]{2,1,0:T(8,128)(2,1)S(1)} %bitcast.93, bf16[2,27,16,512]{3,2,1,0:T(8,128)(2,1)} %bitcast.35.east_ref, ...), custom_call_target="tpu_custom_call" | custom-call | flops 22118400 | bytes 3538944 | tf_op jit(solution)/shard_map/pallas_call | solution.py:180
  66.6 3.0 %last_join.1 = (bf16[4,2,4,48,512]{4,3,2,1,0:T(8,128)(2,1)}, bf16[4,2,4,16,512]{4,3,2,1,0:T(8,128)(2,1)}) custom-call(s32[1]{0:T(128)} %bitcast.12.place_ref, bf16[4,4,64,512]{3,2,1,0:T(8,128)(2,1)} %bitcast.28.mine_ref, bf16[4,4,64,512]{3,2,1,0:T(8,128)(2,1)} %bitcast.29.other_ref), custom_call_target="tpu_custom_call" | custom-call | tf_op jit(solution)/shard_map/last_join/pallas_call | solution.py:600
  75.0 11.1 %shard_map.85 = (bf16[1,2,432,512]{3,2,1,0:T(8,128)(2,1)S(1)}, f32[3,512,512]{2,1,0:T(8,128)S(1)}, f32[512,512]{1,0:T(8,128)S(1)}) custom-call(bf16[1,432,512]{2,1,0:T(8,128)(2,1)S(1)} %bitcast.117, f32[1,432,128]{2,1,0:T(8,128)S(1)} %bitcast.123, bf16[1,432,512]{2,1,0:T(8,128)(2,1)S(1)} %bitcast.118, s32[1,1,432]{2,1,0:T(1,128)S(1)} %get-tuple-element.91.refs_3_, ...), custom_call_target="tpu_custom_call" | custom-call | flops 3411542016 | bytes 2654208 | tf_op jit(solution)/shard_map/pallas_call | solution.py:363
  87.1 22.5 %shard_map.87 = (bf16[2,2,432,512]{3,2,1,0:T(8,128)(2,1)S(1)}, f32[3,512,512]{2,1,0:T(8,128)S(1)}, f32[512,512]{1,0:T(8,128)S(1)}) custom-call(bf16[2,432,512]{2,1,0:T(8,128)(2,1)S(1)} %bitcast.110, f32[2,432,128]{2,1,0:T(8,128)S(1)} %bitcast.119, bf16[2,432,512]{2,1,0:T(8,128)(2,1)S(1)} %bitcast.111, ...), custom_call_target="tpu_custom_call", output_to_operand_aliasing={{1}: (6, {}), {2}: (7, {})} | custom-call | flops 6823084032 | bytes 5308416 | tf_op jit(solution)/shard_map/pallas_call | solution.py:363
  110.8 11.4 %shard_map.89 = (bf16[1,2,432,512]{3,2,1,0:T(8,128)(2,1)S(1)}, bf16[3,512,512]{2,1,0:T(8,128)(2,1)S(1)}, bf16[512,512]{1,0:T(8,128)(2,1)S(1)}) custom-call(bf16[1,432,512]{2,1,0:T(8,128)(2,1)S(1)} %bitcast.115, f32[1,432,128]{2,1,0:T(8,128)S(1)} %bitcast.122, bf16[1,432,512]{2,1,0:T(8,128)(2,1)S(1)} %bitcast.116, ...), custom_call_target="tpu_custom_call" | custom-call | flops 3411542016 | bytes 2654208 | tf_op jit(solution)/shard_map/pallas_call | solution.py:363
  125.7 1.5 copy-done.3
  128.3 2.2 %send.1 = (bf16[36,48,512]{2,1,0:T(8,128)(2,1)}, bf16[36,48,512]{2,1,0:T(8,128)(2,1)}, bf16[2,18,16,512]{3,2,1,0:T(8,128)(2,1)}, bf16[2,9,16,512]{3,2,1,0:T(8,12...) custom-call(bf16[1,2,18,24,512]{4,3,2,1,0:T(8,128)(2,1)S(1)} %bitcast.106, ...), custom_call_target="tpu_custom_call" | custom-call | tf_op jit(solution)/shard_map/send/pallas_call | solution.py:433
  130.6 1.7 convert_add_fusion
  134.0 1.5 collective-permute-start.15
  136.0 1.5 collective-permute-start.17
  137.5 6.0 %collective-permute-done.15 = bf16[1,1,1,2,2,64,512]{6,5,4,3,2,1,0:T(8,128)(2,1)} collective-permute-done((bf16[1,1,1,2,2,64,512]{6,5,4,3,2,1,0:T(8,128)(2,1)}, bf16[1,1,1,2,2,64,512]{6,5,4,3,2,1,0:T(8,128)(2,1)}, u32[]{:S(2)}, u32[]{:S(2)}) %collective-permute-start.15) | collective-permute-done | bytes 262176 | tf_op jit(solution)/shard_map/ppermute | solution.py:547
  143.5 13.7 %collective-permute-done.16 = bf16[1,1,1,2,2,64,512]{6,5,4,3,2,1,0:T(8,128)(2,1)} collective-permute-done((bf16[1,1,1,2,2,64,512]{6,5,4,3,2,1,0:T(8,128)(2,1)}, bf16[1,1,1,2,2,64,512]{6,5,4,3,2,1,0:T(8,128)(2,1)}, u32[]{:S(2)}, u32[]{:S(2)}) %collective-permute-start.16) | collective-permute-done | bytes 262176 | tf_op jit(solution)/shard_map/ppermute | solution.py:547
  160.1 1.9 %collective-permute-start.18 = (bf16[1,1,1,1,1,64,512]{6,5,4,3,2,1,0:T(8,128)(2,1)}, bf16[1,1,1,1,1,64,512]{6,5,4,3,2,1,0:T(8,128)(2,1)}, u32[]{:S(2)}, u32[]{:S(2)}) collective-permute-start(bf16[1,1,1,1,1,64,512]{6,5,4,3,2,1,0:T(8,128)(2,1)} %get-tuple-element.83), channel_id=1, source_target_pairs={{0,1},{1,0},{2,3},{3,2},{4,5},{5,4},{6,7},{7,6},{8,9},{9,8},{10,11... | collective-permute-start | bytes 196616 | tf_op jit(solution)/shard_map/ppermute | solution.py:547
  162.1 3.7 %collective-permute-start.19 = (bf16[1,1,1,1,1,64,512]{6,5,4,3,2,1,0:T(8,128)(2,1)}, bf16[1,1,1,1,1,64,512]{6,5,4,3,2,1,0:T(8,128)(2,1)}, u32[]{:S(2)}, u32[]{:S(2)}) collective-permute-start(bf16[1,1,1,1,1,64,512]{6,5,4,3,2,1,0:T(8,128)(2,1)} %get-tuple-element.85), channel_id=1, source_target_pairs={{0,2},{1,3},{2,0},{3,1},{4,6},{5,7},{6,4},{7,5},{8,10},{9,11},{10,... | collective-permute-start | bytes 196616 | tf_op jit(solution)/shard_map/ppermute | solution.py:547
  166.7 1.5 copy-done.4
  169.3 1.6 finish.1
  170.9 2.5 %rim.1 = (bf16[72,24,512]{2,1,0:T(8,128)(2,1)}, bf16[72,24,512]{2,1,0:T(8,128)(2,1)}) custom-call(bf16[72,24,512]{2,1,0:T(8,128)(2,1)} %bitcast.80, bf16[2,18,24,512]{3,2,1,0:T(8,128)(2,1)} %collective-permute-done.10.low_ref, bf16[2,18,8,512]{3,2,1,0:T(8,128)(2,1)} %collective-permute-done.11.c_ref, ...), custom_call_target="tpu_custom_call", output_to_operand_aliasing={{0}: (4, {}), {1}: (5, {})} | custom-call | tf_op jit(solution)/shard_map/rim/pallas_call | solution.py:508
  173.5 2.0 %edge.2 = (bf16[72,24,512]{2,1,0:T(8,128)(2,1)}, bf16[72,24,512]{2,1,0:T(8,128)(2,1)}) custom-call(bf16[72,24,512]{2,1,0:T(8,128)(2,1)} %bitcast.81, bf16[72,24,512]{2,1,0:T(8,128)(2,1)} %get-tuple-element.68.o_ref, bf16[2,18,8,512]{3,2,1,0:T(8,128)(2,1)} %collective-permute-done.12.r_ref, ...), custom_call_target="tpu_custom_call", output_to_operand_aliasing={{0}: (1, {}), {1}: (4, {})} | custom-call | tf_op jit(solution)/shard_map/edge/pallas_call | solution.py:482
  175.5 2.3 %edge.3 = (bf16[72,24,512]{2,1,0:T(8,128)(2,1)}, bf16[72,24,512]{2,1,0:T(8,128)(2,1)}) custom-call(bf16[72,24,512]{2,1,0:T(8,128)(2,1)} %bitcast.82, bf16[72,24,512]{2,1,0:T(8,128)(2,1)} %get-tuple-element.71.o_ref, bf16[2,36,8,512]{3,2,1,0:T(8,128)(2,1)} %collective-permute-done.13.r_ref, ...), custom_call_target="tpu_custom_call", output_to_operand_aliasing={{0}: (1, {}), {1}: (4, {})} | custom-call | tf_op jit(solution)/shard_map/edge/pallas_call | solution.py:482
  177.8 1.6 fusion.8
  (127 shorter events, 32.5 us)
Async XLA Ops:
  2.2 7.6 %collective-permute-start.1 = (bf16[1,1,1,1,1,64,512]{6,5,4,3,2,1,0:T(8,128)(2,1)S(1)}, bf16[1,1,1,1,1,64,512]{6,5,4,3,2,1,0:T(8,128)(2,1)S(1)}, u32[]{:S(2)}, u32[]{:S(2)}) collective-permute-start(bf16[1,1,1,1,1,64,512]{6,5,4,3,2,1,0:T(8,128)(2,1)S(1)} %bitcast.131), channel_id=1, source_target_pairs={{0,3},{1,2},{2,1},{3,0},{4,7},{5,6},{6,5},{7,4},{8,11},{9,10},{10,... | collective-permute-start | bytes 196616 | tf_op jit(solution)/shard_map/ppermute | solution.py:547
  7.2 5.6 %collective-permute-start.2 = (bf16[1,1,1,1,1,64,512]{6,5,4,3,2,1,0:T(8,128)(2,1)S(1)}, bf16[1,1,1,1,1,64,512]{6,5,4,3,2,1,0:T(8,128)(2,1)S(1)}, u32[]{:S(2)}, u32[]{:S(2)}) collective-permute-start(bf16[1,1,1,1,1,64,512]{6,5,4,3,2,1,0:T(8,128)(2,1)S(1)} %bitcast.132), channel_id=1, source_target_pairs={{0,2},{1,3},{2,0},{3,1},{4,6},{5,7},{6,4},{7,5},{8,10},{9,11},{10,... | collective-permute-start | bytes 196616 | tf_op jit(solution)/shard_map/ppermute | solution.py:547
  7.2 5.6 %collective-permute-start.3 = (bf16[1,1,1,1,1,64,512]{6,5,4,3,2,1,0:T(8,128)(2,1)S(1)}, bf16[1,1,1,1,1,64,512]{6,5,4,3,2,1,0:T(8,128)(2,1)S(1)}, u32[]{:S(2)}, u32[]{:S(2)}) collective-permute-start(bf16[1,1,1,1,1,64,512]{6,5,4,3,2,1,0:T(8,128)(2,1)S(1)} %bitcast.133), channel_id=1, source_target_pairs={{0,1},{1,0},{2,3},{3,2},{4,5},{5,4},{6,7},{7,6},{8,9},{9,8},{10,11... | collective-permute-start | bytes 196616 | tf_op jit(solution)/shard_map/ppermute | solution.py:547
  12.9 10.2 %collective-permute-start.4 = (bf16[1,1,1,2,2,64,512]{6,5,4,3,2,1,0:T(8,128)(2,1)S(1)}, bf16[1,1,1,2,2,64,512]{6,5,4,3,2,1,0:T(8,128)(2,1)S(1)}, u32[]{:S(2)}, u32[]{:S(2)}) collective-permute-start(bf16[1,1,1,2,2,64,512]{6,5,4,3,2,1,0:T(8,128)(2,1)S(1)} %maximum_select_fusion.3), channel_id=1, source_target_pairs={{0,24},{1,25},{2,26},{3,27},{4,28},{5,29},{6,30},{7,31},{8,16},{9,... | collective-permute-start | bytes 786440 | tf_op jit(solution)/shard_map/ppermute | solution.py:547
  15.4 11.9 %collective-permute-start.5 = (bf16[1,1,1,2,2,64,512]{6,5,4,3,2,1,0:T(8,128)(2,1)S(1)}, bf16[1,1,1,2,2,64,512]{6,5,4,3,2,1,0:T(8,128)(2,1)S(1)}, u32[]{:S(2)}, u32[]{:S(2)}) collective-permute-start(bf16[1,1,1,2,2,64,512]{6,5,4,3,2,1,0:T(8,128)(2,1)S(1)} %maximum_select_fusion.3), channel_id=1, source_target_pairs={{0,16},{1,17},{2,18},{3,19},{4,20},{5,21},{6,22},{7,23},{8,24},{9,... | collective-permute-start | bytes 786440 | tf_op jit(solution)/shard_map/ppermute | solution.py:547
  16.0 11.7 %collective-permute-start.6 = (bf16[1,1,1,2,2,64,512]{6,5,4,3,2,1,0:T(8,128)(2,1)S(1)}, bf16[1,1,1,2,2,64,512]{6,5,4,3,2,1,0:T(8,128)(2,1)S(1)}, u32[]{:S(2)}, u32[]{:S(2)}) collective-permute-start(bf16[1,1,1,2,2,64,512]{6,5,4,3,2,1,0:T(8,128)(2,1)S(1)} %maximum_select_fusion.3), channel_id=1, source_target_pairs={{0,8},{1,9},{2,10},{3,11},{4,12},{5,13},{6,14},{7,15},{8,0},{9,1},... | collective-permute-start | bytes 786440 | tf_op jit(solution)/shard_map/ppermute | solution.py:547
  28.8 37.7 %collective-permute-start.7 = (bf16[2,2,1,2,2,64,512]{6,5,4,3,1,2,0:T(8,128)(2,1)}, bf16[2,2,1,2,2,64,512]{6,5,4,3,1,2,0:T(8,128)(2,1)}, u32[]{:S(2)}, u32[]{:S(2)}) collective-permute-start(bf16[2,2,1,2,2,64,512]{6,5,4,3,1,2,0:T(8,128)(2,1)} %maximum_select_fusion), channel_id=1, source_target_pairs={{0,4},{1,5},{2,6},{3,7},{4,0},{5,1},{6,2},{7,3},{8,12},{9,13},{10,... | collective-permute-start | bytes 3145736 | tf_op jit(solution)/shard_map/ppermute | solution.py:547
  28.8 5.8 %copy-start.35 = (s32[24]{0:T(128)S(1)}, s32[24]{0:T(128)}, u32[]{:S(2)}) copy-start(s32[24]{0:T(128)} %param.6) | copy-start | bytes 292
  31.7 22.7 %collective-permute-start = (bf16[2,18,24,512]{3,2,1,0:T(8,128)(2,1)}, bf16[2,18,24,512]{3,2,1,0:T(8,128)(2,1)S(1)}, u32[]{:S(2)}, u32[]{:S(2)}) collective-permute-start(bf16[2,18,24,512]{3,2,1,0:T(8,128)(2,1)} %get-tuple-element.41), channel_id=1, source_target_pairs={{1,0},{2,1},{3,2},{0,3},{5,4},{6,5},{7,6},{4,7},{9,8},{10,9},{11,1... | collective-permute-start | bytes 2654216 | tf_op jit(solution)/shard_map/ppermute | solution.py:530
  33.1 26.8 %collective-permute-start.8 = (bf16[2,54,8,512]{3,2,1,0:T(8,128)(2,1)}, bf16[2,54,8,512]{3,2,1,0:T(8,128)(2,1)}, u32[]{:S(2)}, u32[]{:S(2)}) collective-permute-start(bf16[2,54,8,512]{3,2,1,0:T(8,128)(2,1)} %get-tuple-element.48), channel_id=1, source_target_pairs={{4,0},{5,1},{6,2},{7,3},{8,4},{9,5},{10,6},{11,7},{12,8},{13,9},{1... | collective-permute-start | bytes 2654216 | tf_op jit(solution)/shard_map/ppermute | solution.py:530
  34.7 25.2 %collective-permute-start.9 = (bf16[2,18,8,512]{3,2,1,0:T(8,128)(2,1)}, bf16[2,18,8,512]{3,2,1,0:T(8,128)(2,1)}, u32[]{:S(2)}, u32[]{:S(2)}) collective-permute-start(bf16[2,18,8,512]{3,2,1,0:T(8,128)(2,1)} %get-tuple-element.49), channel_id=1, source_target_pairs={{5,0},{6,1},{7,2},{4,3},{9,4},{10,5},{11,6},{8,7},{13,8},{14,9},{1... | collective-permute-start | bytes 884744 | tf_op jit(solution)/shard_map/ppermute | solution.py:530
  55.3 4.6 %copy-start = (bf16[24,24,3,512]{3,1,2,0:T(8,128)(2,1)S(1)}, bf16[24,24,3,512]{3,1,2,0:T(8,128)(2,1)}, u32[]{:S(2)}) copy-start(bf16[24,24,3,512]{3,1,2,0:T(8,128)(2,1)} %param.5) | copy-start | bytes 5308420
  55.3 4.6 %copy-start.1 = (bf16[24,24,3,512]{3,1,2,0:T(8,128)(2,1)S(1)}, bf16[24,24,3,512]{3,1,2,0:T(8,128)(2,1)}, u32[]{:S(2)}) copy-start(bf16[24,24,3,512]{3,1,2,0:T(8,128)(2,1)} %param.9) | copy-start | bytes 5308420
  75.0 12.1 %copy-start.16 = (bf16[4,2,4,48,512]{4,3,2,1,0:T(8,128)(2,1)S(1)}, bf16[4,2,4,48,512]{4,3,2,1,0:T(8,128)(2,1)}, u32[]{:S(2)}) copy-start(bf16[4,2,4,48,512]{4,3,2,1,0:T(8,128)(2,1)} %get-tuple-element.45) | copy-start | bytes 4718596
  75.0 12.1 %copy-start.18 = (bf16[2,18,24,512]{3,2,1,0:T(8,128)(2,1)S(1)}, bf16[2,18,24,512]{3,2,1,0:T(8,128)(2,1)}, u32[]{:S(2)}) copy-start(bf16[2,18,24,512]{3,2,1,0:T(8,128)(2,1)} %copy-done.17) | copy-start | bytes 2654212
  75.0 12.1 %copy-start.20 = (bf16[2,18,24,512]{3,2,1,0:T(8,128)(2,1)S(1)}, bf16[2,18,24,512]{3,2,1,0:T(8,128)(2,1)}, u32[]{:S(2)}) copy-start(bf16[2,18,24,512]{3,2,1,0:T(8,128)(2,1)} %copy-done.19) | copy-start | bytes 2654212
  75.0 12.1 %copy-start.22 = (bf16[4,2,4,16,512]{4,3,2,1,0:T(8,128)(2,1)S(1)}, bf16[4,2,4,16,512]{4,3,2,1,0:T(8,128)(2,1)}, u32[]{:S(2)}) copy-start(bf16[4,2,4,16,512]{4,3,2,1,0:T(8,128)(2,1)} %get-tuple-element.46) | copy-start | bytes 1572868
  75.0 12.1 %copy-start.28 = (f32[2,18,24,128]{3,2,1,0:T(8,128)S(1)}, f32[2,18,24,128]{3,2,1,0:T(8,128)}, u32[]{:S(2)}) copy-start(f32[2,18,24,128]{3,2,1,0:T(8,128)} %copy-done.27) | copy-start | bytes 1327108
  87.1 23.8 %copy-start.23 = (bf16[1,18,24,512]{3,2,1,0:T(8,128)(2,1)S(1)}, bf16[1,18,24,512]{3,2,1,0:T(8,128)(2,1)}, u32[]{:S(2)}) copy-start(bf16[1,18,24,512]{3,2,1,0:T(8,128)(2,1)} %get-tuple-element.58) | copy-start | bytes 1327108
  87.1 23.8 %copy-start.24 = (bf16[1,18,24,512]{3,2,1,0:T(8,128)(2,1)S(1)}, bf16[1,18,24,512]{3,2,1,0:T(8,128)(2,1)}, u32[]{:S(2)}) copy-start(bf16[1,18,24,512]{3,2,1,0:T(8,128)(2,1)} %get-tuple-element.60) | copy-start | bytes 1327108
  87.1 23.7 %copy-start.31 = (f32[1,18,24,128]{3,2,1,0:T(8,128)S(1)}, f32[1,18,24,128]{3,2,1,0:T(8,128)}, u32[]{:S(2)}) copy-start(f32[1,18,24,128]{3,2,1,0:T(8,128)} %get-tuple-element.59) | copy-start | bytes 663556
  124.5 6.2 %collective-permute-start.14 = (bf16[2,2,1,2,2,64,512]{6,5,4,3,2,1,0:T(8,128)(2,1)}, bf16[2,2,1,2,2,64,512]{6,5,4,3,2,1,0:T(8,128)(2,1)}, u32[]{:S(2)}, u32[]{:S(2)}) collective-permute-start(bf16[2,2,1,2,2,64,512]{6,5,4,3,2,1,0:T(8,128)(2,1)} %fusion), channel_id=1, source_target_pairs={{0,4},{1,5},{2,6},{3,7},{4,0},{5,1},{6,2},{7,3},{8,12},{9,13},{10,... | collective-permute-start | bytes 3145736 | tf_op jit(solution)/shard_map/ppermute | solution.py:547
  130.6 35.2 %collective-permute-start.10 = (bf16[2,18,24,512]{3,2,1,0:T(8,128)(2,1)}, bf16[2,18,24,512]{3,2,1,0:T(8,128)(2,1)}, u32[]{:S(2)}, u32[]{:S(2)}) collective-permute-start(bf16[2,18,24,512]{3,2,1,0:T(8,128)(2,1)} %bitcast.41), channel_id=1, source_target_pairs={{3,0},{0,1},{1,2},{2,3},{7,4},{4,5},{5,6},{6,7},{11,8},{8,9},{9,10... | collective-permute-start | bytes 2654216 | tf_op jit(solution)/shard_map/ppermute | solution.py:530
  134.0 9.5 %collective-permute-start.15 = (bf16[1,1,1,2,2,64,512]{6,5,4,3,2,1,0:T(8,128)(2,1)}, bf16[1,1,1,2,2,64,512]{6,5,4,3,2,1,0:T(8,128)(2,1)}, u32[]{:S(2)}, u32[]{:S(2)}) collective-permute-start(bf16[1,1,1,2,2,64,512]{6,5,4,3,2,1,0:T(8,128)(2,1)} %get-tuple-element.80), channel_id=1, source_target_pairs={{0,8},{1,9},{2,10},{3,11},{4,12},{5,13},{6,14},{7,15},{8,0},{9,1},... | collective-permute-start | bytes 786440 | tf_op jit(solution)/shard_map/ppermute | solution.py:547
  135.5 21.7 %collective-permute-start.16 = (bf16[1,1,1,2,2,64,512]{6,5,4,3,2,1,0:T(8,128)(2,1)}, bf16[1,1,1,2,2,64,512]{6,5,4,3,2,1,0:T(8,128)(2,1)}, u32[]{:S(2)}, u32[]{:S(2)}) collective-permute-start(bf16[1,1,1,2,2,64,512]{6,5,4,3,2,1,0:T(8,128)(2,1)} %get-tuple-element.82), channel_id=1, source_target_pairs={{0,16},{1,17},{2,18},{3,19},{4,20},{5,21},{6,22},{7,23},{8,24},{9,... | collective-permute-start | bytes 786440 | tf_op jit(solution)/shard_map/ppermute | solution.py:547
  136.0 21.2 %collective-permute-start.17 = (bf16[1,1,1,2,2,64,512]{6,5,4,3,2,1,0:T(8,128)(2,1)}, bf16[1,1,1,2,2,64,512]{6,5,4,3,2,1,0:T(8,128)(2,1)}, u32[]{:S(2)}, u32[]{:S(2)}) collective-permute-start(bf16[1,1,1,2,2,64,512]{6,5,4,3,2,1,0:T(8,128)(2,1)} %get-tuple-element.81), channel_id=1, source_target_pairs={{0,24},{1,25},{2,26},{3,27},{4,28},{5,29},{6,30},{7,31},{8,16},{9,... | collective-permute-start | bytes 786440 | tf_op jit(solution)/shard_map/ppermute | solution.py:547
  137.5 38.0 %collective-permute-start.13 = (bf16[2,36,8,512]{3,2,1,0:T(8,128)(2,1)}, bf16[2,36,8,512]{3,2,1,0:T(8,128)(2,1)}, u32[]{:S(2)}, u32[]{:S(2)}) collective-permute-start(bf16[2,36,8,512]{3,2,1,0:T(8,128)(2,1)} %bitcast.50), channel_id=1, source_target_pairs={{28,0},{29,1},{30,2},{31,3},{0,4},{1,5},{2,6},{3,7},{4,8},{5,9},{6... | collective-permute-start | bytes 1769480 | tf_op jit(solution)/shard_map/ppermute | solution.py:530
  143.5 18.6 %collective-permute-start.11 = (bf16[2,18,8,512]{3,2,1,0:T(8,128)(2,1)}, bf16[2,18,8,512]{3,2,1,0:T(8,128)(2,1)}, u32[]{:S(2)}, u32[]{:S(2)}) collective-permute-start(bf16[2,18,8,512]{3,2,1,0:T(8,128)(2,1)} %bitcast.121), channel_id=1, source_target_pairs={{31,0},{28,1},{29,2},{30,3},{3,4},{0,5},{1,6},{2,7},{7,8},{4,9},{5... | collective-permute-start | bytes 884744 | tf_op jit(solution)/shard_map/ppermute | solution.py:530
  157.2 16.3 %collective-permute-start.12 = (bf16[2,18,8,512]{3,2,1,0:T(8,128)(2,1)}, bf16[2,18,8,512]{3,2,1,0:T(8,128)(2,1)}, u32[]{:S(2)}, u32[]{:S(2)}) collective-permute-start(bf16[2,18,8,512]{3,2,1,0:T(8,128)(2,1)} %bitcast.120), channel_id=1, source_target_pairs={{28,0},{29,1},{30,2},{31,3},{0,4},{1,5},{2,6},{3,7},{4,8},{5,9},{6... | collective-permute-start | bytes 884744 | tf_op jit(solution)/shard_map/ppermute | solution.py:530
  160.1 17.6 %collective-permute-start.18 = (bf16[1,1,1,1,1,64,512]{6,5,4,3,2,1,0:T(8,128)(2,1)}, bf16[1,1,1,1,1,64,512]{6,5,4,3,2,1,0:T(8,128)(2,1)}, u32[]{:S(2)}, u32[]{:S(2)}) collective-permute-start(bf16[1,1,1,1,1,64,512]{6,5,4,3,2,1,0:T(8,128)(2,1)} %get-tuple-element.83), channel_id=1, source_target_pairs={{0,1},{1,0},{2,3},{3,2},{4,5},{5,4},{6,7},{7,6},{8,9},{9,8},{10,11... | collective-permute-start | bytes 196616 | tf_op jit(solution)/shard_map/ppermute | solution.py:547
  162.1 15.7 %collective-permute-start.19 = (bf16[1,1,1,1,1,64,512]{6,5,4,3,2,1,0:T(8,128)(2,1)}, bf16[1,1,1,1,1,64,512]{6,5,4,3,2,1,0:T(8,128)(2,1)}, u32[]{:S(2)}, u32[]{:S(2)}) collective-permute-start(bf16[1,1,1,1,1,64,512]{6,5,4,3,2,1,0:T(8,128)(2,1)} %get-tuple-element.85), channel_id=1, source_target_pairs={{0,2},{1,3},{2,0},{3,1},{4,6},{5,7},{6,4},{7,5},{8,10},{9,11},{10,... | collective-permute-start | bytes 196616 | tf_op jit(solution)/shard_map/ppermute | solution.py:547
  165.8 12.0 %collective-permute-start.20 = (bf16[1,1,1,1,1,64,512]{6,5,4,3,2,1,0:T(8,128)(2,1)}, bf16[1,1,1,1,1,64,512]{6,5,4,3,2,1,0:T(8,128)(2,1)}, u32[]{:S(2)}, u32[]{:S(2)}) collective-permute-start(bf16[1,1,1,1,1,64,512]{6,5,4,3,2,1,0:T(8,128)(2,1)} %get-tuple-element.84), channel_id=1, source_target_pairs={{0,3},{1,2},{2,1},{3,0},{4,7},{5,6},{6,5},{7,4},{8,11},{9,10},{10,... | collective-permute-start | bytes 196616 | tf_op jit(solution)/shard_map/ppermute | solution.py:547
  (25 other events, 33.9 us)
